TPU v7x, 256 devices: a whole 4x4x8 slice. The times are simulated.
256 devices in a mesh: leaf: 256 (over x, y, z, core).
Axes of the slice: x: 4, y: 4, z: 8, core: 2. Of those that a mesh axis runs over, the one named last changes fastest.
Arguments:
- coarse_basis: float32 [9, 131072, 256], P(None, 'leaf'), as said below
- rhs_vectors_coarse: float32 [131072, 768], P('leaf'), may hold values from -6 to 6
- vertex_tier_depth: int32 [131072], P('leaf'), may hold values from 0 to 8
Outputs:
- solution: float32 [131072, 768], P('leaf')
Inputs may be any that keep to these rules, and one draw needn't show every extreme that they name: vertex_tier_depth[v] is the coarsest separator level whose block has vertex v in its support; level 0 is the vertex's own leaf block. `coarse_basis`: float32 entries, finite.
All inputs are finite; a program needn't handle non-finite values.
Results may differ from a plain program's by a relative error of at most 0.0001.
Values sent between devices are 32-bit elements; how exact they have to be, the bound alone decides.
No kernel may reach another device: no remote copies, remote signals or barrier semaphores. Data moves between devices by JAX's collectives and lax.ppermute only.
A program may use at most 128 MiB of HBM per device.

v0:
```python
import functools

import jax
import jax.numpy as jnp
from jax import lax
from jax.experimental import pallas as pl
from jax.experimental.pallas import tpu as pltpu
from jax.sharding import PartitionSpec as P

N = 256
V = 512
S = 256
R = 768
UNIT = 16
UNITS = 16
VMEM = pl.BlockSpec(memory_space=pltpu.VMEM)
SMEM = pl.BlockSpec(memory_space=pltpu.SMEM)
HBM = pl.BlockSpec(memory_space=pltpu.HBM)


def place(i):
    return i >> 6, (i >> 4) & 3, (i >> 1) & 7, i & 1


def index(x, y, z, core):
    return x << 6 | y << 4 | z << 1 | core


def pairs(*partners):
    out = []
    for i in range(N):
        x, y, z, core = place(i)
        if partners[core] is not None:
            out.append((i, index(*partners[core](x, y, z), core)))
    return out


def along_x(j):
    return lambda x, y, z: (x ^ j, y, z)


def along_y(j):
    return lambda x, y, z: (x, y ^ j, z)


def along_z(j):
    return lambda x, y, z: (x, y, z ^ j)


def shifted_z(j):
    return lambda x, y, z: (x, y, ((((z + 7) & 7) ^ j) + 1) & 7)


def send(array, perm):
    return lax.ppermute(array, "leaf", perm)


SWAP = [(i, i ^ 1) for i in range(N)]


def slots(me, core):
    x, y, z, _ = place(me)
    turned = (z + 7) & 7
    low, mid = turned & 1, turned >> 1 & 1
    quarter = low ^ 3 * mid
    first = core == 0
    levels = (6 + 2 * core, 5 + 2 * core, 3 + core, 2 - core)
    masks = (
        jnp.where(first, y << 2 | quarter, x << 2 | y),
        jnp.where(first, (y & 1) << 3 | quarter << 1, (x & 1) << 3 | y << 1),
        jnp.where(first, (z & 1) << 3, (low << 1 | mid) << 2),
        jnp.zeros_like(z),
    )
    return levels, masks


def row_a(unit):
    chunk, quarter = unit >> 2, unit & 3
    return jnp.where(chunk < 2, chunk * 192 + quarter * 48, 256 + chunk * 64 + quarter * UNIT)


def row_b(unit):
    return (unit >> 3) * 192 + (unit >> 1 & 3) * 48 + UNIT + (unit & 1) * UNIT


def row_c(unit):
    return unit * UNIT


def row_d(unit):
    return S + unit * UNIT


ROWS = (row_a, row_b, row_c, row_d)


def split(value):
    high = value.astype(jnp.bfloat16)
    low = (value - high.astype(jnp.float32)).astype(jnp.bfloat16)
    return high, low


def masked(basis, depth, level):
    keep = depth[...] >= jnp.asarray(level).astype(jnp.float32)
    return split(
        jnp.concatenate([jnp.where(keep, basis[:, :128], 0.0), jnp.where(keep, basis[:, 128:], 0.0)], 1)
    )


def dot3(a, b, contract):
    dot = functools.partial(
        lax.dot_general,
        dimension_numbers=(((contract,), (0,)), ((), ())),
        preferred_element_type=jnp.float32,
    )
    return dot(a[0], b[0]) + (dot(a[0], b[1]) + dot(a[1], b[0]))


def put(product, out, slot, mask):
    for unit in range(UNITS):
        row = pl.multiple_of(ROWS[slot](unit ^ mask), UNIT)
        out[pl.ds(row, UNIT), :] = product[unit * UNIT : (unit + 1) * UNIT]


def first_kernel(me, depth, rhs_hbm, basis_hbm, out, high, low, depth_out, rhs, basis, sems):
    levels, masks = slots(me[0], 1 - (me[0] & 1))
    copies = [pltpu.make_async_copy(rhs_hbm, rhs, sems.at[0])]
    for slot in (0, 1):
        copies.append(pltpu.make_async_copy(basis_hbm.at[levels[slot]], basis.at[slot], sems.at[slot + 1]))
    for copy in copies:
        copy.start()
    depth_out[...] = jnp.broadcast_to(depth[...].astype(jnp.float32), (128, V)).T
    copies[0].wait()
    high[...], low[...] = split(rhs[...])
    for slot in (0, 1):
        copies[slot + 1].wait()
        product = dot3(masked(basis.at[slot][...], depth_out, levels[slot]), (high[...], low[...]), 0)
        put(product, out, slot, masks[slot])


def first_partials(me, depth, rhs, basis):
    return pl.pallas_call(
        first_kernel,
        out_shape=(
            jax.ShapeDtypeStruct((2 * S, R), jnp.float32),
            jax.ShapeDtypeStruct((V, R), jnp.bfloat16),
            jax.ShapeDtypeStruct((V, R), jnp.bfloat16),
            jax.ShapeDtypeStruct((V, 128), jnp.float32),
        ),
        in_specs=[SMEM, VMEM, HBM, HBM],
        out_specs=(VMEM,) * 4,
        scratch_shapes=[
            pltpu.VMEM((V, R), jnp.float32),
            pltpu.VMEM((2, V, S), jnp.float32),
            pltpu.SemaphoreType.DMA((3,)),
        ],
        compiler_params=pltpu.CompilerParams(vmem_limit_bytes=52 << 20),
        cost_estimate=pl.CostEstimate(flops=12 * R * S * V, bytes_accessed=2 * 4 * S * (R + V), transcendentals=0),
        name="send_ab",
    )(me, depth, rhs, basis)


def partial_kernel(work, me, high, low, depth, basis_hbm, *refs):
    outs, (basis, sems) = refs[:-2], refs[-2:]
    sides = [slots(me[0], me[0] & 1), slots(me[0], 1 - (me[0] & 1))]
    copies = []
    for number, (_, slot, other) in enumerate(work):
        copy = pltpu.make_async_copy(basis_hbm.at[sides[other][0][slot]], basis.at[number], sems.at[number])
        copy.start()
        copies.append(copy)
    for number, (out, slot, other) in enumerate(work):
        copies[number].wait()
        levels, masks = sides[other]
        product = dot3(masked(basis.at[number][...], depth, levels[slot]), (high[...], low[...]), 0)
        put(product, outs[out], slot, masks[slot])


def partials(work, me, high, low, depth, basis, name):
    count = 1 + max(out for out, _, _ in work)
    return pl.pallas_call(
        functools.partial(partial_kernel, work),
        out_shape=tuple(jax.ShapeDtypeStruct((2 * S, R), jnp.float32) for _ in range(count)),
        in_specs=[SMEM, VMEM, VMEM, VMEM, HBM],
        out_specs=(VMEM,) * count,
        scratch_shapes=[pltpu.VMEM((len(work), V, S), jnp.float32), pltpu.SemaphoreType.DMA((len(work),))],
        compiler_params=pltpu.CompilerParams(vmem_limit_bytes=45 << 20),
        cost_estimate=pl.CostEstimate(
            flops=len(work) * 6 * R * S * V, bytes_accessed=len(work) * 4 * S * (R + V), transcendentals=0
        ),
        name=name,
    )(me, high, low, depth, basis)


def leaf_kernel(high, low, depth, basis, out):
    own = masked(basis[0], depth, 0)
    out[...] = dot3(own, split(dot3(own, (high[...], low[...]), 0)), 1)


def leaf(high, low, depth, basis):
    return pl.pallas_call(
        leaf_kernel,
        out_shape=jax.ShapeDtypeStruct((V, R), jnp.float32),
        in_specs=[VMEM, VMEM, VMEM, VMEM],
        out_specs=VMEM,
        compiler_params=pltpu.CompilerParams(vmem_limit_bytes=16 << 20),
        cost_estimate=pl.CostEstimate(flops=12 * R * S * V, bytes_accessed=4 * V * R, transcendentals=0),
        name="leaf",
    )(high, low, depth, basis)


def image_kernel(work, me, depth, before, basis, *refs):
    pieces, (out, high, low) = refs[:-3], refs[-3:]
    sides = [slots(me[0], me[0] & 1), slots(me[0], 1 - (me[0] & 1))]
    for number, (slot, other, plan) in enumerate(work):
        levels, masks = sides[other]
        for unit, (piece, start) in enumerate(plan):
            row = pl.multiple_of(UNIT * (unit ^ masks[slot]), UNIT)
            part_high, part_low = split(pieces[piece][start : start + UNIT, :])
            high[number, pl.ds(row, UNIT), :] = part_high
            low[number, pl.ds(row, UNIT), :] = part_low
        own = masked(basis[levels[slot]], depth, levels[slot])
        image = dot3(own, (high[number], low[number]), 1)
        out[...] = (before[...] if number == 0 else out[...]) + image


def images(work, me, depth, before, basis, pieces, name):
    count = len(work)
    return pl.pallas_call(
        functools.partial(image_kernel, work),
        out_shape=jax.ShapeDtypeStruct((V, R), jnp.float32),
        in_specs=[SMEM, VMEM, VMEM, VMEM] + [VMEM] * len(pieces),
        out_specs=VMEM,
        scratch_shapes=[pltpu.VMEM((count, S, R), jnp.bfloat16), pltpu.VMEM((count, S, R), jnp.bfloat16)],
        compiler_params=pltpu.CompilerParams(vmem_limit_bytes=16 << 20),
        cost_estimate=pl.CostEstimate(
            flops=count * 6 * R * S * V, bytes_accessed=count * 4 * S * (R + V), transcendentals=0
        ),
        name=name,
    )(me, depth, before, basis, *pieces)


def plan_ab(slot):
    out = []
    for unit in range(UNITS):
        if slot == 0:
            chunk, quarter = unit >> 2, unit & 3
            out.append((chunk, quarter * 48 if chunk < 2 else quarter * UNIT))
        else:
            out.append((unit >> 3, (unit >> 1 & 3) * 48 + UNIT + (unit & 1) * UNIT))
    return out


def shift_pieces(plan, by):
    return [(piece + by, row) for piece, row in plan]


PLAN_C = [(u >> 3, (u & 7) * UNIT) for u in range(UNITS)]
PLAN_D = [(2, u * UNIT) for u in range(UNITS)]


def body(basis, rhs, vertex_tier_depth):
    index_here = lax.axis_index("leaf")
    first = (index_here & 1) == 0
    me = index_here.reshape(1)

    send_ab, high, low, depth = first_partials(me, vertex_tier_depth.reshape(1, V), rhs, basis)
    got_ab = send(send_ab, SWAP)
    keep_ab, send_cd, keep_cd = partials(
        [(0, 0, 0), (0, 1, 0), (1, 2, 1), (1, 3, 1), (2, 2, 0), (2, 3, 0)], me, high, low, depth, basis, "rest"
    )
    got_cd = send(send_cd, SWAP)

    step = [None] + [pairs(along_y(j), along_x(j)) for j in (1, 2, 3)]
    ab = keep_ab + got_ab
    r1 = send(ab[192:384], step[1])
    r2 = send(ab[384:448], step[2])
    r3 = send(ab[448:512], step[3])

    near, mid = pairs(along_z(1), shifted_z(1)), pairs(along_z(2), shifted_z(2))
    cd = keep_cd + got_cd
    c, d = cd[:S], cd[S:]
    c = c[:128] + send(c[128:], near)
    d = d + send(d, pairs(along_z(1), None))

    both = (ab[:192] + r1).reshape(4, 48, R)
    both = jnp.concatenate([both[:, :UNIT] + (r2 + r3).reshape(4, UNIT, R), both[:, UNIT:]], 1)
    t1 = send(both[1], pairs(shifted_z(1), along_y(1)))
    t2 = send(both[2], pairs(shifted_z(1), along_y(2)))
    t3 = send(both[3], pairs(None, along_y(3)))
    total = both[0] + t1
    total, passed = jnp.where(first, total, total + t2 + t3), both[3] + t2
    total_t = total + send(jnp.where(first, passed, total), pairs(shifted_z(2), along_z(1)))
    total = total_t + send(total_t, pairs(along_z(4), along_z(2)))
    other = send(total, pairs(shifted_z(2), along_z(4)))
    total = jnp.where(first, total, total + other)
    g1 = send(total, pairs(shifted_z(1), along_y(1)))
    g2 = send(jnp.where(first, other, total), pairs(shifted_z(1), along_y(2)))
    g3 = send(total, pairs(None, along_y(3)))
    done = jnp.stack([total, g1, g2, jnp.where(first, other, g3)])
    top = done[:, :UNIT].reshape(64, R)
    done = done.reshape(192, R)
    ab_pieces = (done, send(done, step[1]), send(top, step[2]), send(top, step[3]))

    m2 = send(c[64:], mid)
    c_low = jnp.where(first, c[:64], c[:64] + m2)
    m3 = send(c_low, pairs(along_z(2), along_z(4)))
    c_low = c_low + m3
    m4 = send(c_low, pairs(None, shifted_z(2)))
    c_half = jnp.concatenate([c_low, jnp.where(first, c[64:] + m2, m4)])
    cd_pieces = (c_half, send(c_half, near), d)

    their_cd = tuple(send(piece, SWAP) for piece in cd_pieces)
    their_ab = tuple(send(piece, SWAP) for piece in ab_pieces)

    result = leaf(high, low, depth, basis)
    result = images(
        [(2, 0, PLAN_C), (3, 0, PLAN_D), (2, 1, shift_pieces(PLAN_C, 3)), (3, 1, shift_pieces(PLAN_D, 3))],
        me, depth, result, basis, cd_pieces + their_cd, "image_cd",
    )
    result = images([(0, 0, plan_ab(0)), (1, 0, plan_ab(1))], me, depth, result, basis, ab_pieces, "image_own")
    return images([(0, 1, plan_ab(0)), (1, 1, plan_ab(1))], me, depth, result, basis, their_ab, "image_last")


def solution(mesh):
    in_specs = (P(None, "leaf", None), P("leaf", None), P("leaf"))
    out_specs = P("leaf", None)
    return jax.shard_map(body, mesh=mesh, in_specs=in_specs, out_specs=out_specs, check_vma=False)
```

profile of v0, /device:TPU:1, one launch (start us, length us, event | category | flops | bytes accessed | tf_op | source)
XLA Modules:
  0.0 132.2 jit_solution(2789820619513707436)
XLA Ops:
  0.7 5.6 %send_ab.1 = (f32[512,768]{1,0:T(8,128)}, bf16[512,768]{1,0:T(8,128)(2,1)S(1)}, bf16[512,768]{1,0:T(8,128)(2,1)S(1)}, f32[512,128]{1,0:T(8,128)S(1)}) custom-call(s32[1]{0:T(128)} %bitcast.me, s32[1,512]{1,0:T(1,128)S(1)} %bitcast.29, f32[512,768]{1,0:T(8,128)} %rhs_hbm.1, f32[9,512,256]{2,1,0:T(8,128)} %basis.7), custom_call_target="tpu_custom_call" | custom-call | flops 1207959552 | bytes 2621440 | tf_op jit(solution)/shard_map/send_ab/pallas_call | solution.py:142
  6.3 3.3 %collective-permute-start.10 = (f32[512,768]{1,0:T(8,128)}, f32[512,768]{1,0:T(8,128)S(1)}, u32[]{:S(2)}, u32[]{:S(2)}) collective-permute-start(f32[512,768]{1,0:T(8,128)} %get-tuple-element.18), channel_id=1, source_target_pairs={{0,1},{1,0},{2,3},{3,2},{4,5},{5,4},{6,7},{7,6},{8,9},{9,8},{10,11... | collective-permute-start | bytes 4718600 | tf_op jit(solution)/shard_map/ppermute | solution.py:55
  9.6 9.5 %rest.1 = (f32[512,768]{1,0:T(8,128)S(1)}, f32[512,768]{1,0:T(8,128)}, f32[512,768]{1,0:T(8,128)S(1)}) custom-call(s32[1]{0:T(128)} %bitcast.me, bf16[512,768]{1,0:T(8,128)(2,1)S(1)} %get-tuple-element.13.high, bf16[512,768]{1,0:T(8,128)(2,1)S(1)} %get-tuple-element.14.low, f32[512,128]{1,0:T(8,128)S(1)} %get-tuple-element.12.depth, f32[9,512,256]{2,1,0:T(8,128)} %basis.7), custom_call_target="tpu_custom_call" | custom-call | flops 3623878656 | bytes 7864320 | tf_op jit(solution)/shard_map/rest/pallas_call | solution.py:180
  21.5 1.5 %collective-permute-start.12 = (f32[64,768]{1,0:T(8,128)}, f32[64,768]{1,0:T(8,128)}, u32[]{:S(2)}, u32[]{:S(2)}) collective-permute-start(f32[64,768]{1,0:T(8,128)} %get-tuple-element.24), channel_id=1, source_target_pairs={{0,32},{1,129},{2,34},{3,131},{4,36},{5,133},{6,38},{7,135},{8,40}... | collective-permute-start | bytes 589832 | tf_op jit(solution)/shard_map/ppermute | solution.py:55
  23.0 1.9 %collective-permute-start.13 = (f32[64,768]{1,0:T(8,128)}, f32[64,768]{1,0:T(8,128)}, u32[]{:S(2)}, u32[]{:S(2)}) collective-permute-start(f32[64,768]{1,0:T(8,128)} %get-tuple-element.23), channel_id=1, source_target_pairs={{0,48},{1,193},{2,50},{3,195},{4,52},{5,197},{6,54},{7,199},{8,56}... | collective-permute-start | bytes 589832 | tf_op jit(solution)/shard_map/ppermute | solution.py:55
  25.0 1.6 %add.51 = f32[512,768]{1,0:T(8,128)S(1)} add(f32[512,768]{1,0:T(8,128)S(1)} %get-tuple-element.15, f32[512,768]{1,0:T(8,128)} %collective-permute-done) | non-fusion elementwise | flops 393216 | bytes 4718592 | tf_op jit(solution)/shard_map/add | solution.py:280
  27.4 4.1 %collective-permute-start.1 = (f32[128,768]{1,0:T(8,128)S(1)}, f32[128,768]{1,0:T(8,128)S(1)}, u32[]{:S(2)}, u32[]{:S(2)}) collective-permute-start(f32[128,768]{1,0:T(8,128)S(1)} %slice.71), channel_id=1, source_target_pairs={{0,2},{1,15},{2,0},{3,5},{4,6},{5,3},{6,4},{7,9},{8,10},{9,7},{10,... | collective-permute-start | bytes 1179656 | tf_op jit(solution)/shard_map/ppermute | solution.py:55
  33.3 1.5 %slice_add_fusion = f32[192,768]{1,0:T(8,128)S(1)} fusion(f32[192,768]{1,0:T(8,128)} %collective-permute-done.11, f32[512,768]{1,0:T(8,128)} %copy-done.1), kind=kLoop, calls=%fused_computation.6 | loop fusion | flops 147456 | bytes 1769472 | tf_op jit(solution)/shard_map/add | solution.py:285
  36.0 2.9 %collective-permute-start.15 = (f32[48,768]{1,0:T(8,128)S(1)}, f32[48,768]{1,0:T(8,128)S(1)}, u32[]{:S(2)}, u32[]{:S(2)}) collective-permute-start(f32[48,768]{1,0:T(8,128)S(1)} %get-tuple-element.27), channel_id=1, source_target_pairs={{0,14},{1,33},{2,4},{3,35},{4,2},{5,37},{6,8},{7,39},{8,6},{9,41},... | collective-permute-start | bytes 442376 | tf_op jit(solution)/shard_map/ppermute | solution.py:55
  38.9 1.9 %collective-permute-start.16 = (f32[48,768]{1,0:T(8,128)S(1)}, f32[48,768]{1,0:T(8,128)S(1)}, u32[]{:S(2)}, u32[]{:S(2)}) collective-permute-start(f32[48,768]{1,0:T(8,128)S(1)} %get-tuple-element.26), channel_id=1, source_target_pairs={{1,49},{3,51},{5,53},{7,55},{9,57},{11,59},{13,61},{15,63},{17,33}... | collective-permute-start | bytes 442376 | tf_op jit(solution)/shard_map/ppermute | solution.py:55
  40.9 6.0 %collective-permute-start.2 = (f32[64,768]{1,0:T(8,128)S(1)}, f32[64,768]{1,0:T(8,128)S(1)}, u32[]{:S(2)}, u32[]{:S(2)}) collective-permute-start(f32[64,768]{1,0:T(8,128)S(1)} %slice.73), channel_id=1, source_target_pairs={{0,4},{1,13},{2,6},{3,7},{4,0},{5,9},{6,2},{7,3},{8,12},{9,5},{10,... | collective-permute-start | bytes 589832 | tf_op jit(solution)/shard_map/ppermute | solution.py:55
  47.5 5.7 %collective-permute-done.17 = f32[48,768]{1,0:T(8,128)S(1)} collective-permute-done((f32[48,768]{1,0:T(8,128)S(1)}, f32[48,768]{1,0:T(8,128)S(1)}, u32[]{:S(2)}, u32[]{:S(2)}) %collective-permute-start.17) | collective-permute-done | bytes 147488 | tf_op jit(solution)/shard_map/ppermute | solution.py:55
  53.2 2.0 %collective-permute-start.18 = (f32[48,768]{1,0:T(8,128)S(1)}, f32[48,768]{1,0:T(8,128)S(1)}, u32[]{:S(2)}, u32[]{:S(2)}) collective-permute-start(f32[48,768]{1,0:T(8,128)S(1)} %add.65), channel_id=1, source_target_pairs={{0,8},{1,5},{2,10},{3,7},{4,12},{5,1},{6,14},{7,3},{8,0},{9,13},{1... | collective-permute-start | bytes 442376 | tf_op jit(solution)/shard_map/ppermute | solution.py:55
  55.2 3.9 %collective-permute-start.3 = (f32[64,768]{1,0:T(8,128)S(1)}, f32[64,768]{1,0:T(8,128)S(1)}, u32[]{:S(2)}, u32[]{:S(2)}) collective-permute-start(f32[64,768]{1,0:T(8,128)S(1)} %add_select_fusion), channel_id=1, source_target_pairs={{0,4},{1,9},{2,6},{3,11},{4,0},{5,13},{6,2},{7,15},{8,12},{9,1},{1... | collective-permute-start | bytes 589832 | tf_op jit(solution)/shard_map/ppermute | solution.py:55
  59.1 1.6 %collective-permute-done.18 = f32[48,768]{1,0:T(8,128)S(1)} collective-permute-done((f32[48,768]{1,0:T(8,128)S(1)}, f32[48,768]{1,0:T(8,128)S(1)}, u32[]{:S(2)}, u32[]{:S(2)}) %collective-permute-start.18) | collective-permute-done | bytes 147488 | tf_op jit(solution)/shard_map/ppermute | solution.py:55
  60.8 11.5 %collective-permute-start.19 = (f32[48,768]{1,0:T(8,128)S(1)}, f32[48,768]{1,0:T(8,128)S(1)}, u32[]{:S(2)}, u32[]{:S(2)}) collective-permute-start(f32[48,768]{1,0:T(8,128)S(1)} %add.66), channel_id=1, source_target_pairs={{0,12},{1,9},{2,6},{3,11},{4,8},{5,13},{6,2},{7,15},{8,4},{9,1},{1... | collective-permute-start | bytes 442376 | tf_op jit(solution)/shard_map/ppermute | solution.py:55
  72.3 1.6 %collective-permute-start.9 = (f32[256,768]{1,0:T(8,128)S(1)}, f32[256,768]{1,0:T(8,128)S(1)}, u32[]{:S(2)}, u32[]{:S(2)}) collective-permute-start(f32[256,768]{1,0:T(8,128)S(1)} %slice_add_fusion.3.refs_2_), channel_id=1, source_target_pairs={{0,1},{1,0},{2,3},{3,2},{4,5},{5,4},{6,7},{7,6},{8,9},{9,8},{10,11... | collective-permute-start | bytes 2359304 | tf_op jit(solution)/shard_map/ppermute | solution.py:55
  74.0 1.9 %collective-permute-start.4 = (f32[64,768]{1,0:T(8,128)S(1)}, f32[64,768]{1,0:T(8,128)S(1)}, u32[]{:S(2)}, u32[]{:S(2)}) collective-permute-start(f32[64,768]{1,0:T(8,128)S(1)} %add.54), channel_id=1, source_target_pairs={{1,13},{3,7},{5,9},{7,3},{9,5},{11,15},{13,1},{15,11},{17,29},{19,... | collective-permute-start | bytes 589832 | tf_op jit(solution)/shard_map/ppermute | solution.py:55
  75.9 7.5 %collective-permute-start.22 = (f32[48,768]{1,0:T(8,128)S(1)}, f32[48,768]{1,0:T(8,128)S(1)}, u32[]{:S(2)}, u32[]{:S(2)}) collective-permute-start(f32[48,768]{1,0:T(8,128)S(1)} %get-tuple-element.20), channel_id=1, source_target_pairs={{1,49},{3,51},{5,53},{7,55},{9,57},{11,59},{13,61},{15,63},{17,33}... | collective-permute-start | bytes 442376 | tf_op jit(solution)/shard_map/ppermute | solution.py:55
  83.5 2.5 %collective-permute-start.20 = (f32[48,768]{1,0:T(8,128)S(1)}, f32[48,768]{1,0:T(8,128)S(1)}, u32[]{:S(2)}, u32[]{:S(2)}) collective-permute-start(f32[48,768]{1,0:T(8,128)S(1)} %get-tuple-element.20), channel_id=1, source_target_pairs={{0,14},{1,17},{2,4},{3,19},{4,2},{5,21},{6,8},{7,23},{8,6},{9,25},... | collective-permute-start | bytes 442376 | tf_op jit(solution)/shard_map/ppermute | solution.py:55
  86.0 4.1 %collective-permute-start.21 = (f32[48,768]{1,0:T(8,128)S(1)}, f32[48,768]{1,0:T(8,128)S(1)}, u32[]{:S(2)}, u32[]{:S(2)}) collective-permute-start(f32[48,768]{1,0:T(8,128)S(1)} %get-tuple-element.19), channel_id=1, source_target_pairs={{0,14},{1,33},{2,4},{3,35},{4,2},{5,37},{6,8},{7,39},{8,6},{9,41},... | collective-permute-start | bytes 442376 | tf_op jit(solution)/shard_map/ppermute | solution.py:55
  90.2 4.1 %collective-permute-done.21 = f32[48,768]{1,0:T(8,128)S(1)} collective-permute-done((f32[48,768]{1,0:T(8,128)S(1)}, f32[48,768]{1,0:T(8,128)S(1)}, u32[]{:S(2)}, u32[]{:S(2)}) %collective-permute-start.21) | collective-permute-done | bytes 147488 | tf_op jit(solution)/shard_map/ppermute | solution.py:55
  94.3 6.5 %collective-permute-start.23 = (f32[192,768]{1,0:T(8,128)S(1)}, f32[192,768]{1,0:T(8,128)S(1)}, u32[]{:S(2)}, u32[]{:S(2)}) collective-permute-start(f32[192,768]{1,0:T(8,128)S(1)} %bitcast.26), channel_id=1, source_target_pairs={{0,16},{1,65},{2,18},{3,67},{4,20},{5,69},{6,22},{7,71},{8,24},{9,... | collective-permute-start | bytes 1769480 | tf_op jit(solution)/shard_map/ppermute | solution.py:55
  100.8 5.2 %collective-permute-start.5 = (f32[128,768]{1,0:T(8,128)S(1)}, f32[128,768]{1,0:T(8,128)S(1)}, u32[]{:S(2)}, u32[]{:S(2)}) collective-permute-start(f32[128,768]{1,0:T(8,128)S(1)} %pad_maximum_fusion.1.refs_0_), channel_id=1, source_target_pairs={{0,2},{1,15},{2,0},{3,5},{4,6},{5,3},{6,4},{7,9},{8,10},{9,7},{10,... | collective-permute-start | bytes 1179656 | tf_op jit(solution)/shard_map/ppermute | solution.py:55
  106.1 5.0 %collective-permute-done.5.refs_1_ = f32[128,768]{1,0:T(8,128)S(1)} collective-permute-done((f32[128,768]{1,0:T(8,128)S(1)}, f32[128,768]{1,0:T(8,128)S(1)}, u32[]{:S(2)}, u32[]{:S(2)}) %collective-permute-start.5) | collective-permute-done | bytes 393248 | tf_op jit(solution)/shard_map/ppermute | solution.py:55
  111.7 1.9 %collective-permute-start.27 = (f32[192,768]{1,0:T(8,128)S(1)}, f32[192,768]{1,0:T(8,128)S(1)}, u32[]{:S(2)}, u32[]{:S(2)}) collective-permute-start(f32[192,768]{1,0:T(8,128)S(1)} %collective-permute-done.23.refs_1_), channel_id=1, source_target_pairs={{0,1},{1,0},{2,3},{3,2},{4,5},{5,4},{6,7},{7,6},{8,9},{9,8},{10,11... | collective-permute-start | bytes 1769480 | tf_op jit(solution)/shard_map/ppermute | solution.py:55
  113.6 1.9 %leaf.1.before = f32[512,768]{1,0:T(8,128)S(1)} custom-call(bf16[512,768]{1,0:T(8,128)(2,1)S(1)} %get-tuple-element.13.high, bf16[512,768]{1,0:T(8,128)(2,1)S(1)} %get-tuple-element.14.low, f32[512,128]{1,0:T(8,128)S(1)} %get-tuple-element.12.depth, f32[9,512,256]{2,1,0:T(8,128)S(1)} %bitcast.25), custom_call_target="tpu_custom_call" | custom-call | flops 1207959552 | bytes 1572864 | tf_op jit(solution)/shard_map/leaf/pallas_call | solution.py:200
  115.5 3.8 %collective-permute-done.25.refs_3_ = f32[64,768]{1,0:T(8,128)S(1)} collective-permute-done((f32[64,768]{1,0:T(8,128)S(1)}, f32[64,768]{1,0:T(8,128)S(1)}, u32[]{:S(2)}, u32[]{:S(2)}) %collective-permute-start.25) | collective-permute-done | bytes 196640 | tf_op jit(solution)/shard_map/ppermute | solution.py:55
  119.3 5.3 %collective-permute-start.28 = (f32[64,768]{1,0:T(8,128)S(1)}, f32[64,768]{1,0:T(8,128)S(1)}, u32[]{:S(2)}, u32[]{:S(2)}) collective-permute-start(f32[64,768]{1,0:T(8,128)S(1)} %collective-permute-done.24.refs_2_), channel_id=1, source_target_pairs={{0,1},{1,0},{2,3},{3,2},{4,5},{5,4},{6,7},{7,6},{8,9},{9,8},{10,11... | collective-permute-start | bytes 589832 | tf_op jit(solution)/shard_map/ppermute | solution.py:55
  124.6 3.1 %image_cd.1.before = f32[512,768]{1,0:T(8,128)S(1)} custom-call(s32[1]{0:T(128)} %bitcast.me, f32[512,128]{1,0:T(8,128)S(1)} %get-tuple-element.12.depth, f32[512,768]{1,0:T(8,128)S(1)} %leaf.1.before, f32[9,512,256]{2,1,0:T(8,128)S(1)} %bitcast.25, f32[128,768]{1,0:T(8,128)S(1)} %pad_maximum_fusion.1.refs_0_, ...), custom_call_target="tpu_custom_call" | custom-call | flops 2415919104 | bytes 5242880 | tf_op jit(solution)/shard_map/image_cd/pallas_call | solution.py:228
  127.7 1.7 %image_own.1.before = f32[512,768]{1,0:T(8,128)S(1)} custom-call(s32[1]{0:T(128)} %bitcast.me, f32[512,128]{1,0:T(8,128)S(1)} %get-tuple-element.12.depth, f32[512,768]{1,0:T(8,128)S(1)} %image_cd.1.before, f32[9,512,256]{2,1,0:T(8,128)S(1)} %bitcast.25, f32[192,768]{1,0:T(8,128)S(1)} %bitcast.28, f32[192,768]{1,0:T(8,128)S(1)} %collective-permute-done.23.refs_1_, ...), custom_call_target="tpu_custom_call" | custom-call | flops 1207959552 | bytes 2621440 | tf_op jit(solution)/shard_map/image_own/pallas_call | solution.py:228
  129.4 2.8 %image_last.1 = f32[512,768]{1,0:T(8,128)} custom-call(s32[1]{0:T(128)} %bitcast.me, f32[512,128]{1,0:T(8,128)S(1)} %get-tuple-element.12.depth, f32[512,768]{1,0:T(8,128)S(1)} %image_own.1.before, f32[9,512,256]{2,1,0:T(8,128)S(1)} %bitcast.25, f32[192,768]{1,0:T(8,128)S(1)} %collective-permute-done.26.refs_0_, ...), custom_call_target="tpu_custom_call" | custom-call | flops 1207959552 | bytes 2621440 | tf_op jit(solution)/shard_map/image_last/pallas_call | solution.py:228
  (68 shorter events, 8.5 us)
Async XLA Ops:
  6.3 12.9 %collective-permute-start.10 = (f32[512,768]{1,0:T(8,128)}, f32[512,768]{1,0:T(8,128)S(1)}, u32[]{:S(2)}, u32[]{:S(2)}) collective-permute-start(f32[512,768]{1,0:T(8,128)} %get-tuple-element.18), channel_id=1, source_target_pairs={{0,1},{1,0},{2,3},{3,2},{4,5},{5,4},{6,7},{7,6},{8,9},{9,8},{10,11... | collective-permute-start | bytes 4718600 | tf_op jit(solution)/shard_map/ppermute | solution.py:55
  19.1 5.9 %collective-permute-start = (f32[512,768]{1,0:T(8,128)}, f32[512,768]{1,0:T(8,128)}, u32[]{:S(2)}, u32[]{:S(2)}) collective-permute-start(f32[512,768]{1,0:T(8,128)} %get-tuple-element.16), channel_id=1, source_target_pairs={{0,1},{1,0},{2,3},{3,2},{4,5},{5,4},{6,7},{7,6},{8,9},{9,8},{10,11... | collective-permute-start | bytes 4718600 | tf_op jit(solution)/shard_map/ppermute | solution.py:55
  20.3 13.0 %collective-permute-start.11 = (f32[192,768]{1,0:T(8,128)}, f32[192,768]{1,0:T(8,128)}, u32[]{:S(2)}, u32[]{:S(2)}) collective-permute-start(f32[192,768]{1,0:T(8,128)} %slice.76), channel_id=1, source_target_pairs={{0,16},{1,65},{2,18},{3,67},{4,20},{5,69},{6,22},{7,71},{8,24},{9,... | collective-permute-start | bytes 1769480 | tf_op jit(solution)/shard_map/ppermute | solution.py:55
  21.5 10.7 %collective-permute-start.12 = (f32[64,768]{1,0:T(8,128)}, f32[64,768]{1,0:T(8,128)}, u32[]{:S(2)}, u32[]{:S(2)}) collective-permute-start(f32[64,768]{1,0:T(8,128)} %get-tuple-element.24), channel_id=1, source_target_pairs={{0,32},{1,129},{2,34},{3,131},{4,36},{5,133},{6,38},{7,135},{8,40}... | collective-permute-start | bytes 589832 | tf_op jit(solution)/shard_map/ppermute | solution.py:55
  23.0 9.2 %collective-permute-start.13 = (f32[64,768]{1,0:T(8,128)}, f32[64,768]{1,0:T(8,128)}, u32[]{:S(2)}, u32[]{:S(2)}) collective-permute-start(f32[64,768]{1,0:T(8,128)} %get-tuple-element.23), channel_id=1, source_target_pairs={{0,48},{1,193},{2,50},{3,195},{4,52},{5,197},{6,54},{7,199},{8,56}... | collective-permute-start | bytes 589832 | tf_op jit(solution)/shard_map/ppermute | solution.py:55
  26.6 45.6 %collective-permute-start.6 = (f32[256,768]{1,0:T(8,128)S(1)}, f32[256,768]{1,0:T(8,128)S(1)}, u32[]{:S(2)}, u32[]{:S(2)}) collective-permute-start(f32[256,768]{1,0:T(8,128)S(1)} %slice.74), channel_id=1, source_target_pairs={{0,2},{2,0},{4,6},{6,4},{8,10},{10,8},{12,14},{14,12},{16,18},{18,... | collective-permute-start | bytes 2359304 | tf_op jit(solution)/shard_map/ppermute | solution.py:55
  27.4 13.5 %collective-permute-start.1 = (f32[128,768]{1,0:T(8,128)S(1)}, f32[128,768]{1,0:T(8,128)S(1)}, u32[]{:S(2)}, u32[]{:S(2)}) collective-permute-start(f32[128,768]{1,0:T(8,128)S(1)} %slice.71), channel_id=1, source_target_pairs={{0,2},{1,15},{2,0},{3,5},{4,6},{5,3},{6,4},{7,9},{8,10},{9,7},{10,... | collective-permute-start | bytes 1179656 | tf_op jit(solution)/shard_map/ppermute | solution.py:55
  33.3 80.3 %slice-start = ((s8[4718592]{0:T(1024)(128)(4,1)}), s8[4194304]{0:T(1024)(128)(4,1)S(1)}, s32[]{:S(2)}) async-start(s8[4718592]{0:T(1024)(128)(4,1)} %bitcast.24), calls=%async_computation | async-start | bytes 8388608
  34.9 12.1 %collective-permute-start.14 = (f32[48,768]{1,0:T(8,128)S(1)}, f32[48,768]{1,0:T(8,128)S(1)}, u32[]{:S(2)}, u32[]{:S(2)}) collective-permute-start(f32[48,768]{1,0:T(8,128)S(1)} %get-tuple-element.25), channel_id=1, source_target_pairs={{0,14},{1,17},{2,4},{3,19},{4,2},{5,21},{6,8},{7,23},{8,6},{9,25},... | collective-permute-start | bytes 442376 | tf_op jit(solution)/shard_map/ppermute | solution.py:55
  36.0 11.0 %collective-permute-start.15 = (f32[48,768]{1,0:T(8,128)S(1)}, f32[48,768]{1,0:T(8,128)S(1)}, u32[]{:S(2)}, u32[]{:S(2)}) collective-permute-start(f32[48,768]{1,0:T(8,128)S(1)} %get-tuple-element.27), channel_id=1, source_target_pairs={{0,14},{1,33},{2,4},{3,35},{4,2},{5,37},{6,8},{7,39},{8,6},{9,41},... | collective-permute-start | bytes 442376 | tf_op jit(solution)/shard_map/ppermute | solution.py:55
  38.9 8.1 %collective-permute-start.16 = (f32[48,768]{1,0:T(8,128)S(1)}, f32[48,768]{1,0:T(8,128)S(1)}, u32[]{:S(2)}, u32[]{:S(2)}) collective-permute-start(f32[48,768]{1,0:T(8,128)S(1)} %get-tuple-element.26), channel_id=1, source_target_pairs={{1,49},{3,51},{5,53},{7,55},{9,57},{11,59},{13,61},{15,63},{17,33}... | collective-permute-start | bytes 442376 | tf_op jit(solution)/shard_map/ppermute | solution.py:55
  40.9 14.3 %collective-permute-start.2 = (f32[64,768]{1,0:T(8,128)S(1)}, f32[64,768]{1,0:T(8,128)S(1)}, u32[]{:S(2)}, u32[]{:S(2)}) collective-permute-start(f32[64,768]{1,0:T(8,128)S(1)} %slice.73), channel_id=1, source_target_pairs={{0,4},{1,13},{2,6},{3,7},{4,0},{5,9},{6,2},{7,3},{8,12},{9,5},{10,... | collective-permute-start | bytes 589832 | tf_op jit(solution)/shard_map/ppermute | solution.py:55
  47.0 6.2 %collective-permute-start.17 = (f32[48,768]{1,0:T(8,128)S(1)}, f32[48,768]{1,0:T(8,128)S(1)}, u32[]{:S(2)}, u32[]{:S(2)}) collective-permute-start(f32[48,768]{1,0:T(8,128)S(1)} %get-tuple-element.21), channel_id=1, source_target_pairs={{0,12},{1,3},{2,6},{3,1},{4,8},{5,7},{6,2},{7,5},{8,4},{9,11},{10,... | collective-permute-start | bytes 442376 | tf_op jit(solution)/shard_map/ppermute | solution.py:55
  53.2 60.4 %slice-start.1 = ((s8[4718592]{0:T(1024)(128)(4,1)}), s8[524288]{0:T(1024)(128)(4,1)S(1)}, s32[]{:S(2)}) async-start(s8[4718592]{0:T(1024)(128)(4,1)} %bitcast.24), calls=%async_computation.1 | async-start | bytes 1048576
  53.2 7.5 %collective-permute-start.18 = (f32[48,768]{1,0:T(8,128)S(1)}, f32[48,768]{1,0:T(8,128)S(1)}, u32[]{:S(2)}, u32[]{:S(2)}) collective-permute-start(f32[48,768]{1,0:T(8,128)S(1)} %add.65), channel_id=1, source_target_pairs={{0,8},{1,5},{2,10},{3,7},{4,12},{5,1},{6,14},{7,3},{8,0},{9,13},{1... | collective-permute-start | bytes 442376 | tf_op jit(solution)/shard_map/ppermute | solution.py:55
  55.2 18.7 %collective-permute-start.3 = (f32[64,768]{1,0:T(8,128)S(1)}, f32[64,768]{1,0:T(8,128)S(1)}, u32[]{:S(2)}, u32[]{:S(2)}) collective-permute-start(f32[64,768]{1,0:T(8,128)S(1)} %add_select_fusion), channel_id=1, source_target_pairs={{0,4},{1,9},{2,6},{3,11},{4,0},{5,13},{6,2},{7,15},{8,12},{9,1},{1... | collective-permute-start | bytes 589832 | tf_op jit(solution)/shard_map/ppermute | solution.py:55
  60.8 15.1 %collective-permute-start.19 = (f32[48,768]{1,0:T(8,128)S(1)}, f32[48,768]{1,0:T(8,128)S(1)}, u32[]{:S(2)}, u32[]{:S(2)}) collective-permute-start(f32[48,768]{1,0:T(8,128)S(1)} %add.66), channel_id=1, source_target_pairs={{0,12},{1,9},{2,6},{3,11},{4,8},{5,13},{6,2},{7,15},{8,4},{9,1},{1... | collective-permute-start | bytes 442376 | tf_op jit(solution)/shard_map/ppermute | solution.py:55
  72.3 52.3 %collective-permute-start.9 = (f32[256,768]{1,0:T(8,128)S(1)}, f32[256,768]{1,0:T(8,128)S(1)}, u32[]{:S(2)}, u32[]{:S(2)}) collective-permute-start(f32[256,768]{1,0:T(8,128)S(1)} %slice_add_fusion.3.refs_2_), channel_id=1, source_target_pairs={{0,1},{1,0},{2,3},{3,2},{4,5},{5,4},{6,7},{7,6},{8,9},{9,8},{10,11... | collective-permute-start | bytes 2359304 | tf_op jit(solution)/shard_map/ppermute | solution.py:55
  74.0 9.5 %collective-permute-start.4 = (f32[64,768]{1,0:T(8,128)S(1)}, f32[64,768]{1,0:T(8,128)S(1)}, u32[]{:S(2)}, u32[]{:S(2)}) collective-permute-start(f32[64,768]{1,0:T(8,128)S(1)} %add.54), channel_id=1, source_target_pairs={{1,13},{3,7},{5,9},{7,3},{9,5},{11,15},{13,1},{15,11},{17,29},{19,... | collective-permute-start | bytes 589832 | tf_op jit(solution)/shard_map/ppermute | solution.py:55
  75.9 14.2 %collective-permute-start.22 = (f32[48,768]{1,0:T(8,128)S(1)}, f32[48,768]{1,0:T(8,128)S(1)}, u32[]{:S(2)}, u32[]{:S(2)}) collective-permute-start(f32[48,768]{1,0:T(8,128)S(1)} %get-tuple-element.20), channel_id=1, source_target_pairs={{1,49},{3,51},{5,53},{7,55},{9,57},{11,59},{13,61},{15,63},{17,33}... | collective-permute-start | bytes 442376 | tf_op jit(solution)/shard_map/ppermute | solution.py:55
  83.5 10.7 %collective-permute-start.20 = (f32[48,768]{1,0:T(8,128)S(1)}, f32[48,768]{1,0:T(8,128)S(1)}, u32[]{:S(2)}, u32[]{:S(2)}) collective-permute-start(f32[48,768]{1,0:T(8,128)S(1)} %get-tuple-element.20), channel_id=1, source_target_pairs={{0,14},{1,17},{2,4},{3,19},{4,2},{5,21},{6,8},{7,23},{8,6},{9,25},... | collective-permute-start | bytes 442376 | tf_op jit(solution)/shard_map/ppermute | solution.py:55
  86.0 8.2 %collective-permute-start.21 = (f32[48,768]{1,0:T(8,128)S(1)}, f32[48,768]{1,0:T(8,128)S(1)}, u32[]{:S(2)}, u32[]{:S(2)}) collective-permute-start(f32[48,768]{1,0:T(8,128)S(1)} %get-tuple-element.19), channel_id=1, source_target_pairs={{0,14},{1,33},{2,4},{3,35},{4,2},{5,37},{6,8},{7,39},{8,6},{9,41},... | collective-permute-start | bytes 442376 | tf_op jit(solution)/shard_map/ppermute | solution.py:55
  94.3 17.4 %collective-permute-start.23 = (f32[192,768]{1,0:T(8,128)S(1)}, f32[192,768]{1,0:T(8,128)S(1)}, u32[]{:S(2)}, u32[]{:S(2)}) collective-permute-start(f32[192,768]{1,0:T(8,128)S(1)} %bitcast.26), channel_id=1, source_target_pairs={{0,16},{1,65},{2,18},{3,67},{4,20},{5,69},{6,22},{7,71},{8,24},{9,... | collective-permute-start | bytes 1769480 | tf_op jit(solution)/shard_map/ppermute | solution.py:55
  100.8 10.3 %collective-permute-start.5 = (f32[128,768]{1,0:T(8,128)S(1)}, f32[128,768]{1,0:T(8,128)S(1)}, u32[]{:S(2)}, u32[]{:S(2)}) collective-permute-start(f32[128,768]{1,0:T(8,128)S(1)} %pad_maximum_fusion.1.refs_0_), channel_id=1, source_target_pairs={{0,2},{1,15},{2,0},{3,5},{4,6},{5,3},{6,4},{7,9},{8,10},{9,7},{10,... | collective-permute-start | bytes 1179656 | tf_op jit(solution)/shard_map/ppermute | solution.py:55
  106.0 5.6 %collective-permute-start.7 = (f32[128,768]{1,0:T(8,128)S(1)}, f32[128,768]{1,0:T(8,128)S(1)}, u32[]{:S(2)}, u32[]{:S(2)}) collective-permute-start(f32[128,768]{1,0:T(8,128)S(1)} %pad_maximum_fusion.1.refs_0_), channel_id=1, source_target_pairs={{0,1},{1,0},{2,3},{3,2},{4,5},{5,4},{6,7},{7,6},{8,9},{9,8},{10,11... | collective-permute-start | bytes 1179656 | tf_op jit(solution)/shard_map/ppermute | solution.py:55
  106.0 7.6 %collective-permute-start.24 = (f32[64,768]{1,0:T(8,128)S(1)}, f32[64,768]{1,0:T(8,128)S(1)}, u32[]{:S(2)}, u32[]{:S(2)}) collective-permute-start(f32[64,768]{1,0:T(8,128)S(1)} %bitcast.34), channel_id=1, source_target_pairs={{0,32},{1,129},{2,34},{3,131},{4,36},{5,133},{6,38},{7,135},{8,40}... | collective-permute-start | bytes 589832 | tf_op jit(solution)/shard_map/ppermute | solution.py:55
  111.1 13.5 %collective-permute-start.8 = (f32[128,768]{1,0:T(8,128)S(1)}, f32[128,768]{1,0:T(8,128)S(1)}, u32[]{:S(2)}, u32[]{:S(2)}) collective-permute-start(f32[128,768]{1,0:T(8,128)S(1)} %collective-permute-done.5.refs_1_), channel_id=1, source_target_pairs={{0,1},{1,0},{2,3},{3,2},{4,5},{5,4},{6,7},{7,6},{8,9},{9,8},{10,11... | collective-permute-start | bytes 1179656 | tf_op jit(solution)/shard_map/ppermute | solution.py:55
  111.6 17.8 %collective-permute-start.26 = (f32[192,768]{1,0:T(8,128)S(1)}, f32[192,768]{1,0:T(8,128)S(1)}, u32[]{:S(2)}, u32[]{:S(2)}) collective-permute-start(f32[192,768]{1,0:T(8,128)S(1)} %bitcast.27), channel_id=1, source_target_pairs={{0,1},{1,0},{2,3},{3,2},{4,5},{5,4},{6,7},{7,6},{8,9},{9,8},{10,11... | collective-permute-start | bytes 1769480 | tf_op jit(solution)/shard_map/ppermute | solution.py:55
  111.7 17.7 %collective-permute-start.27 = (f32[192,768]{1,0:T(8,128)S(1)}, f32[192,768]{1,0:T(8,128)S(1)}, u32[]{:S(2)}, u32[]{:S(2)}) collective-permute-start(f32[192,768]{1,0:T(8,128)S(1)} %collective-permute-done.23.refs_1_), channel_id=1, source_target_pairs={{0,1},{1,0},{2,3},{3,2},{4,5},{5,4},{6,7},{7,6},{8,9},{9,8},{10,11... | collective-permute-start | bytes 1769480 | tf_op jit(solution)/shard_map/ppermute | solution.py:55
  113.6 5.7 %collective-permute-start.25 = (f32[64,768]{1,0:T(8,128)S(1)}, f32[64,768]{1,0:T(8,128)S(1)}, u32[]{:S(2)}, u32[]{:S(2)}) collective-permute-start(f32[64,768]{1,0:T(8,128)S(1)} %bitcast.35), channel_id=1, source_target_pairs={{0,48},{1,193},{2,50},{3,195},{4,52},{5,197},{6,54},{7,199},{8,56}... | collective-permute-start | bytes 589832 | tf_op jit(solution)/shard_map/ppermute | solution.py:55
  119.3 10.1 %collective-permute-start.28 = (f32[64,768]{1,0:T(8,128)S(1)}, f32[64,768]{1,0:T(8,128)S(1)}, u32[]{:S(2)}, u32[]{:S(2)}) collective-permute-start(f32[64,768]{1,0:T(8,128)S(1)} %collective-permute-done.24.refs_2_), channel_id=1, source_target_pairs={{0,1},{1,0},{2,3},{3,2},{4,5},{5,4},{6,7},{7,6},{8,9},{9,8},{10,11... | collective-permute-start | bytes 589832 | tf_op jit(solution)/shard_map/ppermute | solution.py:55
  124.6 4.8 %collective-permute-start.29 = (f32[64,768]{1,0:T(8,128)S(1)}, f32[64,768]{1,0:T(8,128)S(1)}, u32[]{:S(2)}, u32[]{:S(2)}) collective-permute-start(f32[64,768]{1,0:T(8,128)S(1)} %collective-permute-done.25.refs_3_), channel_id=1, source_target_pairs={{0,1},{1,0},{2,3},{3,2},{4,5},{5,4},{6,7},{7,6},{8,9},{9,8},{10,11... | collective-permute-start | bytes 589832 | tf_op jit(solution)/shard_map/ppermute | solution.py:55
  (2 other events, 2.0 us)
where the time goes:
time: 132 us
  starting transfers between devices  78.6 us (60%)
  Pallas kernels  24.5 us (19%)
  waiting for transfers between devices  21.1 us (16%)
  other arithmetic  4.77 us (4%)
  local copies, waits for them, and re-layouts  2.92 us (2%)
    ppermute x30, starting transfers between devices, send(): return lax.ppermute(array, 'leaf', perm)  78.6 us
    ppermute x30, waiting for transfers between devices, send(): return lax.ppermute(array, 'leaf', perm)  21.1 us
    pallas_call x1, Pallas kernels, partials(): pl.pallas_call(functools.partial(partial_kernel, work), out_shape=tuple((...  9.51 us
    pallas_call x3, Pallas kernels, images(): pl.pallas_call(functools.partial(image_kernel, work), out_shape=jax.Shape...  7.54 us
    pallas_call x1, Pallas kernels, first_partials(): pl.pallas_call(first_kernel, out_shape=(jax.ShapeDtypeStruct((2 * S, R),...  5.59 us
  transfers between devices with their start and end apart: 30, of which 6 were waited for; matrix products, arithmetic and copies ran while one was open for 5% of the time, Pallas kernels for 12%

commit v1 on v0

--- a/solution.py
+++ b/solution.py
@@ -6,6 +6,7 @@
 from jax.experimental import pallas as pl
 from jax.experimental.pallas import tpu as pltpu
 from jax.sharding import PartitionSpec as P
+
 
 N = 256
 V = 512
@@ -122,13 +123,16 @@
         out[pl.ds(row, UNIT), :] = product[unit * UNIT : (unit + 1) * UNIT]
 
 
-def first_kernel(me, depth, rhs_hbm, basis_hbm, out, high, low, depth_out, rhs, basis, sems):
+def first_kernel(me, depth_hbm, rhs_hbm, basis_hbm, out, high, low, depth_out, depth, rhs, basis, sems):
     levels, masks = slots(me[0], 1 - (me[0] & 1))
     copies = [pltpu.make_async_copy(rhs_hbm, rhs, sems.at[0])]
     for slot in (0, 1):
         copies.append(pltpu.make_async_copy(basis_hbm.at[levels[slot]], basis.at[slot], sems.at[slot + 1]))
+    depth_copy = pltpu.make_async_copy(depth_hbm, depth, sems.at[3])
+    depth_copy.start()
     for copy in copies:
         copy.start()
+    depth_copy.wait()
     depth_out[...] = jnp.broadcast_to(depth[...].astype(jnp.float32), (128, V)).T
     copies[0].wait()
     high[...], low[...] = split(rhs[...])
@@ -147,47 +151,37 @@
             jax.ShapeDtypeStruct((V, R), jnp.bfloat16),
             jax.ShapeDtypeStruct((V, 128), jnp.float32),
         ),
-        in_specs=[SMEM, VMEM, HBM, HBM],
+        in_specs=[SMEM, HBM, HBM, HBM],
         out_specs=(VMEM,) * 4,
         scratch_shapes=[
+            pltpu.VMEM((1, V), jnp.int32),
             pltpu.VMEM((V, R), jnp.float32),
             pltpu.VMEM((2, V, S), jnp.float32),
-            pltpu.SemaphoreType.DMA((3,)),
+            pltpu.SemaphoreType.DMA((4,)),
         ],
-        compiler_params=pltpu.CompilerParams(vmem_limit_bytes=52 << 20),
+        compiler_params=pltpu.CompilerParams(vmem_limit_bytes=50 << 20),
         cost_estimate=pl.CostEstimate(flops=12 * R * S * V, bytes_accessed=2 * 4 * S * (R + V), transcendentals=0),
         name="send_ab",
     )(me, depth, rhs, basis)
 
 
-def partial_kernel(work, me, high, low, depth, basis_hbm, *refs):
-    outs, (basis, sems) = refs[:-2], refs[-2:]
-    sides = [slots(me[0], me[0] & 1), slots(me[0], 1 - (me[0] & 1))]
-    copies = []
-    for number, (_, slot, other) in enumerate(work):
-        copy = pltpu.make_async_copy(basis_hbm.at[sides[other][0][slot]], basis.at[number], sems.at[number])
-        copy.start()
-        copies.append(copy)
-    for number, (out, slot, other) in enumerate(work):
-        copies[number].wait()
-        levels, masks = sides[other]
-        product = dot3(masked(basis.at[number][...], depth, levels[slot]), (high[...], low[...]), 0)
-        put(product, outs[out], slot, masks[slot])
-
-
-def partials(work, me, high, low, depth, basis, name):
-    count = 1 + max(out for out, _, _ in work)
+def partial_kernel(work, me, high, low, depth, basis, out):
+    for slot, other in work:
+        levels, masks = slots(me[0], (me[0] & 1) ^ other)
+        product = dot3(masked(basis[levels[slot]], depth, levels[slot]), (high[...], low[...]), 0)
+        put(product, out, slot, masks[slot])
+
+
+def partials(work, me, high, low, depth, basis):
     return pl.pallas_call(
         functools.partial(partial_kernel, work),
-        out_shape=tuple(jax.ShapeDtypeStruct((2 * S, R), jnp.float32) for _ in range(count)),
-        in_specs=[SMEM, VMEM, VMEM, VMEM, HBM],
-        out_specs=(VMEM,) * count,
-        scratch_shapes=[pltpu.VMEM((len(work), V, S), jnp.float32), pltpu.SemaphoreType.DMA((len(work),))],
-        compiler_params=pltpu.CompilerParams(vmem_limit_bytes=45 << 20),
+        out_shape=jax.ShapeDtypeStruct((2 * S, R), jnp.float32),
+        in_specs=[SMEM, VMEM, VMEM, VMEM, VMEM],
+        out_specs=VMEM,
+        compiler_params=pltpu.CompilerParams(vmem_limit_bytes=12 << 20),
         cost_estimate=pl.CostEstimate(
-            flops=len(work) * 6 * R * S * V, bytes_accessed=len(work) * 4 * S * (R + V), transcendentals=0
+            flops=12 * R * S * V, bytes_accessed=8 * S * (R + V), transcendentals=0
         ),
-        name=name,
     )(me, high, low, depth, basis)
 
 
@@ -202,40 +196,52 @@
         out_shape=jax.ShapeDtypeStruct((V, R), jnp.float32),
         in_specs=[VMEM, VMEM, VMEM, VMEM],
         out_specs=VMEM,
-        compiler_params=pltpu.CompilerParams(vmem_limit_bytes=16 << 20),
+        compiler_params=pltpu.CompilerParams(vmem_limit_bytes=12 << 20),
         cost_estimate=pl.CostEstimate(flops=12 * R * S * V, bytes_accessed=4 * V * R, transcendentals=0),
         name="leaf",
     )(high, low, depth, basis)
 
 
-def image_kernel(work, me, depth, before, basis, *refs):
-    pieces, (out, high, low) = refs[:-3], refs[-3:]
-    sides = [slots(me[0], me[0] & 1), slots(me[0], 1 - (me[0] & 1))]
-    for number, (slot, other, plan) in enumerate(work):
-        levels, masks = sides[other]
+def image_kernel(work, me, depth, before, basis_hbm, *refs):
+    pieces, (out, basis, high, low, sems) = refs[:-5], refs[-5:]
+    sides = [slots(me[0], (me[0] & 1) ^ other) for _, other, _ in work]
+    copies = []
+    for number, (slot, _, _) in enumerate(work):
+        copy = pltpu.make_async_copy(basis_hbm.at[sides[number][0][slot]], basis.at[number], sems.at[number])
+        copy.start()
+        copies.append(copy)
+    for number, (slot, _, plan) in enumerate(work):
+        mask = sides[number][1][slot]
         for unit, (piece, start) in enumerate(plan):
-            row = pl.multiple_of(UNIT * (unit ^ masks[slot]), UNIT)
+            row = pl.multiple_of(UNIT * (unit ^ mask), UNIT)
             part_high, part_low = split(pieces[piece][start : start + UNIT, :])
             high[number, pl.ds(row, UNIT), :] = part_high
             low[number, pl.ds(row, UNIT), :] = part_low
-        own = masked(basis[levels[slot]], depth, levels[slot])
+    for copy in copies:
+        copy.wait()
+    for number, (slot, _, _) in enumerate(work):
+        own = masked(basis.at[number][...], depth, sides[number][0][slot])
         image = dot3(own, (high[number], low[number]), 1)
         out[...] = (before[...] if number == 0 else out[...]) + image
 
 
-def images(work, me, depth, before, basis, pieces, name):
+def images(work, me, depth, before, basis, pieces):
     count = len(work)
     return pl.pallas_call(
         functools.partial(image_kernel, work),
         out_shape=jax.ShapeDtypeStruct((V, R), jnp.float32),
-        in_specs=[SMEM, VMEM, VMEM, VMEM] + [VMEM] * len(pieces),
+        in_specs=[SMEM, VMEM, VMEM, HBM] + [VMEM] * len(pieces),
         out_specs=VMEM,
-        scratch_shapes=[pltpu.VMEM((count, S, R), jnp.bfloat16), pltpu.VMEM((count, S, R), jnp.bfloat16)],
-        compiler_params=pltpu.CompilerParams(vmem_limit_bytes=16 << 20),
+        scratch_shapes=[
+            pltpu.VMEM((count, V, S), jnp.float32),
+            pltpu.VMEM((count, S, R), jnp.bfloat16),
+            pltpu.VMEM((count, S, R), jnp.bfloat16),
+            pltpu.SemaphoreType.DMA((count,)),
+        ],
+        compiler_params=pltpu.CompilerParams(vmem_limit_bytes=50 << 20),
         cost_estimate=pl.CostEstimate(
             flops=count * 6 * R * S * V, bytes_accessed=count * 4 * S * (R + V), transcendentals=0
         ),
-        name=name,
     )(me, depth, before, basis, *pieces)
 
 
@@ -258,32 +264,56 @@
 PLAN_D = [(2, u * UNIT) for u in range(UNITS)]
 
 
-def body(basis, rhs, vertex_tier_depth):
+def local(kernel, rows, *arrays):
+    return pl.pallas_call(
+        kernel,
+        out_shape=tuple(jax.ShapeDtypeStruct((height, R), jnp.float32) for height in rows),
+        in_specs=[VMEM] * len(arrays),
+        out_specs=(VMEM,) * len(rows),
+        compiler_params=pltpu.CompilerParams(vmem_limit_bytes=8 << 20),
+    )(*arrays)
+
+
+def cut_kernel(kept, got, *outs):
+    start = 0
+    for out in outs:
+        part = slice(start, start + out.shape[0])
+        out[...] = kept[part, :] + got[part, :]
+        start = part.stop
+
+
+def join_kernel(base, r1, r2, r3, *outs):
+    for quarter, out in enumerate(outs):
+        at = quarter * 48
+        top = slice(quarter * UNIT, (quarter + 1) * UNIT)
+        out[:UNIT, :] = (base[at : at + UNIT, :] + r1[at : at + UNIT, :]) + (r2[top, :] + r3[top, :])
+        out[UNIT:, :] = base[at + UNIT : at + 48, :] + r1[at + UNIT : at + 48, :]
+
+
+def steps(basis, rhs, vertex_tier_depth):
     index_here = lax.axis_index("leaf")
     first = (index_here & 1) == 0
     me = index_here.reshape(1)
 
     send_ab, high, low, depth = first_partials(me, vertex_tier_depth.reshape(1, V), rhs, basis)
     got_ab = send(send_ab, SWAP)
-    keep_ab, send_cd, keep_cd = partials(
-        [(0, 0, 0), (0, 1, 0), (1, 2, 1), (1, 3, 1), (2, 2, 0), (2, 3, 0)], me, high, low, depth, basis, "rest"
-    )
+    keep_ab = partials([(0, 0), (1, 0)], me, high, low, depth, basis)
+
+    step = [None] + [pairs(along_y(j), along_x(j)) for j in (1, 2, 3)]
+    base, s1, s2, s3 = local(cut_kernel, (192, 192, 64, 64), keep_ab, got_ab)
+    r1 = send(s1, step[1])
+    r2 = send(s2, step[2])
+    r3 = send(s3, step[3])
+
+    send_cd = partials([(2, 1), (3, 1)], me, high, low, depth, basis)
     got_cd = send(send_cd, SWAP)
-
-    step = [None] + [pairs(along_y(j), along_x(j)) for j in (1, 2, 3)]
-    ab = keep_ab + got_ab
-    r1 = send(ab[192:384], step[1])
-    r2 = send(ab[384:448], step[2])
-    r3 = send(ab[448:512], step[3])
-
+    keep_cd = partials([(2, 0), (3, 0)], me, high, low, depth, basis)
     near, mid = pairs(along_z(1), shifted_z(1)), pairs(along_z(2), shifted_z(2))
-    cd = keep_cd + got_cd
-    c, d = cd[:S], cd[S:]
-    c = c[:128] + send(c[128:], near)
+    c_low, c_high, d = local(cut_kernel, (128, 128, 256), keep_cd, got_cd)
+    c = c_low + send(c_high, near)
     d = d + send(d, pairs(along_z(1), None))
 
-    both = (ab[:192] + r1).reshape(4, 48, R)
-    both = jnp.concatenate([both[:, :UNIT] + (r2 + r3).reshape(4, UNIT, R), both[:, UNIT:]], 1)
+    both = local(join_kernel, (48,) * 4, base, r1, r2, r3)
     t1 = send(both[1], pairs(shifted_z(1), along_y(1)))
     t2 = send(both[2], pairs(shifted_z(1), along_y(2)))
     t3 = send(both[3], pairs(None, along_y(3)))
@@ -299,7 +329,8 @@
     done = jnp.stack([total, g1, g2, jnp.where(first, other, g3)])
     top = done[:, :UNIT].reshape(64, R)
     done = done.reshape(192, R)
-    ab_pieces = (done, send(done, step[1]), send(top, step[2]), send(top, step[3]))
+    q1, q2, q3 = send(done, step[1]), send(top, step[2]), send(top, step[3])
+    ab_pieces = (done, q1, q2, q3)
 
     m2 = send(c[64:], mid)
     c_low = jnp.where(first, c[:64], c[:64] + m2)
@@ -315,13 +346,13 @@
     result = leaf(high, low, depth, basis)
     result = images(
         [(2, 0, PLAN_C), (3, 0, PLAN_D), (2, 1, shift_pieces(PLAN_C, 3)), (3, 1, shift_pieces(PLAN_D, 3))],
-        me, depth, result, basis, cd_pieces + their_cd, "image_cd",
+        me, depth, result, basis, cd_pieces + their_cd,
     )
-    result = images([(0, 0, plan_ab(0)), (1, 0, plan_ab(1))], me, depth, result, basis, ab_pieces, "image_own")
-    return images([(0, 1, plan_ab(0)), (1, 1, plan_ab(1))], me, depth, result, basis, their_ab, "image_last")
+    result = images([(0, 0, plan_ab(0)), (1, 0, plan_ab(1))], me, depth, result, basis, ab_pieces)
+    return images([(0, 1, plan_ab(0)), (1, 1, plan_ab(1))], me, depth, result, basis, their_ab)
 
 
 def solution(mesh):
     in_specs = (P(None, "leaf", None), P("leaf", None), P("leaf"))
     out_specs = P("leaf", None)
-    return jax.shard_map(body, mesh=mesh, in_specs=in_specs, out_specs=out_specs, check_vma=False)
+    return jax.shard_map(steps, mesh=mesh, in_specs=in_specs, out_specs=out_specs, check_vma=False)

time: 132 us -> 134 us (1.015)
  starting transfers between devices: 78.6 us -> 60.3 us
  waiting for transfers between devices: 21.1 us -> 35.6 us
  Pallas kernels: 24.5 us -> 28.7 us
  local copies, waits for them, and re-layouts: 2.92 us -> 6.07 us
  other arithmetic: 4.77 us -> 2.62 us
    ppermute x30, starting transfers between devices: 78.6 us -> 60.3 us  [send(): return lax.ppermute(array, 'leaf', perm)]
    ppermute x30, waiting for transfers between devices: 21.1 us -> 35.6 us  [send(): return lax.ppermute(array, 'leaf', perm)]
    pallas_call x3, Pallas kernels: 7.54 us -> 15 us  [images(): pl.pallas_call(functools.partial(image_kernel, work), out_shape=jax.Shape...]
    unnamed x8 -> x16, local copies, waits for them, and re-layouts: 1.12 us -> 6.04 us
    add x10 -> x5, other arithmetic: 4.52 us -> 1.29 us  [the longest x1 1.09 us: steps(): total + send(jnp.where(first, passed, total), pairs(shifted_z(2), along_z...]
    pallas_call x1 -> x6, Pallas kernels: 9.51 us -> 7.23 us  [the longest x3 4.48 us: partials(): pl.pallas_call(functools.partial(partial_kernel, work), out_shape=jax.Sha...]
    slice x7 -> x2, local copies, waits for them, and re-layouts: 1.8 us -> 0.03 us  [the longest x1 0.01 us: steps(): m2 = send(c[64:], mid)]
  transfers between devices with their start and end apart: 30 -> 30, of which waited for: 6 -> 9; matrix products, arithmetic and copies ran while one was open for 5% -> 2% of each run, Pallas kernels for 12% -> 15%
where the time goes in v1:
time: 134 us
  starting transfers between devices  60.3 us (45%)
  waiting for transfers between devices  35.6 us (27%)
  Pallas kernels  28.7 us (21%)
  local copies, waits for them, and re-layouts  6.07 us (5%)
  other arithmetic  2.62 us (2%)
    ppermute x30, starting transfers between devices, send(): return lax.ppermute(array, 'leaf', perm)  60.3 us
    ppermute x30, waiting for transfers between devices, send(): return lax.ppermute(array, 'leaf', perm)  35.6 us
    pallas_call x3, Pallas kernels, images(): pl.pallas_call(functools.partial(image_kernel, work), out_shape=jax.Shape...  15 us
    unnamed x16, local copies, waits for them, and re-layouts  6.04 us
    pallas_call x1, Pallas kernels, first_partials(): pl.pallas_call(first_kernel, out_shape=(jax.ShapeDtypeStruct((2 * S, R),...  4.61 us
    pallas_call x3, Pallas kernels, partials(): pl.pallas_call(functools.partial(partial_kernel, work), out_shape=jax.Sha...  4.48 us
    pallas_call x3, Pallas kernels, local(): pl.pallas_call(kernel, out_shape=tuple((jax.ShapeDtypeStruct((height, R),...  2.74 us
  transfers between devices with their start and end apart: 30, of which 9 were waited for; matrix products, arithmetic and copies ran while one was open for 2% of the time, Pallas kernels for 15%

profile of v1, /device:TPU:1, one launch (start us, length us, event | category | flops | bytes accessed | tf_op | source)
XLA Modules:
  0.0 133.8 jit_solution(16170741602776080538)
XLA Ops:
  0.7 4.6 %send_ab.1 = (f32[512,768]{1,0:T(8,128)S(1)}, bf16[512,768]{1,0:T(8,128)(2,1)S(1)}, bf16[512,768]{1,0:T(8,128)(2,1)S(1)}, f32[512,128]{1,0:T(8,128)S(1)}) custom-call(s32[1]{0:T(128)} %bitcast.me, s32[1,512]{1,0:T(1,128)S(1)} %bitcast.14, f32[512,768]{1,0:T(8,128)} %rhs_hbm.1, f32[9,512,256]{2,1,0:T(8,128)} %basis_hbm.7), custom_call_target="tpu_custom_call" | custom-call | flops 1207959552 | bytes 2621440 | tf_op jit(solution)/shard_map/send_ab/pallas_call | solution.py:146
  5.3 3.3 %collective-permute-start.10 = (f32[512,768]{1,0:T(8,128)S(1)}, f32[512,768]{1,0:T(8,128)S(1)}, u32[]{:S(2)}, u32[]{:S(2)}) collective-permute-start(f32[512,768]{1,0:T(8,128)S(1)} %get-tuple-element.26), channel_id=1, source_target_pairs={{0,1},{1,0},{2,3},{3,2},{4,5},{5,4},{6,7},{7,6},{8,9},{9,8},{10,11... | collective-permute-start | bytes 4718600 | tf_op jit(solution)/shard_map/ppermute | solution.py:56
  8.6 1.5 %shard_map.38 = f32[512,768]{1,0:T(8,128)S(1)} custom-call(s32[1]{0:T(128)} %bitcast.me, bf16[512,768]{1,0:T(8,128)(2,1)S(1)} %get-tuple-element.21.high, bf16[512,768]{1,0:T(8,128)(2,1)S(1)} %get-tuple-element.22.low, f32[512,128]{1,0:T(8,128)S(1)} %get-tuple-element.20.depth, f32[9,512,256]{2,1,0:T(8,128)S(1)} %copy-done), custom_call_target="tpu_custom_call" | custom-call | flops 1207959552 | bytes 2621440 | tf_op jit(solution)/shard_map/pallas_call | solution.py:176
  10.2 1.5 %shard_map.41.kept = f32[512,768]{1,0:T(8,128)S(1)} custom-call(s32[1]{0:T(128)} %bitcast.me, bf16[512,768]{1,0:T(8,128)(2,1)S(1)} %get-tuple-element.21.high, bf16[512,768]{1,0:T(8,128)(2,1)S(1)} %get-tuple-element.22.low, f32[512,128]{1,0:T(8,128)S(1)} %get-tuple-element.20.depth, f32[9,512,256]{2,1,0:T(8,128)S(1)} %copy-done), custom_call_target="tpu_custom_call" | custom-call | flops 1207959552 | bytes 2621440 | tf_op jit(solution)/shard_map/pallas_call | solution.py:176
  12.0 1.9 %collective-permute-start.12 = (f32[64,768]{1,0:T(8,128)S(1)}, f32[64,768]{1,0:T(8,128)S(1)}, u32[]{:S(2)}, u32[]{:S(2)}) collective-permute-start(f32[64,768]{1,0:T(8,128)S(1)} %get-tuple-element.29), channel_id=1, source_target_pairs={{0,32},{1,129},{2,34},{3,131},{4,36},{5,133},{6,38},{7,135},{8,40}... | collective-permute-start | bytes 589832 | tf_op jit(solution)/shard_map/ppermute | solution.py:56
  14.0 1.9 %collective-permute-start.13 = (f32[64,768]{1,0:T(8,128)S(1)}, f32[64,768]{1,0:T(8,128)S(1)}, u32[]{:S(2)}, u32[]{:S(2)}) collective-permute-start(f32[64,768]{1,0:T(8,128)S(1)} %get-tuple-element.30), channel_id=1, source_target_pairs={{0,48},{1,193},{2,50},{3,195},{4,52},{5,197},{6,54},{7,199},{8,56}... | collective-permute-start | bytes 589832 | tf_op jit(solution)/shard_map/ppermute | solution.py:56
  15.9 7.8 %collective-permute-done.12.r2 = f32[64,768]{1,0:T(8,128)S(1)} collective-permute-done((f32[64,768]{1,0:T(8,128)S(1)}, f32[64,768]{1,0:T(8,128)S(1)}, u32[]{:S(2)}, u32[]{:S(2)}) %collective-permute-start.12) | collective-permute-done | bytes 196640 | tf_op jit(solution)/shard_map/ppermute | solution.py:56
  25.5 2.9 %collective-permute-start.15 = (f32[48,768]{1,0:T(8,128)}, f32[48,768]{1,0:T(8,128)}, u32[]{:S(2)}, u32[]{:S(2)}) collective-permute-start(f32[48,768]{1,0:T(8,128)} %get-tuple-element.33), channel_id=1, source_target_pairs={{0,14},{1,33},{2,4},{3,35},{4,2},{5,37},{6,8},{7,39},{8,6},{9,41},... | collective-permute-start | bytes 442376 | tf_op jit(solution)/shard_map/ppermute | solution.py:56
  28.4 1.9 %collective-permute-start.16 = (f32[48,768]{1,0:T(8,128)}, f32[48,768]{1,0:T(8,128)}, u32[]{:S(2)}, u32[]{:S(2)}) collective-permute-start(f32[48,768]{1,0:T(8,128)} %get-tuple-element.34), channel_id=1, source_target_pairs={{1,49},{3,51},{5,53},{7,55},{9,57},{11,59},{13,61},{15,63},{17,33}... | collective-permute-start | bytes 442376 | tf_op jit(solution)/shard_map/ppermute | solution.py:56
  30.3 2.3 %copy-done.1 = f32[9,512,256]{2,1,0:T(8,128)S(1)} copy-done((f32[9,512,256]{2,1,0:T(8,128)S(1)}, f32[9,512,256]{2,1,0:T(8,128)}, u32[]{:S(2)}) %copy-start.1) | copy-done | bytes 4718616
  32.6 1.5 %shard_map.37.kept = f32[512,768]{1,0:T(8,128)S(1)} custom-call(s32[1]{0:T(128)} %bitcast.me, bf16[512,768]{1,0:T(8,128)(2,1)S(1)} %get-tuple-element.21.high, bf16[512,768]{1,0:T(8,128)(2,1)S(1)} %get-tuple-element.22.low, f32[512,128]{1,0:T(8,128)S(1)} %get-tuple-element.20.depth, f32[9,512,256]{2,1,0:T(8,128)S(1)} %copy-done.1), custom_call_target="tpu_custom_call" | custom-call | flops 1207959552 | bytes 2621440 | tf_op jit(solution)/shard_map/pallas_call | solution.py:176
  34.2 1.7 %shard_map.39 = (f32[128,768]{1,0:T(8,128)S(1)}, f32[128,768]{1,0:T(8,128)S(1)}, f32[256,768]{1,0:T(8,128)S(1)}) custom-call(f32[512,768]{1,0:T(8,128)S(1)} %shard_map.37.kept, f32[512,768]{1,0:T(8,128)} %collective-permute-done.got), custom_call_target="tpu_custom_call" | custom-call | tf_op jit(solution)/shard_map/pallas_call | solution.py:268
  35.9 5.6 %collective-permute-start.1 = (f32[128,768]{1,0:T(8,128)S(1)}, f32[128,768]{1,0:T(8,128)S(1)}, u32[]{:S(2)}, u32[]{:S(2)}) collective-permute-start(f32[128,768]{1,0:T(8,128)S(1)} %get-tuple-element.24), channel_id=1, source_target_pairs={{0,2},{1,15},{2,0},{3,5},{4,6},{5,3},{6,4},{7,9},{8,10},{9,7},{10,... | collective-permute-start | bytes 1179656 | tf_op jit(solution)/shard_map/ppermute | solution.py:56
  43.5 3.4 %collective-permute-done.1 = f32[128,768]{1,0:T(8,128)S(1)} collective-permute-done((f32[128,768]{1,0:T(8,128)S(1)}, f32[128,768]{1,0:T(8,128)S(1)}, u32[]{:S(2)}, u32[]{:S(2)}) %collective-permute-start.1) | collective-permute-done | bytes 393248 | tf_op jit(solution)/shard_map/ppermute | solution.py:56
  46.9 3.8 %collective-permute-start.2 = (f32[64,768]{1,0:T(8,128)S(1)}, f32[64,768]{1,0:T(8,128)S(1)}, u32[]{:S(2)}, u32[]{:S(2)}) collective-permute-start(f32[64,768]{1,0:T(8,128)S(1)} %slice.15), channel_id=1, source_target_pairs={{0,4},{1,13},{2,6},{3,7},{4,0},{5,9},{6,2},{7,3},{8,12},{9,5},{10,... | collective-permute-start | bytes 589832 | tf_op jit(solution)/shard_map/ppermute | solution.py:56
  52.5 8.6 %collective-permute-done.2 = f32[64,768]{1,0:T(8,128)S(1)} collective-permute-done((f32[64,768]{1,0:T(8,128)S(1)}, f32[64,768]{1,0:T(8,128)S(1)}, u32[]{:S(2)}, u32[]{:S(2)}) %collective-permute-start.2) | collective-permute-done | bytes 196640 | tf_op jit(solution)/shard_map/ppermute | solution.py:56
  61.1 4.0 %collective-permute-start.3 = (f32[64,768]{1,0:T(8,128)S(1)}, f32[64,768]{1,0:T(8,128)S(1)}, u32[]{:S(2)}, u32[]{:S(2)}) collective-permute-start(f32[64,768]{1,0:T(8,128)S(1)} %add_select_fusion), channel_id=1, source_target_pairs={{0,4},{1,9},{2,6},{3,11},{4,0},{5,13},{6,2},{7,15},{8,12},{9,1},{1... | collective-permute-start | bytes 589832 | tf_op jit(solution)/shard_map/ppermute | solution.py:56
  65.1 1.5 %collective-permute-start.19 = (f32[48,768]{1,0:T(8,128)S(1)}, f32[48,768]{1,0:T(8,128)S(1)}, u32[]{:S(2)}, u32[]{:S(2)}) collective-permute-start(f32[48,768]{1,0:T(8,128)S(1)} %add.46), channel_id=1, source_target_pairs={{0,12},{1,9},{2,6},{3,11},{4,8},{5,13},{6,2},{7,15},{8,4},{9,1},{1... | collective-permute-start | bytes 442376 | tf_op jit(solution)/shard_map/ppermute | solution.py:56
  66.8 15.9 %collective-permute-start.9 = (f32[256,768]{1,0:T(8,128)S(1)}, f32[256,768]{1,0:T(8,128)S(1)}, u32[]{:S(2)}, u32[]{:S(2)}) collective-permute-start(f32[256,768]{1,0:T(8,128)S(1)} %add.40.refs_2_), channel_id=1, source_target_pairs={{0,1},{1,0},{2,3},{3,2},{4,5},{5,4},{6,7},{7,6},{8,9},{9,8},{10,11... | collective-permute-start | bytes 2359304 | tf_op jit(solution)/shard_map/ppermute | solution.py:56
  82.7 1.9 %collective-permute-start.4 = (f32[64,768]{1,0:T(8,128)S(1)}, f32[64,768]{1,0:T(8,128)S(1)}, u32[]{:S(2)}, u32[]{:S(2)}) collective-permute-start(f32[64,768]{1,0:T(8,128)S(1)} %add.38), channel_id=1, source_target_pairs={{1,13},{3,7},{5,9},{7,3},{9,5},{11,15},{13,1},{15,11},{17,29},{19,... | collective-permute-start | bytes 589832 | tf_op jit(solution)/shard_map/ppermute | solution.py:56
  84.7 4.0 %collective-permute-start.22 = (f32[48,768]{1,0:T(8,128)S(1)}, f32[48,768]{1,0:T(8,128)S(1)}, u32[]{:S(2)}, u32[]{:S(2)}) collective-permute-start(f32[48,768]{1,0:T(8,128)S(1)} %get-tuple-element.36), channel_id=1, source_target_pairs={{1,49},{3,51},{5,53},{7,55},{9,57},{11,59},{13,61},{15,63},{17,33}... | collective-permute-start | bytes 442376 | tf_op jit(solution)/shard_map/ppermute | solution.py:56
  88.7 2.6 %collective-permute-done.4 = f32[64,768]{1,0:T(8,128)S(1)} collective-permute-done((f32[64,768]{1,0:T(8,128)S(1)}, f32[64,768]{1,0:T(8,128)S(1)}, u32[]{:S(2)}, u32[]{:S(2)}) %collective-permute-start.4) | collective-permute-done | bytes 196640 | tf_op jit(solution)/shard_map/ppermute | solution.py:56
  91.4 3.2 %collective-permute-start.21 = (f32[48,768]{1,0:T(8,128)S(1)}, f32[48,768]{1,0:T(8,128)S(1)}, u32[]{:S(2)}, u32[]{:S(2)}) collective-permute-start(f32[48,768]{1,0:T(8,128)S(1)} %get-tuple-element.35), channel_id=1, source_target_pairs={{0,14},{1,33},{2,4},{3,35},{4,2},{5,37},{6,8},{7,39},{8,6},{9,41},... | collective-permute-start | bytes 442376 | tf_op jit(solution)/shard_map/ppermute | solution.py:56
  95.7 3.0 %collective-permute-done.21 = f32[48,768]{1,0:T(8,128)S(1)} collective-permute-done((f32[48,768]{1,0:T(8,128)S(1)}, f32[48,768]{1,0:T(8,128)S(1)}, u32[]{:S(2)}, u32[]{:S(2)}) %collective-permute-start.21) | collective-permute-done | bytes 147488 | tf_op jit(solution)/shard_map/ppermute | solution.py:56
  99.5 1.9 %collective-permute-start.24 = (f32[64,768]{1,0:T(8,128)S(1)}, f32[64,768]{1,0:T(8,128)S(1)}, u32[]{:S(2)}, u32[]{:S(2)}) collective-permute-start(f32[64,768]{1,0:T(8,128)S(1)} %bitcast.16), channel_id=1, source_target_pairs={{0,32},{1,129},{2,34},{3,131},{4,36},{5,133},{6,38},{7,135},{8,40}... | collective-permute-start | bytes 589832 | tf_op jit(solution)/shard_map/ppermute | solution.py:56
  101.4 6.1 %collective-permute-done.5.refs_1_ = f32[128,768]{1,0:T(8,128)S(1)} collective-permute-done((f32[128,768]{1,0:T(8,128)S(1)}, f32[128,768]{1,0:T(8,128)S(1)}, u32[]{:S(2)}, u32[]{:S(2)}) %collective-permute-start.5) | collective-permute-done | bytes 393248 | tf_op jit(solution)/shard_map/ppermute | solution.py:56
  108.1 2.0 %collective-permute-done.24.refs_2_ = f32[64,768]{1,0:T(8,128)S(1)} collective-permute-done((f32[64,768]{1,0:T(8,128)S(1)}, f32[64,768]{1,0:T(8,128)S(1)}, u32[]{:S(2)}, u32[]{:S(2)}) %collective-permute-start.24) | collective-permute-done | bytes 196640 | tf_op jit(solution)/shard_map/ppermute | solution.py:56
  110.1 1.9 %collective-permute-start.25 = (f32[64,768]{1,0:T(8,128)S(1)}, f32[64,768]{1,0:T(8,128)S(1)}, u32[]{:S(2)}, u32[]{:S(2)}) collective-permute-start(f32[64,768]{1,0:T(8,128)S(1)} %bitcast.17), channel_id=1, source_target_pairs={{0,48},{1,193},{2,50},{3,195},{4,52},{5,197},{6,54},{7,199},{8,56}... | collective-permute-start | bytes 589832 | tf_op jit(solution)/shard_map/ppermute | solution.py:56
  112.1 1.9 %leaf.1.before = f32[512,768]{1,0:T(8,128)S(1)} custom-call(bf16[512,768]{1,0:T(8,128)(2,1)S(1)} %get-tuple-element.21.high, bf16[512,768]{1,0:T(8,128)(2,1)S(1)} %get-tuple-element.22.low, f32[512,128]{1,0:T(8,128)S(1)} %get-tuple-element.20.depth, f32[9,512,256]{2,1,0:T(8,128)S(1)} %bitcast.10), custom_call_target="tpu_custom_call" | custom-call | flops 1207959552 | bytes 1572864 | tf_op jit(solution)/shard_map/leaf/pallas_call | solution.py:194
  116.7 6.9 %shard_map.40.before = f32[512,768]{1,0:T(8,128)} custom-call(s32[1]{0:T(128)} %bitcast.me, f32[512,128]{1,0:T(8,128)S(1)} %get-tuple-element.20.depth, f32[512,768]{1,0:T(8,128)} %copy-done.2, f32[9,512,256]{2,1,0:T(8,128)} %basis_hbm.7, f32[128,768]{1,0:T(8,128)S(1)} %pad_maximum_fusion.1.refs_0_, f32[128,768]{1,0:T(8,128)S(1)} %collective-permute-done.5.refs_1_, ...), custom_call_target="tpu_custom_call" | custom-call | flops 2415919104 | bytes 5242880 | tf_op jit(solution)/shard_map/pallas_call | solution.py:230
  123.6 4.1 %shard_map.44.before = f32[512,768]{1,0:T(8,128)S(1)} custom-call(s32[1]{0:T(128)} %bitcast.me, f32[512,128]{1,0:T(8,128)S(1)} %get-tuple-element.20.depth, f32[512,768]{1,0:T(8,128)} %shard_map.40.before, f32[9,512,256]{2,1,0:T(8,128)} %basis_hbm.7, f32[192,768]{1,0:T(8,128)S(1)} %bitcast.13, f32[192,768]{1,0:T(8,128)S(1)} %collective-permute-done.23.refs_1_, ...), custom_call_target="tpu_custom_call" | custom-call | flops 1207959552 | bytes 2621440 | tf_op jit(solution)/shard_map/pallas_call | solution.py:230
  129.7 3.9 %shard_map.45 = f32[512,768]{1,0:T(8,128)} custom-call(s32[1]{0:T(128)} %bitcast.me, f32[512,128]{1,0:T(8,128)S(1)} %get-tuple-element.20.depth, f32[512,768]{1,0:T(8,128)S(1)} %shard_map.44.before, f32[9,512,256]{2,1,0:T(8,128)} %basis_hbm.7, f32[192,768]{1,0:T(8,128)S(1)} %collective-permute-done.26.refs_0_, f32[192,768]{1,0:T(8,128)S(1)} %copy-done.4, ...), custom_call_target="tpu_custom_call" | custom-call | flops 1207959552 | bytes 2621440 | tf_op jit(solution)/shard_map/pallas_call | solution.py:230
  (70 shorter events, 14.0 us)
Async XLA Ops:
  5.3 6.4 %collective-permute-start.10 = (f32[512,768]{1,0:T(8,128)S(1)}, f32[512,768]{1,0:T(8,128)S(1)}, u32[]{:S(2)}, u32[]{:S(2)}) collective-permute-start(f32[512,768]{1,0:T(8,128)S(1)} %get-tuple-element.26), channel_id=1, source_target_pairs={{0,1},{1,0},{2,3},{3,2},{4,5},{5,4},{6,7},{7,6},{8,9},{9,8},{10,11... | collective-permute-start | bytes 4718600 | tf_op jit(solution)/shard_map/ppermute | solution.py:56
  10.1 24.0 %collective-permute-start = (f32[512,768]{1,0:T(8,128)S(1)}, f32[512,768]{1,0:T(8,128)}, u32[]{:S(2)}, u32[]{:S(2)}) collective-permute-start(f32[512,768]{1,0:T(8,128)S(1)} %shard_map.38), channel_id=1, source_target_pairs={{0,1},{1,0},{2,3},{3,2},{4,5},{5,4},{6,7},{7,6},{8,9},{9,8},{10,11... | collective-permute-start | bytes 4718600 | tf_op jit(solution)/shard_map/ppermute | solution.py:56
  11.9 11.7 %collective-permute-start.11 = (f32[192,768]{1,0:T(8,128)S(1)}, f32[192,768]{1,0:T(8,128)S(1)}, u32[]{:S(2)}, u32[]{:S(2)}) collective-permute-start(f32[192,768]{1,0:T(8,128)S(1)} %get-tuple-element.28), channel_id=1, source_target_pairs={{0,16},{1,65},{2,18},{3,67},{4,20},{5,69},{6,22},{7,71},{8,24},{9,... | collective-permute-start | bytes 1769480 | tf_op jit(solution)/shard_map/ppermute | solution.py:56
  12.0 11.6 %collective-permute-start.12 = (f32[64,768]{1,0:T(8,128)S(1)}, f32[64,768]{1,0:T(8,128)S(1)}, u32[]{:S(2)}, u32[]{:S(2)}) collective-permute-start(f32[64,768]{1,0:T(8,128)S(1)} %get-tuple-element.29), channel_id=1, source_target_pairs={{0,32},{1,129},{2,34},{3,131},{4,36},{5,133},{6,38},{7,135},{8,40}... | collective-permute-start | bytes 589832 | tf_op jit(solution)/shard_map/ppermute | solution.py:56
  14.0 9.7 %collective-permute-start.13 = (f32[64,768]{1,0:T(8,128)S(1)}, f32[64,768]{1,0:T(8,128)S(1)}, u32[]{:S(2)}, u32[]{:S(2)}) collective-permute-start(f32[64,768]{1,0:T(8,128)S(1)} %get-tuple-element.30), channel_id=1, source_target_pairs={{0,48},{1,193},{2,50},{3,195},{4,52},{5,197},{6,54},{7,199},{8,56}... | collective-permute-start | bytes 589832 | tf_op jit(solution)/shard_map/ppermute | solution.py:56
  24.5 17.0 %collective-permute-start.14 = (f32[48,768]{1,0:T(8,128)}, f32[48,768]{1,0:T(8,128)}, u32[]{:S(2)}, u32[]{:S(2)}) collective-permute-start(f32[48,768]{1,0:T(8,128)} %get-tuple-element.32), channel_id=1, source_target_pairs={{0,14},{1,17},{2,4},{3,19},{4,2},{5,21},{6,8},{7,23},{8,6},{9,25},... | collective-permute-start | bytes 442376 | tf_op jit(solution)/shard_map/ppermute | solution.py:56
  25.5 16.0 %collective-permute-start.15 = (f32[48,768]{1,0:T(8,128)}, f32[48,768]{1,0:T(8,128)}, u32[]{:S(2)}, u32[]{:S(2)}) collective-permute-start(f32[48,768]{1,0:T(8,128)} %get-tuple-element.33), channel_id=1, source_target_pairs={{0,14},{1,33},{2,4},{3,35},{4,2},{5,37},{6,8},{7,39},{8,6},{9,41},... | collective-permute-start | bytes 442376 | tf_op jit(solution)/shard_map/ppermute | solution.py:56
  28.4 13.1 %collective-permute-start.16 = (f32[48,768]{1,0:T(8,128)}, f32[48,768]{1,0:T(8,128)}, u32[]{:S(2)}, u32[]{:S(2)}) collective-permute-start(f32[48,768]{1,0:T(8,128)} %get-tuple-element.34), channel_id=1, source_target_pairs={{1,49},{3,51},{5,53},{7,55},{9,57},{11,59},{13,61},{15,63},{17,33}... | collective-permute-start | bytes 442376 | tf_op jit(solution)/shard_map/ppermute | solution.py:56
  34.2 77.9 %slice-start = ((s8[4718592]{0:T(1024)(128)(4,1)}), s8[4194304]{0:T(1024)(128)(4,1)S(1)}, s32[]{:S(2)}) async-start(s8[4718592]{0:T(1024)(128)(4,1)} %bitcast.9), calls=%async_computation | async-start | bytes 8388608
  35.9 11.0 %collective-permute-start.1 = (f32[128,768]{1,0:T(8,128)S(1)}, f32[128,768]{1,0:T(8,128)S(1)}, u32[]{:S(2)}, u32[]{:S(2)}) collective-permute-start(f32[128,768]{1,0:T(8,128)S(1)} %get-tuple-element.24), channel_id=1, source_target_pairs={{0,2},{1,15},{2,0},{3,5},{4,6},{5,3},{6,4},{7,9},{8,10},{9,7},{10,... | collective-permute-start | bytes 1179656 | tf_op jit(solution)/shard_map/ppermute | solution.py:56
  42.7 8.1 %collective-permute-start.17 = (f32[48,768]{1,0:T(8,128)S(1)}, f32[48,768]{1,0:T(8,128)S(1)}, u32[]{:S(2)}, u32[]{:S(2)}) collective-permute-start(f32[48,768]{1,0:T(8,128)S(1)} %add_select_fusion.3), channel_id=1, source_target_pairs={{0,12},{1,3},{2,6},{3,1},{4,8},{5,7},{6,2},{7,5},{8,4},{9,11},{10,... | collective-permute-start | bytes 442376 | tf_op jit(solution)/shard_map/ppermute | solution.py:56
  42.8 23.9 %collective-permute-start.6 = (f32[256,768]{1,0:T(8,128)S(1)}, f32[256,768]{1,0:T(8,128)S(1)}, u32[]{:S(2)}, u32[]{:S(2)}) collective-permute-start(f32[256,768]{1,0:T(8,128)S(1)} %get-tuple-element.25), channel_id=1, source_target_pairs={{0,2},{2,0},{4,6},{6,4},{8,10},{10,8},{12,14},{14,12},{16,18},{18,... | collective-permute-start | bytes 2359304 | tf_op jit(solution)/shard_map/ppermute | solution.py:56
  46.9 14.1 %collective-permute-start.2 = (f32[64,768]{1,0:T(8,128)S(1)}, f32[64,768]{1,0:T(8,128)S(1)}, u32[]{:S(2)}, u32[]{:S(2)}) collective-permute-start(f32[64,768]{1,0:T(8,128)S(1)} %slice.15), channel_id=1, source_target_pairs={{0,4},{1,13},{2,6},{3,7},{4,0},{5,9},{6,2},{7,3},{8,12},{9,5},{10,... | collective-permute-start | bytes 589832 | tf_op jit(solution)/shard_map/ppermute | solution.py:56
  51.9 13.2 %collective-permute-start.18 = (f32[48,768]{1,0:T(8,128)S(1)}, f32[48,768]{1,0:T(8,128)S(1)}, u32[]{:S(2)}, u32[]{:S(2)}) collective-permute-start(f32[48,768]{1,0:T(8,128)S(1)} %fusion), channel_id=1, source_target_pairs={{0,8},{1,5},{2,10},{3,7},{4,12},{5,1},{6,14},{7,3},{8,0},{9,13},{1... | collective-permute-start | bytes 442376 | tf_op jit(solution)/shard_map/ppermute | solution.py:56
  61.1 51.0 %slice-start.1 = ((s8[4718592]{0:T(1024)(128)(4,1)}), s8[524288]{0:T(1024)(128)(4,1)S(1)}, s32[]{:S(2)}) async-start(s8[4718592]{0:T(1024)(128)(4,1)} %bitcast.9), calls=%async_computation.1 | async-start | bytes 1048576
  61.1 21.6 %collective-permute-start.3 = (f32[64,768]{1,0:T(8,128)S(1)}, f32[64,768]{1,0:T(8,128)S(1)}, u32[]{:S(2)}, u32[]{:S(2)}) collective-permute-start(f32[64,768]{1,0:T(8,128)S(1)} %add_select_fusion), channel_id=1, source_target_pairs={{0,4},{1,9},{2,6},{3,11},{4,0},{5,13},{6,2},{7,15},{8,12},{9,1},{1... | collective-permute-start | bytes 589832 | tf_op jit(solution)/shard_map/ppermute | solution.py:56
  65.1 19.5 %collective-permute-start.19 = (f32[48,768]{1,0:T(8,128)S(1)}, f32[48,768]{1,0:T(8,128)S(1)}, u32[]{:S(2)}, u32[]{:S(2)}) collective-permute-start(f32[48,768]{1,0:T(8,128)S(1)} %add.46), channel_id=1, source_target_pairs={{0,12},{1,9},{2,6},{3,11},{4,8},{5,13},{6,2},{7,15},{8,4},{9,1},{1... | collective-permute-start | bytes 442376 | tf_op jit(solution)/shard_map/ppermute | solution.py:56
  66.8 49.8 %collective-permute-start.9 = (f32[256,768]{1,0:T(8,128)S(1)}, f32[256,768]{1,0:T(8,128)S(1)}, u32[]{:S(2)}, u32[]{:S(2)}) collective-permute-start(f32[256,768]{1,0:T(8,128)S(1)} %add.40.refs_2_), channel_id=1, source_target_pairs={{0,1},{1,0},{2,3},{3,2},{4,5},{5,4},{6,7},{7,6},{8,9},{9,8},{10,11... | collective-permute-start | bytes 2359304 | tf_op jit(solution)/shard_map/ppermute | solution.py:56
  82.7 8.5 %collective-permute-start.4 = (f32[64,768]{1,0:T(8,128)S(1)}, f32[64,768]{1,0:T(8,128)S(1)}, u32[]{:S(2)}, u32[]{:S(2)}) collective-permute-start(f32[64,768]{1,0:T(8,128)S(1)} %add.38), channel_id=1, source_target_pairs={{1,13},{3,7},{5,9},{7,3},{9,5},{11,15},{13,1},{15,11},{17,29},{19,... | collective-permute-start | bytes 589832 | tf_op jit(solution)/shard_map/ppermute | solution.py:56
  84.7 9.9 %collective-permute-start.22 = (f32[48,768]{1,0:T(8,128)S(1)}, f32[48,768]{1,0:T(8,128)S(1)}, u32[]{:S(2)}, u32[]{:S(2)}) collective-permute-start(f32[48,768]{1,0:T(8,128)S(1)} %get-tuple-element.36), channel_id=1, source_target_pairs={{1,49},{3,51},{5,53},{7,55},{9,57},{11,59},{13,61},{15,63},{17,33}... | collective-permute-start | bytes 442376 | tf_op jit(solution)/shard_map/ppermute | solution.py:56
  91.3 4.4 %collective-permute-start.20 = (f32[48,768]{1,0:T(8,128)S(1)}, f32[48,768]{1,0:T(8,128)S(1)}, u32[]{:S(2)}, u32[]{:S(2)}) collective-permute-start(f32[48,768]{1,0:T(8,128)S(1)} %get-tuple-element.36), channel_id=1, source_target_pairs={{0,14},{1,17},{2,4},{3,19},{4,2},{5,21},{6,8},{7,23},{8,6},{9,25},... | collective-permute-start | bytes 442376 | tf_op jit(solution)/shard_map/ppermute | solution.py:56
  91.4 7.3 %collective-permute-start.21 = (f32[48,768]{1,0:T(8,128)S(1)}, f32[48,768]{1,0:T(8,128)S(1)}, u32[]{:S(2)}, u32[]{:S(2)}) collective-permute-start(f32[48,768]{1,0:T(8,128)S(1)} %get-tuple-element.35), channel_id=1, source_target_pairs={{0,14},{1,33},{2,4},{3,35},{4,2},{5,37},{6,8},{7,39},{8,6},{9,41},... | collective-permute-start | bytes 442376 | tf_op jit(solution)/shard_map/ppermute | solution.py:56
  98.8 9.3 %collective-permute-start.23 = (f32[192,768]{1,0:T(8,128)S(1)}, f32[192,768]{1,0:T(8,128)S(1)}, u32[]{:S(2)}, u32[]{:S(2)}) collective-permute-start(f32[192,768]{1,0:T(8,128)S(1)} %bitcast.11), channel_id=1, source_target_pairs={{0,16},{1,65},{2,18},{3,67},{4,20},{5,69},{6,22},{7,71},{8,24},{9,... | collective-permute-start | bytes 1769480 | tf_op jit(solution)/shard_map/ppermute | solution.py:56
  99.3 8.2 %collective-permute-start.5 = (f32[128,768]{1,0:T(8,128)S(1)}, f32[128,768]{1,0:T(8,128)S(1)}, u32[]{:S(2)}, u32[]{:S(2)}) collective-permute-start(f32[128,768]{1,0:T(8,128)S(1)} %pad_maximum_fusion.1.refs_0_), channel_id=1, source_target_pairs={{0,2},{1,15},{2,0},{3,5},{4,6},{5,3},{6,4},{7,9},{8,10},{9,7},{10,... | collective-permute-start | bytes 1179656 | tf_op jit(solution)/shard_map/ppermute | solution.py:56
  99.4 8.1 %collective-permute-start.7 = (f32[128,768]{1,0:T(8,128)S(1)}, f32[128,768]{1,0:T(8,128)S(1)}, u32[]{:S(2)}, u32[]{:S(2)}) collective-permute-start(f32[128,768]{1,0:T(8,128)S(1)} %pad_maximum_fusion.1.refs_0_), channel_id=1, source_target_pairs={{0,1},{1,0},{2,3},{3,2},{4,5},{5,4},{6,7},{7,6},{8,9},{9,8},{10,11... | collective-permute-start | bytes 1179656 | tf_op jit(solution)/shard_map/ppermute | solution.py:56
  99.5 10.6 %collective-permute-start.24 = (f32[64,768]{1,0:T(8,128)S(1)}, f32[64,768]{1,0:T(8,128)S(1)}, u32[]{:S(2)}, u32[]{:S(2)}) collective-permute-start(f32[64,768]{1,0:T(8,128)S(1)} %bitcast.16), channel_id=1, source_target_pairs={{0,32},{1,129},{2,34},{3,131},{4,36},{5,133},{6,38},{7,135},{8,40}... | collective-permute-start | bytes 589832 | tf_op jit(solution)/shard_map/ppermute | solution.py:56
  107.5 9.1 %collective-permute-start.8 = (f32[128,768]{1,0:T(8,128)S(1)}, f32[128,768]{1,0:T(8,128)S(1)}, u32[]{:S(2)}, u32[]{:S(2)}) collective-permute-start(f32[128,768]{1,0:T(8,128)S(1)} %collective-permute-done.5.refs_1_), channel_id=1, source_target_pairs={{0,1},{1,0},{2,3},{3,2},{4,5},{5,4},{6,7},{7,6},{8,9},{9,8},{10,11... | collective-permute-start | bytes 1179656 | tf_op jit(solution)/shard_map/ppermute | solution.py:56
  107.5 20.3 %collective-permute-start.26 = (f32[192,768]{1,0:T(8,128)S(1)}, f32[192,768]{1,0:T(8,128)S(1)}, u32[]{:S(2)}, u32[]{:S(2)}) collective-permute-start(f32[192,768]{1,0:T(8,128)S(1)} %bitcast.12), channel_id=1, source_target_pairs={{0,1},{1,0},{2,3},{3,2},{4,5},{5,4},{6,7},{7,6},{8,9},{9,8},{10,11... | collective-permute-start | bytes 1769480 | tf_op jit(solution)/shard_map/ppermute | solution.py:56
  108.0 19.8 %collective-permute-start.27 = (f32[192,768]{1,0:T(8,128)S(1)}, f32[192,768]{1,0:T(8,128)S(1)}, u32[]{:S(2)}, u32[]{:S(2)}) collective-permute-start(f32[192,768]{1,0:T(8,128)S(1)} %collective-permute-done.23.refs_1_), channel_id=1, source_target_pairs={{0,1},{1,0},{2,3},{3,2},{4,5},{5,4},{6,7},{7,6},{8,9},{9,8},{10,11... | collective-permute-start | bytes 1769480 | tf_op jit(solution)/shard_map/ppermute | solution.py:56
  110.1 6.0 %collective-permute-start.25 = (f32[64,768]{1,0:T(8,128)S(1)}, f32[64,768]{1,0:T(8,128)S(1)}, u32[]{:S(2)}, u32[]{:S(2)}) collective-permute-start(f32[64,768]{1,0:T(8,128)S(1)} %bitcast.17), channel_id=1, source_target_pairs={{0,48},{1,193},{2,50},{3,195},{4,52},{5,197},{6,54},{7,199},{8,56}... | collective-permute-start | bytes 589832 | tf_op jit(solution)/shard_map/ppermute | solution.py:56
  116.1 11.6 %collective-permute-start.28 = (f32[64,768]{1,0:T(8,128)S(1)}, f32[64,768]{1,0:T(8,128)S(1)}, u32[]{:S(2)}, u32[]{:S(2)}) collective-permute-start(f32[64,768]{1,0:T(8,128)S(1)} %collective-permute-done.24.refs_2_), channel_id=1, source_target_pairs={{0,1},{1,0},{2,3},{3,2},{4,5},{5,4},{6,7},{7,6},{8,9},{9,8},{10,11... | collective-permute-start | bytes 589832 | tf_op jit(solution)/shard_map/ppermute | solution.py:56
  116.5 11.2 %collective-permute-start.29 = (f32[64,768]{1,0:T(8,128)S(1)}, f32[64,768]{1,0:T(8,128)S(1)}, u32[]{:S(2)}, u32[]{:S(2)}) collective-permute-start(f32[64,768]{1,0:T(8,128)S(1)} %collective-permute-done.25.refs_3_), channel_id=1, source_target_pairs={{0,1},{1,0},{2,3},{3,2},{4,5},{5,4},{6,7},{7,6},{8,9},{9,8},{10,11... | collective-permute-start | bytes 589832 | tf_op jit(solution)/shard_map/ppermute | solution.py:56
  (6 other events, 14.0 us)

commit v2 on v1

--- a/solution.py
+++ b/solution.py
@@ -185,64 +185,36 @@
     )(me, high, low, depth, basis)
 
 
-def leaf_kernel(high, low, depth, basis, out):
-    own = masked(basis[0], depth, 0)
-    out[...] = dot3(own, split(dot3(own, (high[...], low[...]), 0)), 1)
-
-
-def leaf(high, low, depth, basis):
-    return pl.pallas_call(
-        leaf_kernel,
-        out_shape=jax.ShapeDtypeStruct((V, R), jnp.float32),
-        in_specs=[VMEM, VMEM, VMEM, VMEM],
-        out_specs=VMEM,
-        compiler_params=pltpu.CompilerParams(vmem_limit_bytes=12 << 20),
-        cost_estimate=pl.CostEstimate(flops=12 * R * S * V, bytes_accessed=4 * V * R, transcendentals=0),
-        name="leaf",
-    )(high, low, depth, basis)
-
-
-def image_kernel(work, me, depth, before, basis_hbm, *refs):
-    pieces, (out, basis, high, low, sems) = refs[:-5], refs[-5:]
-    sides = [slots(me[0], (me[0] & 1) ^ other) for _, other, _ in work]
-    copies = []
-    for number, (slot, _, _) in enumerate(work):
-        copy = pltpu.make_async_copy(basis_hbm.at[sides[number][0][slot]], basis.at[number], sems.at[number])
-        copy.start()
-        copies.append(copy)
-    for number, (slot, _, plan) in enumerate(work):
-        mask = sides[number][1][slot]
+def image_kernel(work, fresh, me, depth, basis, *refs):
+    given, pieces, (out, high, low) = refs[: 2 if fresh else 1], refs[2 if fresh else 1 : -3], refs[-3:]
+    if fresh:
+        own = masked(basis[0], depth, 0)
+        out[...] = dot3(own, split(dot3(own, (given[0][...], given[1][...]), 0)), 1)
+    for number, (slot, other, plan) in enumerate(work):
+        levels, masks = slots(me[0], (me[0] & 1) ^ other)
         for unit, (piece, start) in enumerate(plan):
-            row = pl.multiple_of(UNIT * (unit ^ mask), UNIT)
+            row = pl.multiple_of(UNIT * (unit ^ masks[slot]), UNIT)
             part_high, part_low = split(pieces[piece][start : start + UNIT, :])
             high[number, pl.ds(row, UNIT), :] = part_high
             low[number, pl.ds(row, UNIT), :] = part_low
-    for copy in copies:
-        copy.wait()
-    for number, (slot, _, _) in enumerate(work):
-        own = masked(basis.at[number][...], depth, sides[number][0][slot])
+        own = masked(basis[levels[slot]], depth, levels[slot])
         image = dot3(own, (high[number], low[number]), 1)
-        out[...] = (before[...] if number == 0 else out[...]) + image
-
-
-def images(work, me, depth, before, basis, pieces):
+        out[...] = (out[...] if fresh or number else given[0][...]) + image
+
+
+def images(work, fresh, limit, me, depth, basis, given, pieces):
     count = len(work)
     return pl.pallas_call(
-        functools.partial(image_kernel, work),
+        functools.partial(image_kernel, work, fresh),
         out_shape=jax.ShapeDtypeStruct((V, R), jnp.float32),
-        in_specs=[SMEM, VMEM, VMEM, HBM] + [VMEM] * len(pieces),
+        in_specs=[SMEM] + [VMEM] * (2 + len(given) + len(pieces)),
         out_specs=VMEM,
-        scratch_shapes=[
-            pltpu.VMEM((count, V, S), jnp.float32),
-            pltpu.VMEM((count, S, R), jnp.bfloat16),
-            pltpu.VMEM((count, S, R), jnp.bfloat16),
-            pltpu.SemaphoreType.DMA((count,)),
-        ],
-        compiler_params=pltpu.CompilerParams(vmem_limit_bytes=50 << 20),
+        scratch_shapes=[pltpu.VMEM((count, S, R), jnp.bfloat16), pltpu.VMEM((count, S, R), jnp.bfloat16)],
+        compiler_params=pltpu.CompilerParams(vmem_limit_bytes=limit << 20),
         cost_estimate=pl.CostEstimate(
-            flops=count * 6 * R * S * V, bytes_accessed=count * 4 * S * (R + V), transcendentals=0
+            flops=(count + 2 * fresh) * 6 * R * S * V, bytes_accessed=count * 4 * S * (R + V), transcendentals=0
         ),
-    )(me, depth, before, basis, *pieces)
+    )(me, depth, basis, *given, *pieces)
 
 
 def plan_ab(slot):
@@ -268,9 +240,9 @@
     return pl.pallas_call(
         kernel,
         out_shape=tuple(jax.ShapeDtypeStruct((height, R), jnp.float32) for height in rows),
-        in_specs=[VMEM] * len(arrays),
+        in_specs=[SMEM if array.ndim == 1 else VMEM for array in arrays],
         out_specs=(VMEM,) * len(rows),
-        compiler_params=pltpu.CompilerParams(vmem_limit_bytes=8 << 20),
+        compiler_params=pltpu.CompilerParams(vmem_limit_bytes=4 << 20),
     )(*arrays)
 
 
@@ -290,9 +262,76 @@
         out[UNIT:, :] = base[at + UNIT : at + 48, :] + r1[at + UNIT : at + 48, :]
 
 
+def by_core(me, zero, one):
+    @pl.when((me[0] & 1) == 0)
+    def _():
+        zero()
+
+    @pl.when((me[0] & 1) == 1)
+    def _():
+        one()
+
+
+def settle_kernel(me, u0, u3, t1, t2, t3, total, passed):
+    def zero():
+        total[...] = u0[...] + t1[...]
+        passed[...] = u3[...] + t2[...]
+
+    def one():
+        total[...] = (u0[...] + t1[...]) + (t2[...] + t3[...])
+        passed[...] = total[...]
+
+    by_core(me, zero, one)
+
+
+def finish_kernel(me, total, other, out, passed):
+    def zero():
+        out[...] = total[...]
+        passed[...] = other[...]
+
+    def one():
+        out[...] = total[...] + other[...]
+        passed[...] = out[...]
+
+    by_core(me, zero, one)
+
+
+def stack_kernel(me, total, g1, g2, g3, other, done, top):
+    for quarter, part in enumerate((total, g1, g2)):
+        done[quarter * 48 : (quarter + 1) * 48, :] = part[...]
+        top[quarter * UNIT : (quarter + 1) * UNIT, :] = part[:UNIT, :]
+
+    def last(part):
+        done[144:, :] = part[...]
+        top[48:, :] = part[:UNIT, :]
+
+    by_core(me, lambda: last(other), lambda: last(g3))
+
+
+def half_kernel(me, c, m2, out):
+    def zero():
+        out[...] = c[...]
+
+    def one():
+        out[...] = c[...] + m2[...]
+
+    by_core(me, zero, one)
+
+
+def whole_kernel(me, c_low, c_high, m2, m4, out):
+    out[:64, :] = c_low[...]
+
+    def zero():
+        out[64:, :] = c_high[...] + m2[...]
+
+    def one():
+        out[64:, :] = m4[...]
+
+    by_core(me, zero, one)
+
+
 def steps(basis, rhs, vertex_tier_depth):
     index_here = lax.axis_index("leaf")
-    first = (index_here & 1) == 0
     me = index_here.reshape(1)
 
     send_ab, high, low, depth = first_partials(me, vertex_tier_depth.reshape(1, V), rhs, basis)
@@ -310,46 +349,41 @@
     keep_cd = partials([(2, 0), (3, 0)], me, high, low, depth, basis)
     near, mid = pairs(along_z(1), shifted_z(1)), pairs(along_z(2), shifted_z(2))
     c_low, c_high, d = local(cut_kernel, (128, 128, 256), keep_cd, got_cd)
-    c = c_low + send(c_high, near)
+    c_low, c_high = local(cut_kernel, (64, 64), c_low, send(c_high, near))
     d = d + send(d, pairs(along_z(1), None))
 
-    both = local(join_kernel, (48,) * 4, base, r1, r2, r3)
-    t1 = send(both[1], pairs(shifted_z(1), along_y(1)))
-    t2 = send(both[2], pairs(shifted_z(1), along_y(2)))
-    t3 = send(both[3], pairs(None, along_y(3)))
-    total = both[0] + t1
-    total, passed = jnp.where(first, total, total + t2 + t3), both[3] + t2
-    total_t = total + send(jnp.where(first, passed, total), pairs(shifted_z(2), along_z(1)))
-    total = total_t + send(total_t, pairs(along_z(4), along_z(2)))
+    u0, u1, u2, u3 = local(join_kernel, (48,) * 4, base, r1, r2, r3)
+    t1 = send(u1, pairs(shifted_z(1), along_y(1)))
+    t2 = send(u2, pairs(shifted_z(1), along_y(2)))
+    t3 = send(u3, pairs(None, along_y(3)))
+    total, passed = local(settle_kernel, (48, 48), me, u0, u3, t1, t2, t3)
+    total = total + send(passed, pairs(shifted_z(2), along_z(1)))
+    total = total + send(total, pairs(along_z(4), along_z(2)))
     other = send(total, pairs(shifted_z(2), along_z(4)))
-    total = jnp.where(first, total, total + other)
+    total, passed = local(finish_kernel, (48, 48), me, total, other)
     g1 = send(total, pairs(shifted_z(1), along_y(1)))
-    g2 = send(jnp.where(first, other, total), pairs(shifted_z(1), along_y(2)))
+    g2 = send(passed, pairs(shifted_z(1), along_y(2)))
     g3 = send(total, pairs(None, along_y(3)))
-    done = jnp.stack([total, g1, g2, jnp.where(first, other, g3)])
-    top = done[:, :UNIT].reshape(64, R)
-    done = done.reshape(192, R)
+    done, top = local(stack_kernel, (192, 64), me, total, g1, g2, g3, other)
     q1, q2, q3 = send(done, step[1]), send(top, step[2]), send(top, step[3])
     ab_pieces = (done, q1, q2, q3)
 
-    m2 = send(c[64:], mid)
-    c_low = jnp.where(first, c[:64], c[:64] + m2)
-    m3 = send(c_low, pairs(along_z(2), along_z(4)))
-    c_low = c_low + m3
+    m2 = send(c_high, mid)
+    (c_low,) = local(half_kernel, (64,), me, c_low, m2)
+    c_low = c_low + send(c_low, pairs(along_z(2), along_z(4)))
     m4 = send(c_low, pairs(None, shifted_z(2)))
-    c_half = jnp.concatenate([c_low, jnp.where(first, c[64:] + m2, m4)])
+    (c_half,) = local(whole_kernel, (128,), me, c_low, c_high, m2, m4)
     cd_pieces = (c_half, send(c_half, near), d)
 
     their_cd = tuple(send(piece, SWAP) for piece in cd_pieces)
     their_ab = tuple(send(piece, SWAP) for piece in ab_pieces)
 
-    result = leaf(high, low, depth, basis)
     result = images(
         [(2, 0, PLAN_C), (3, 0, PLAN_D), (2, 1, shift_pieces(PLAN_C, 3)), (3, 1, shift_pieces(PLAN_D, 3))],
-        me, depth, result, basis, cd_pieces + their_cd,
+        True, 16, me, depth, basis, (high, low), cd_pieces + their_cd,
     )
-    result = images([(0, 0, plan_ab(0)), (1, 0, plan_ab(1))], me, depth, result, basis, ab_pieces)
-    return images([(0, 1, plan_ab(0)), (1, 1, plan_ab(1))], me, depth, result, basis, their_ab)
+    result = images([(0, 0, plan_ab(0)), (1, 0, plan_ab(1))], False, 12, me, depth, basis, (result,), ab_pieces)
+    return images([(0, 1, plan_ab(0)), (1, 1, plan_ab(1))], False, 12, me, depth, basis, (result,), their_ab)
 
 
 def solution(mesh):

time: 134 us -> 107 us (0.80)
  Pallas kernels: 28.7 us -> 18.6 us
  starting transfers between devices: 60.3 us -> 52.5 us
  local copies, waits for them, and re-layouts: 6.07 us -> 0.68 us
  other arithmetic: 2.62 us -> 0.16 us
    pallas_call x4 -> x3, Pallas kernels: 16.9 us -> 8.82 us  [images(): pl.pallas_call(functools.partial(image_kernel, work, fresh), out_shape=ja...]
    ppermute x30, starting transfers between devices: 60.3 us -> 52.5 us  [send(): return lax.ppermute(array, 'leaf', perm)]
    unnamed x16 -> x4, local copies, waits for them, and re-layouts: 6.04 us -> 0.68 us
    pallas_call x3 -> x9, Pallas kernels: 2.74 us -> 0.64 us  [local(): pl.pallas_call(kernel, out_shape=tuple((jax.ShapeDtypeStruct((height, R),...]
  transfers between devices with their start and end apart: 30 -> 30, of which waited for: 9 -> 10; matrix products, arithmetic and copies ran while one was open for 2% -> 0% of each run, Pallas kernels for 15% -> 10%
where the time goes in v2:
time: 107 us; the launch traced here: 106 us
  starting transfers between devices  52.5 us (49%)
  waiting for transfers between devices  34.3 us (32%)
  Pallas kernels  18.6 us (17%)
    ppermute x30, starting transfers between devices, send(): return lax.ppermute(array, 'leaf', perm)  52.5 us
    ppermute x30, waiting for transfers between devices, send(): return lax.ppermute(array, 'leaf', perm)  34.3 us
    pallas_call x3, Pallas kernels, images(): pl.pallas_call(functools.partial(image_kernel, work, fresh), out_shape=ja...  8.82 us
    pallas_call x1, Pallas kernels, first_partials(): pl.pallas_call(first_kernel, out_shape=(jax.ShapeDtypeStruct((2 * S, R),...  4.65 us
    pallas_call x3, Pallas kernels, partials(): pl.pallas_call(functools.partial(partial_kernel, work), out_shape=jax.Sha...  4.49 us
  transfers between devices with their start and end apart: 30, of which 10 were waited for; matrix products, arithmetic and copies ran while one was open for 0% of the time, Pallas kernels for 10%

profile of v2, /device:TPU:1, one launch (start us, length us, event | category | flops | bytes accessed | tf_op | source)
XLA Modules:
  0.0 106.5 jit_solution(15447028719417024195)
XLA Ops:
  0.7 4.7 %send_ab.1 = (f32[512,768]{1,0:T(8,128)S(1)}, bf16[512,768]{1,0:T(8,128)(2,1)S(1)}, bf16[512,768]{1,0:T(8,128)(2,1)S(1)}, f32[512,128]{1,0:T(8,128)S(1)}) custom-call(s32[1]{0:T(128)} %bitcast.me, s32[1,512]{1,0:T(1,128)S(1)} %bitcast.2, f32[512,768]{1,0:T(8,128)} %rhs_hbm.1, f32[9,512,256]{2,1,0:T(8,128)} %basis.11), custom_call_target="tpu_custom_call" | custom-call | flops 1207959552 | bytes 2621440 | tf_op jit(solution)/shard_map/send_ab/pallas_call | solution.py:146
  5.3 3.3 %collective-permute-start.10 = (f32[512,768]{1,0:T(8,128)S(1)}, f32[512,768]{1,0:T(8,128)S(1)}, u32[]{:S(2)}, u32[]{:S(2)}) collective-permute-start(f32[512,768]{1,0:T(8,128)S(1)} %get-tuple-element.36), channel_id=1, source_target_pairs={{0,1},{1,0},{2,3},{3,2},{4,5},{5,4},{6,7},{7,6},{8,9},{9,8},{10,11... | collective-permute-start | bytes 4718600 | tf_op jit(solution)/shard_map/ppermute | solution.py:56
  8.6 1.5 %shard_map.38 = f32[512,768]{1,0:T(8,128)S(1)} custom-call(s32[1]{0:T(128)} %bitcast.me, bf16[512,768]{1,0:T(8,128)(2,1)S(1)} %get-tuple-element.29.high.refs_0_, bf16[512,768]{1,0:T(8,128)(2,1)S(1)} %get-tuple-element.30.low.refs_1_, f32[512,128]{1,0:T(8,128)S(1)} %get-tuple-element.28.depth, f32[9,512,256]{2,1,0:T(8,128)S(1)} %copy-done), custom_call_target="tpu_custom_call" | custom-call | flops 1207959552 | bytes 2621440 | tf_op jit(solution)/shard_map/pallas_call | solution.py:176
  10.3 1.5 %shard_map.44.kept = f32[512,768]{1,0:T(8,128)S(1)} custom-call(s32[1]{0:T(128)} %bitcast.me, bf16[512,768]{1,0:T(8,128)(2,1)S(1)} %get-tuple-element.29.high.refs_0_, bf16[512,768]{1,0:T(8,128)(2,1)S(1)} %get-tuple-element.30.low.refs_1_, f32[512,128]{1,0:T(8,128)S(1)} %get-tuple-element.28.depth, f32[9,512,256]{2,1,0:T(8,128)S(1)} %copy-done), custom_call_target="tpu_custom_call" | custom-call | flops 1207959552 | bytes 2621440 | tf_op jit(solution)/shard_map/pallas_call | solution.py:176
  12.0 1.5 %shard_map.37.kept = f32[512,768]{1,0:T(8,128)S(1)} custom-call(s32[1]{0:T(128)} %bitcast.me, bf16[512,768]{1,0:T(8,128)(2,1)S(1)} %get-tuple-element.29.high.refs_0_, bf16[512,768]{1,0:T(8,128)(2,1)S(1)} %get-tuple-element.30.low.refs_1_, f32[512,128]{1,0:T(8,128)S(1)} %get-tuple-element.28.depth, f32[9,512,256]{2,1,0:T(8,128)S(1)} %copy-done), custom_call_target="tpu_custom_call" | custom-call | flops 1207959552 | bytes 2621440 | tf_op jit(solution)/shard_map/pallas_call | solution.py:176
  14.1 4.8 %collective-permute-start.1 = (f32[128,768]{1,0:T(8,128)S(1)}, f32[128,768]{1,0:T(8,128)S(1)}, u32[]{:S(2)}, u32[]{:S(2)}) collective-permute-start(f32[128,768]{1,0:T(8,128)S(1)} %get-tuple-element.32), channel_id=1, source_target_pairs={{0,2},{1,15},{2,0},{3,5},{4,6},{5,3},{6,4},{7,9},{8,10},{9,7},{10,... | collective-permute-start | bytes 1179656 | tf_op jit(solution)/shard_map/ppermute | solution.py:56
  18.9 2.4 %collective-permute-start.12 = (f32[64,768]{1,0:T(8,128)S(1)}, f32[64,768]{1,0:T(8,128)S(1)}, u32[]{:S(2)}, u32[]{:S(2)}) collective-permute-start(f32[64,768]{1,0:T(8,128)S(1)} %get-tuple-element.39), channel_id=1, source_target_pairs={{0,32},{1,129},{2,34},{3,131},{4,36},{5,133},{6,38},{7,135},{8,40}... | collective-permute-start | bytes 589832 | tf_op jit(solution)/shard_map/ppermute | solution.py:56
  22.3 2.5 %collective-permute-done.12.r2 = f32[64,768]{1,0:T(8,128)S(1)} collective-permute-done((f32[64,768]{1,0:T(8,128)S(1)}, f32[64,768]{1,0:T(8,128)S(1)}, u32[]{:S(2)}, u32[]{:S(2)}) %collective-permute-start.12) | collective-permute-done | bytes 196640 | tf_op jit(solution)/shard_map/ppermute | solution.py:56
  24.9 2.2 %collective-permute-done.13.r3 = f32[64,768]{1,0:T(8,128)S(1)} collective-permute-done((f32[64,768]{1,0:T(8,128)S(1)}, f32[64,768]{1,0:T(8,128)S(1)}, u32[]{:S(2)}, u32[]{:S(2)}) %collective-permute-start.13) | collective-permute-done | bytes 196640 | tf_op jit(solution)/shard_map/ppermute | solution.py:56
  27.1 1.4 %collective-permute-start.14 = (f32[48,768]{1,0:T(8,128)S(1)}, f32[48,768]{1,0:T(8,128)S(1)}, u32[]{:S(2)}, u32[]{:S(2)}) collective-permute-start(f32[48,768]{1,0:T(8,128)S(1)} %get-tuple-element.43), channel_id=1, source_target_pairs={{0,14},{1,17},{2,4},{3,19},{4,2},{5,21},{6,8},{7,23},{8,6},{9,25},... | collective-permute-start | bytes 442376 | tf_op jit(solution)/shard_map/ppermute | solution.py:56
  28.5 2.6 %collective-permute-start.15 = (f32[48,768]{1,0:T(8,128)S(1)}, f32[48,768]{1,0:T(8,128)S(1)}, u32[]{:S(2)}, u32[]{:S(2)}) collective-permute-start(f32[48,768]{1,0:T(8,128)S(1)} %get-tuple-element.44), channel_id=1, source_target_pairs={{0,14},{1,33},{2,4},{3,35},{4,2},{5,37},{6,8},{7,39},{8,6},{9,41},... | collective-permute-start | bytes 442376 | tf_op jit(solution)/shard_map/ppermute | solution.py:56
  31.1 1.9 %collective-permute-start.16 = (f32[48,768]{1,0:T(8,128)S(1)}, f32[48,768]{1,0:T(8,128)S(1)}, u32[]{:S(2)}, u32[]{:S(2)}) collective-permute-start(f32[48,768]{1,0:T(8,128)S(1)} %get-tuple-element.42.u3), channel_id=1, source_target_pairs={{1,49},{3,51},{5,53},{7,55},{9,57},{11,59},{13,61},{15,63},{17,33}... | collective-permute-start | bytes 442376 | tf_op jit(solution)/shard_map/ppermute | solution.py:56
  33.1 3.6 %collective-permute-start.2 = (f32[64,768]{1,0:T(8,128)S(1)}, f32[64,768]{1,0:T(8,128)S(1)}, u32[]{:S(2)}, u32[]{:S(2)}) collective-permute-start(f32[64,768]{1,0:T(8,128)S(1)} %get-tuple-element.34.c_high), channel_id=1, source_target_pairs={{0,4},{1,13},{2,6},{3,7},{4,0},{5,9},{6,2},{7,3},{8,12},{9,5},{10,... | collective-permute-start | bytes 589832 | tf_op jit(solution)/shard_map/ppermute | solution.py:56
  36.7 1.8 %collective-permute-done.16.t3 = f32[48,768]{1,0:T(8,128)S(1)} collective-permute-done((f32[48,768]{1,0:T(8,128)S(1)}, f32[48,768]{1,0:T(8,128)S(1)}, u32[]{:S(2)}, u32[]{:S(2)}) %collective-permute-start.16) | collective-permute-done | bytes 147488 | tf_op jit(solution)/shard_map/ppermute | solution.py:56
  38.8 1.7 %collective-permute-done.2.m2 = f32[64,768]{1,0:T(8,128)S(1)} collective-permute-done((f32[64,768]{1,0:T(8,128)S(1)}, f32[64,768]{1,0:T(8,128)S(1)}, u32[]{:S(2)}, u32[]{:S(2)}) %collective-permute-start.2) | collective-permute-done | bytes 196640 | tf_op jit(solution)/shard_map/ppermute | solution.py:56
  40.6 8.1 %collective-permute-start.3 = (f32[64,768]{1,0:T(8,128)S(1)}, f32[64,768]{1,0:T(8,128)S(1)}, u32[]{:S(2)}, u32[]{:S(2)}) collective-permute-start(f32[64,768]{1,0:T(8,128)S(1)} %shard_map.41), channel_id=1, source_target_pairs={{0,4},{1,9},{2,6},{3,11},{4,0},{5,13},{6,2},{7,15},{8,12},{9,1},{1... | collective-permute-start | bytes 589832 | tf_op jit(solution)/shard_map/ppermute | solution.py:56
  48.8 13.4 %collective-permute-done.18 = f32[48,768]{1,0:T(8,128)S(1)} collective-permute-done((f32[48,768]{1,0:T(8,128)S(1)}, f32[48,768]{1,0:T(8,128)S(1)}, u32[]{:S(2)}, u32[]{:S(2)}) %collective-permute-start.18) | collective-permute-done | bytes 147488 | tf_op jit(solution)/shard_map/ppermute | solution.py:56
  62.2 3.6 %collective-permute-start.19 = (f32[48,768]{1,0:T(8,128)S(1)}, f32[48,768]{1,0:T(8,128)S(1)}, u32[]{:S(2)}, u32[]{:S(2)}) collective-permute-start(f32[48,768]{1,0:T(8,128)S(1)} %add.15.total), channel_id=1, source_target_pairs={{0,12},{1,9},{2,6},{3,11},{4,8},{5,13},{6,2},{7,15},{8,4},{9,1},{1... | collective-permute-start | bytes 442376 | tf_op jit(solution)/shard_map/ppermute | solution.py:56
  65.8 1.9 %collective-permute-start.4 = (f32[64,768]{1,0:T(8,128)S(1)}, f32[64,768]{1,0:T(8,128)S(1)}, u32[]{:S(2)}, u32[]{:S(2)}) collective-permute-start(f32[64,768]{1,0:T(8,128)S(1)} %add.12.c_low), channel_id=1, source_target_pairs={{1,13},{3,7},{5,9},{7,3},{9,5},{11,15},{13,1},{15,11},{17,29},{19,... | collective-permute-start | bytes 589832 | tf_op jit(solution)/shard_map/ppermute | solution.py:56
  67.7 2.8 %collective-permute-done.19.other = f32[48,768]{1,0:T(8,128)S(1)} collective-permute-done((f32[48,768]{1,0:T(8,128)S(1)}, f32[48,768]{1,0:T(8,128)S(1)}, u32[]{:S(2)}, u32[]{:S(2)}) %collective-permute-start.19) | collective-permute-done | bytes 147488 | tf_op jit(solution)/shard_map/ppermute | solution.py:56
  71.1 0.8 collective-permute-start.21
  71.9 4.6 %collective-permute-start.22 = (f32[48,768]{1,0:T(8,128)S(1)}, f32[48,768]{1,0:T(8,128)S(1)}, u32[]{:S(2)}, u32[]{:S(2)}) collective-permute-start(f32[48,768]{1,0:T(8,128)S(1)} %get-tuple-element.47.total), channel_id=1, source_target_pairs={{1,49},{3,51},{5,53},{7,55},{9,57},{11,59},{13,61},{15,63},{17,33}... | collective-permute-start | bytes 442376 | tf_op jit(solution)/shard_map/ppermute | solution.py:56
  76.5 1.4 %collective-permute-start.9 = (f32[256,768]{1,0:T(8,128)S(1)}, f32[256,768]{1,0:T(8,128)S(1)}, u32[]{:S(2)}, u32[]{:S(2)}) collective-permute-start(f32[256,768]{1,0:T(8,128)S(1)} %add.13.refs_4_), channel_id=1, source_target_pairs={{0,1},{1,0},{2,3},{3,2},{4,5},{5,4},{6,7},{7,6},{8,9},{9,8},{10,11... | collective-permute-start | bytes 2359304 | tf_op jit(solution)/shard_map/ppermute | solution.py:56
  78.0 3.0 %collective-permute-start.5 = (f32[128,768]{1,0:T(8,128)S(1)}, f32[128,768]{1,0:T(8,128)S(1)}, u32[]{:S(2)}, u32[]{:S(2)}) collective-permute-start(f32[128,768]{1,0:T(8,128)S(1)} %shard_map.42.refs_2_), channel_id=1, source_target_pairs={{0,2},{1,15},{2,0},{3,5},{4,6},{5,3},{6,4},{7,9},{8,10},{9,7},{10,... | collective-permute-start | bytes 1179656 | tf_op jit(solution)/shard_map/ppermute | solution.py:56
  81.1 0.9 collective-permute-start.23
  82.1 4.1 %collective-permute-done.5.refs_3_ = f32[128,768]{1,0:T(8,128)S(1)} collective-permute-done((f32[128,768]{1,0:T(8,128)S(1)}, f32[128,768]{1,0:T(8,128)S(1)}, u32[]{:S(2)}, u32[]{:S(2)}) %collective-permute-start.5) | collective-permute-done | bytes 393248 | tf_op jit(solution)/shard_map/ppermute | solution.py:56
  86.2 5.0 %collective-permute-start.24 = (f32[64,768]{1,0:T(8,128)S(1)}, f32[64,768]{1,0:T(8,128)S(1)}, u32[]{:S(2)}, u32[]{:S(2)}) collective-permute-start(f32[64,768]{1,0:T(8,128)S(1)} %get-tuple-element.50), channel_id=1, source_target_pairs={{0,32},{1,129},{2,34},{3,131},{4,36},{5,133},{6,38},{7,135},{8,40}... | collective-permute-start | bytes 589832 | tf_op jit(solution)/shard_map/ppermute | solution.py:56
  91.2 3.8 %collective-permute-done.24.refs_3_ = f32[64,768]{1,0:T(8,128)S(1)} collective-permute-done((f32[64,768]{1,0:T(8,128)S(1)}, f32[64,768]{1,0:T(8,128)S(1)}, u32[]{:S(2)}, u32[]{:S(2)}) %collective-permute-start.24) | collective-permute-done | bytes 196640 | tf_op jit(solution)/shard_map/ppermute | solution.py:56
  95.5 1.6 %collective-permute-done.25.refs_4_ = f32[64,768]{1,0:T(8,128)S(1)} collective-permute-done((f32[64,768]{1,0:T(8,128)S(1)}, f32[64,768]{1,0:T(8,128)S(1)}, u32[]{:S(2)}, u32[]{:S(2)}) %collective-permute-start.25) | collective-permute-done | bytes 196640 | tf_op jit(solution)/shard_map/ppermute | solution.py:56
  97.6 4.3 %shard_map.43.refs_0_ = f32[512,768]{1,0:T(8,128)S(1)} custom-call(s32[1]{0:T(128)} %bitcast.me, f32[512,128]{1,0:T(8,128)S(1)} %get-tuple-element.28.depth, f32[9,512,256]{2,1,0:T(8,128)S(1)} %copy-done, bf16[512,768]{1,0:T(8,128)(2,1)S(1)} %get-tuple-element.29.high.refs_0_, bf16[512,768]{1,0:T(8,128)(2,1)S(1)} %get-tuple-element.30.low.refs_1_, ...), custom_call_target="tpu_custom_call" | custom-call | flops 3623878656 | bytes 5242880 | tf_op jit(solution)/shard_map/pallas_call | solution.py:207
  101.9 1.7 %shard_map.50.refs_0_ = f32[512,768]{1,0:T(8,128)S(1)} custom-call(s32[1]{0:T(128)} %bitcast.me, f32[512,128]{1,0:T(8,128)S(1)} %get-tuple-element.28.depth, f32[9,512,256]{2,1,0:T(8,128)S(1)} %copy-done, f32[512,768]{1,0:T(8,128)S(1)} %shard_map.43.refs_0_, f32[192,768]{1,0:T(8,128)S(1)} %get-tuple-element.49.refs_1_, ...), custom_call_target="tpu_custom_call" | custom-call | flops 1207959552 | bytes 2621440 | tf_op jit(solution)/shard_map/pallas_call | solution.py:207
  103.6 2.8 %shard_map.51 = f32[512,768]{1,0:T(8,128)} custom-call(s32[1]{0:T(128)} %bitcast.me, f32[512,128]{1,0:T(8,128)S(1)} %get-tuple-element.28.depth, f32[9,512,256]{2,1,0:T(8,128)S(1)} %copy-done, f32[512,768]{1,0:T(8,128)S(1)} %shard_map.50.refs_0_, f32[192,768]{1,0:T(8,128)S(1)} %collective-permute-done.26.refs_1_, ...), custom_call_target="tpu_custom_call" | custom-call | flops 1207959552 | bytes 2621440 | tf_op jit(solution)/shard_map/pallas_call | solution.py:207
  (52 shorter events, 5.1 us)
Async XLA Ops:
  0.0 0.7 copy-start.1
  0.7 8.0 %copy-start = (f32[9,512,256]{2,1,0:T(8,128)S(1)}, f32[9,512,256]{2,1,0:T(8,128)}, u32[]{:S(2)}) copy-start(f32[9,512,256]{2,1,0:T(8,128)} %basis.11) | copy-start | bytes 14155780
  5.3 6.4 %collective-permute-start.10 = (f32[512,768]{1,0:T(8,128)S(1)}, f32[512,768]{1,0:T(8,128)S(1)}, u32[]{:S(2)}, u32[]{:S(2)}) collective-permute-start(f32[512,768]{1,0:T(8,128)S(1)} %get-tuple-element.36), channel_id=1, source_target_pairs={{0,1},{1,0},{2,3},{3,2},{4,5},{5,4},{6,7},{7,6},{8,9},{9,8},{10,11... | collective-permute-start | bytes 4718600 | tf_op jit(solution)/shard_map/ppermute | solution.py:56
  10.1 3.8 %collective-permute-start = (f32[512,768]{1,0:T(8,128)S(1)}, f32[512,768]{1,0:T(8,128)S(1)}, u32[]{:S(2)}, u32[]{:S(2)}) collective-permute-start(f32[512,768]{1,0:T(8,128)S(1)} %shard_map.38), channel_id=1, source_target_pairs={{0,1},{1,0},{2,3},{3,2},{4,5},{5,4},{6,7},{7,6},{8,9},{9,8},{10,11... | collective-permute-start | bytes 4718600 | tf_op jit(solution)/shard_map/ppermute | solution.py:56
  11.9 15.1 %collective-permute-start.11 = (f32[192,768]{1,0:T(8,128)S(1)}, f32[192,768]{1,0:T(8,128)S(1)}, u32[]{:S(2)}, u32[]{:S(2)}) collective-permute-start(f32[192,768]{1,0:T(8,128)S(1)} %get-tuple-element.38), channel_id=1, source_target_pairs={{0,16},{1,65},{2,18},{3,67},{4,20},{5,69},{6,22},{7,71},{8,24},{9,... | collective-permute-start | bytes 1769480 | tf_op jit(solution)/shard_map/ppermute | solution.py:56
  14.1 19.0 %collective-permute-start.1 = (f32[128,768]{1,0:T(8,128)S(1)}, f32[128,768]{1,0:T(8,128)S(1)}, u32[]{:S(2)}, u32[]{:S(2)}) collective-permute-start(f32[128,768]{1,0:T(8,128)S(1)} %get-tuple-element.32), channel_id=1, source_target_pairs={{0,2},{1,15},{2,0},{3,5},{4,6},{5,3},{6,4},{7,9},{8,10},{9,7},{10,... | collective-permute-start | bytes 1179656 | tf_op jit(solution)/shard_map/ppermute | solution.py:56
  18.9 6.0 %collective-permute-start.12 = (f32[64,768]{1,0:T(8,128)S(1)}, f32[64,768]{1,0:T(8,128)S(1)}, u32[]{:S(2)}, u32[]{:S(2)}) collective-permute-start(f32[64,768]{1,0:T(8,128)S(1)} %get-tuple-element.39), channel_id=1, source_target_pairs={{0,32},{1,129},{2,34},{3,131},{4,36},{5,133},{6,38},{7,135},{8,40}... | collective-permute-start | bytes 589832 | tf_op jit(solution)/shard_map/ppermute | solution.py:56
  21.3 5.7 %collective-permute-start.13 = (f32[64,768]{1,0:T(8,128)S(1)}, f32[64,768]{1,0:T(8,128)S(1)}, u32[]{:S(2)}, u32[]{:S(2)}) collective-permute-start(f32[64,768]{1,0:T(8,128)S(1)} %get-tuple-element.40), channel_id=1, source_target_pairs={{0,48},{1,193},{2,50},{3,195},{4,52},{5,197},{6,54},{7,199},{8,56}... | collective-permute-start | bytes 589832 | tf_op jit(solution)/shard_map/ppermute | solution.py:56
  21.6 54.8 %collective-permute-start.6 = (f32[256,768]{1,0:T(8,128)S(1)}, f32[256,768]{1,0:T(8,128)S(1)}, u32[]{:S(2)}, u32[]{:S(2)}) collective-permute-start(f32[256,768]{1,0:T(8,128)S(1)} %get-tuple-element.35), channel_id=1, source_target_pairs={{0,2},{2,0},{4,6},{6,4},{8,10},{10,8},{12,14},{14,12},{16,18},{18,... | collective-permute-start | bytes 2359304 | tf_op jit(solution)/shard_map/ppermute | solution.py:56
  27.1 9.6 %collective-permute-start.14 = (f32[48,768]{1,0:T(8,128)S(1)}, f32[48,768]{1,0:T(8,128)S(1)}, u32[]{:S(2)}, u32[]{:S(2)}) collective-permute-start(f32[48,768]{1,0:T(8,128)S(1)} %get-tuple-element.43), channel_id=1, source_target_pairs={{0,14},{1,17},{2,4},{3,19},{4,2},{5,21},{6,8},{7,23},{8,6},{9,25},... | collective-permute-start | bytes 442376 | tf_op jit(solution)/shard_map/ppermute | solution.py:56
  28.5 8.2 %collective-permute-start.15 = (f32[48,768]{1,0:T(8,128)S(1)}, f32[48,768]{1,0:T(8,128)S(1)}, u32[]{:S(2)}, u32[]{:S(2)}) collective-permute-start(f32[48,768]{1,0:T(8,128)S(1)} %get-tuple-element.44), channel_id=1, source_target_pairs={{0,14},{1,33},{2,4},{3,35},{4,2},{5,37},{6,8},{7,39},{8,6},{9,41},... | collective-permute-start | bytes 442376 | tf_op jit(solution)/shard_map/ppermute | solution.py:56
  31.1 7.4 %collective-permute-start.16 = (f32[48,768]{1,0:T(8,128)S(1)}, f32[48,768]{1,0:T(8,128)S(1)}, u32[]{:S(2)}, u32[]{:S(2)}) collective-permute-start(f32[48,768]{1,0:T(8,128)S(1)} %get-tuple-element.42.u3), channel_id=1, source_target_pairs={{1,49},{3,51},{5,53},{7,55},{9,57},{11,59},{13,61},{15,63},{17,33}... | collective-permute-start | bytes 442376 | tf_op jit(solution)/shard_map/ppermute | solution.py:56
  33.1 7.4 %collective-permute-start.2 = (f32[64,768]{1,0:T(8,128)S(1)}, f32[64,768]{1,0:T(8,128)S(1)}, u32[]{:S(2)}, u32[]{:S(2)}) collective-permute-start(f32[64,768]{1,0:T(8,128)S(1)} %get-tuple-element.34.c_high), channel_id=1, source_target_pairs={{0,4},{1,13},{2,6},{3,7},{4,0},{5,9},{6,2},{7,3},{8,12},{9,5},{10,... | collective-permute-start | bytes 589832 | tf_op jit(solution)/shard_map/ppermute | solution.py:56
  38.6 10.1 %collective-permute-start.17 = (f32[48,768]{1,0:T(8,128)S(1)}, f32[48,768]{1,0:T(8,128)S(1)}, u32[]{:S(2)}, u32[]{:S(2)}) collective-permute-start(f32[48,768]{1,0:T(8,128)S(1)} %get-tuple-element.46), channel_id=1, source_target_pairs={{0,12},{1,3},{2,6},{3,1},{4,8},{5,7},{6,2},{7,5},{8,4},{9,11},{10,... | collective-permute-start | bytes 442376 | tf_op jit(solution)/shard_map/ppermute | solution.py:56
  40.6 25.2 %collective-permute-start.3 = (f32[64,768]{1,0:T(8,128)S(1)}, f32[64,768]{1,0:T(8,128)S(1)}, u32[]{:S(2)}, u32[]{:S(2)}) collective-permute-start(f32[64,768]{1,0:T(8,128)S(1)} %shard_map.41), channel_id=1, source_target_pairs={{0,4},{1,9},{2,6},{3,11},{4,0},{5,13},{6,2},{7,15},{8,12},{9,1},{1... | collective-permute-start | bytes 589832 | tf_op jit(solution)/shard_map/ppermute | solution.py:56
  48.7 13.5 %collective-permute-start.18 = (f32[48,768]{1,0:T(8,128)S(1)}, f32[48,768]{1,0:T(8,128)S(1)}, u32[]{:S(2)}, u32[]{:S(2)}) collective-permute-start(f32[48,768]{1,0:T(8,128)S(1)} %add.14), channel_id=1, source_target_pairs={{0,8},{1,5},{2,10},{3,7},{4,12},{5,1},{6,14},{7,3},{8,0},{9,13},{1... | collective-permute-start | bytes 442376 | tf_op jit(solution)/shard_map/ppermute | solution.py:56
  62.2 8.4 %collective-permute-start.19 = (f32[48,768]{1,0:T(8,128)S(1)}, f32[48,768]{1,0:T(8,128)S(1)}, u32[]{:S(2)}, u32[]{:S(2)}) collective-permute-start(f32[48,768]{1,0:T(8,128)S(1)} %add.15.total), channel_id=1, source_target_pairs={{0,12},{1,9},{2,6},{3,11},{4,8},{5,13},{6,2},{7,15},{8,4},{9,1},{1... | collective-permute-start | bytes 442376 | tf_op jit(solution)/shard_map/ppermute | solution.py:56
  65.8 12.2 %collective-permute-start.4 = (f32[64,768]{1,0:T(8,128)S(1)}, f32[64,768]{1,0:T(8,128)S(1)}, u32[]{:S(2)}, u32[]{:S(2)}) collective-permute-start(f32[64,768]{1,0:T(8,128)S(1)} %add.12.c_low), channel_id=1, source_target_pairs={{1,13},{3,7},{5,9},{7,3},{9,5},{11,15},{13,1},{15,11},{17,29},{19,... | collective-permute-start | bytes 589832 | tf_op jit(solution)/shard_map/ppermute | solution.py:56
  70.6 10.4 %collective-permute-start.20 = (f32[48,768]{1,0:T(8,128)S(1)}, f32[48,768]{1,0:T(8,128)S(1)}, u32[]{:S(2)}, u32[]{:S(2)}) collective-permute-start(f32[48,768]{1,0:T(8,128)S(1)} %get-tuple-element.47.total), channel_id=1, source_target_pairs={{0,14},{1,17},{2,4},{3,19},{4,2},{5,21},{6,8},{7,23},{8,6},{9,25},... | collective-permute-start | bytes 442376 | tf_op jit(solution)/shard_map/ppermute | solution.py:56
  71.1 9.9 %collective-permute-start.21 = (f32[48,768]{1,0:T(8,128)S(1)}, f32[48,768]{1,0:T(8,128)S(1)}, u32[]{:S(2)}, u32[]{:S(2)}) collective-permute-start(f32[48,768]{1,0:T(8,128)S(1)} %get-tuple-element.48), channel_id=1, source_target_pairs={{0,14},{1,33},{2,4},{3,35},{4,2},{5,37},{6,8},{7,39},{8,6},{9,41},... | collective-permute-start | bytes 442376 | tf_op jit(solution)/shard_map/ppermute | solution.py:56
  71.9 9.1 %collective-permute-start.22 = (f32[48,768]{1,0:T(8,128)S(1)}, f32[48,768]{1,0:T(8,128)S(1)}, u32[]{:S(2)}, u32[]{:S(2)}) collective-permute-start(f32[48,768]{1,0:T(8,128)S(1)} %get-tuple-element.47.total), channel_id=1, source_target_pairs={{1,49},{3,51},{5,53},{7,55},{9,57},{11,59},{13,61},{15,63},{17,33}... | collective-permute-start | bytes 442376 | tf_op jit(solution)/shard_map/ppermute | solution.py:56
  76.5 20.5 %collective-permute-start.9 = (f32[256,768]{1,0:T(8,128)S(1)}, f32[256,768]{1,0:T(8,128)S(1)}, u32[]{:S(2)}, u32[]{:S(2)}) collective-permute-start(f32[256,768]{1,0:T(8,128)S(1)} %add.13.refs_4_), channel_id=1, source_target_pairs={{0,1},{1,0},{2,3},{3,2},{4,5},{5,4},{6,7},{7,6},{8,9},{9,8},{10,11... | collective-permute-start | bytes 2359304 | tf_op jit(solution)/shard_map/ppermute | solution.py:56
  78.0 8.1 %collective-permute-start.5 = (f32[128,768]{1,0:T(8,128)S(1)}, f32[128,768]{1,0:T(8,128)S(1)}, u32[]{:S(2)}, u32[]{:S(2)}) collective-permute-start(f32[128,768]{1,0:T(8,128)S(1)} %shard_map.42.refs_2_), channel_id=1, source_target_pairs={{0,2},{1,15},{2,0},{3,5},{4,6},{5,3},{6,4},{7,9},{8,10},{9,7},{10,... | collective-permute-start | bytes 1179656 | tf_op jit(solution)/shard_map/ppermute | solution.py:56
  81.1 13.9 %collective-permute-start.23 = (f32[192,768]{1,0:T(8,128)S(1)}, f32[192,768]{1,0:T(8,128)S(1)}, u32[]{:S(2)}, u32[]{:S(2)}) collective-permute-start(f32[192,768]{1,0:T(8,128)S(1)} %get-tuple-element.49.refs_1_), channel_id=1, source_target_pairs={{0,16},{1,65},{2,18},{3,67},{4,20},{5,69},{6,22},{7,71},{8,24},{9,... | collective-permute-start | bytes 1769480 | tf_op jit(solution)/shard_map/ppermute | solution.py:56
  82.0 9.1 %collective-permute-start.7 = (f32[128,768]{1,0:T(8,128)S(1)}, f32[128,768]{1,0:T(8,128)S(1)}, u32[]{:S(2)}, u32[]{:S(2)}) collective-permute-start(f32[128,768]{1,0:T(8,128)S(1)} %shard_map.42.refs_2_), channel_id=1, source_target_pairs={{0,1},{1,0},{2,3},{3,2},{4,5},{5,4},{6,7},{7,6},{8,9},{9,8},{10,11... | collective-permute-start | bytes 1179656 | tf_op jit(solution)/shard_map/ppermute | solution.py:56
  86.2 11.4 %collective-permute-start.8 = (f32[128,768]{1,0:T(8,128)S(1)}, f32[128,768]{1,0:T(8,128)S(1)}, u32[]{:S(2)}, u32[]{:S(2)}) collective-permute-start(f32[128,768]{1,0:T(8,128)S(1)} %collective-permute-done.5.refs_3_), channel_id=1, source_target_pairs={{0,1},{1,0},{2,3},{3,2},{4,5},{5,4},{6,7},{7,6},{8,9},{9,8},{10,11... | collective-permute-start | bytes 1179656 | tf_op jit(solution)/shard_map/ppermute | solution.py:56
  86.2 8.8 %collective-permute-start.24 = (f32[64,768]{1,0:T(8,128)S(1)}, f32[64,768]{1,0:T(8,128)S(1)}, u32[]{:S(2)}, u32[]{:S(2)}) collective-permute-start(f32[64,768]{1,0:T(8,128)S(1)} %get-tuple-element.50), channel_id=1, source_target_pairs={{0,32},{1,129},{2,34},{3,131},{4,36},{5,133},{6,38},{7,135},{8,40}... | collective-permute-start | bytes 589832 | tf_op jit(solution)/shard_map/ppermute | solution.py:56
  91.1 5.9 %collective-permute-start.25 = (f32[64,768]{1,0:T(8,128)S(1)}, f32[64,768]{1,0:T(8,128)S(1)}, u32[]{:S(2)}, u32[]{:S(2)}) collective-permute-start(f32[64,768]{1,0:T(8,128)S(1)} %get-tuple-element.50), channel_id=1, source_target_pairs={{0,48},{1,193},{2,50},{3,195},{4,52},{5,197},{6,54},{7,199},{8,56}... | collective-permute-start | bytes 589832 | tf_op jit(solution)/shard_map/ppermute | solution.py:56
  95.0 8.6 %collective-permute-start.26 = (f32[192,768]{1,0:T(8,128)S(1)}, f32[192,768]{1,0:T(8,128)S(1)}, u32[]{:S(2)}, u32[]{:S(2)}) collective-permute-start(f32[192,768]{1,0:T(8,128)S(1)} %get-tuple-element.49.refs_1_), channel_id=1, source_target_pairs={{0,1},{1,0},{2,3},{3,2},{4,5},{5,4},{6,7},{7,6},{8,9},{9,8},{10,11... | collective-permute-start | bytes 1769480 | tf_op jit(solution)/shard_map/ppermute | solution.py:56
  95.0 8.6 %collective-permute-start.27 = (f32[192,768]{1,0:T(8,128)S(1)}, f32[192,768]{1,0:T(8,128)S(1)}, u32[]{:S(2)}, u32[]{:S(2)}) collective-permute-start(f32[192,768]{1,0:T(8,128)S(1)} %collective-permute-done.23.refs_2_), channel_id=1, source_target_pairs={{0,1},{1,0},{2,3},{3,2},{4,5},{5,4},{6,7},{7,6},{8,9},{9,8},{10,11... | collective-permute-start | bytes 1769480 | tf_op jit(solution)/shard_map/ppermute | solution.py:56
  97.1 6.5 %collective-permute-start.28 = (f32[64,768]{1,0:T(8,128)S(1)}, f32[64,768]{1,0:T(8,128)S(1)}, u32[]{:S(2)}, u32[]{:S(2)}) collective-permute-start(f32[64,768]{1,0:T(8,128)S(1)} %collective-permute-done.24.refs_3_), channel_id=1, source_target_pairs={{0,1},{1,0},{2,3},{3,2},{4,5},{5,4},{6,7},{7,6},{8,9},{9,8},{10,11... | collective-permute-start | bytes 589832 | tf_op jit(solution)/shard_map/ppermute | solution.py:56
  97.1 6.5 %collective-permute-start.29 = (f32[64,768]{1,0:T(8,128)S(1)}, f32[64,768]{1,0:T(8,128)S(1)}, u32[]{:S(2)}, u32[]{:S(2)}) collective-permute-start(f32[64,768]{1,0:T(8,128)S(1)} %collective-permute-done.25.refs_4_), channel_id=1, source_target_pairs={{0,1},{1,0},{2,3},{3,2},{4,5},{5,4},{6,7},{7,6},{8,9},{9,8},{10,11... | collective-permute-start | bytes 589832 | tf_op jit(solution)/shard_map/ppermute | solution.py:56

commit v3 on v2

--- a/solution.py
+++ b/solution.py
@@ -185,11 +185,25 @@
     )(me, high, low, depth, basis)
 
 
-def image_kernel(work, fresh, me, depth, basis, *refs):
-    given, pieces, (out, high, low) = refs[: 2 if fresh else 1], refs[2 if fresh else 1 : -3], refs[-3:]
-    if fresh:
-        own = masked(basis[0], depth, 0)
-        out[...] = dot3(own, split(dot3(own, (given[0][...], given[1][...]), 0)), 1)
+def leaf_kernel(high, low, depth, basis, out):
+    own = masked(basis[0], depth, 0)
+    out[...] = dot3(own, split(dot3(own, (high[...], low[...]), 0)), 1)
+
+
+def leaf(high, low, depth, basis):
+    return pl.pallas_call(
+        leaf_kernel,
+        out_shape=jax.ShapeDtypeStruct((V, R), jnp.float32),
+        in_specs=[VMEM] * 4,
+        out_specs=VMEM,
+        compiler_params=pltpu.CompilerParams(vmem_limit_bytes=12 << 20),
+        cost_estimate=pl.CostEstimate(flops=12 * R * S * V, bytes_accessed=4 * V * R, transcendentals=0),
+        name="leaf",
+    )(high, low, depth, basis)
+
+
+def image_kernel(work, me, depth, basis, before, *refs):
+    pieces, (out, high, low) = refs[:-3], refs[-3:]
     for number, (slot, other, plan) in enumerate(work):
         levels, masks = slots(me[0], (me[0] & 1) ^ other)
         for unit, (piece, start) in enumerate(plan):
@@ -199,22 +213,22 @@
             low[number, pl.ds(row, UNIT), :] = part_low
         own = masked(basis[levels[slot]], depth, levels[slot])
         image = dot3(own, (high[number], low[number]), 1)
-        out[...] = (out[...] if fresh or number else given[0][...]) + image
-
-
-def images(work, fresh, limit, me, depth, basis, given, pieces):
+        out[...] = (out[...] if number else before[...]) + image
+
+
+def images(work, me, depth, basis, before, pieces):
     count = len(work)
     return pl.pallas_call(
-        functools.partial(image_kernel, work, fresh),
+        functools.partial(image_kernel, work),
         out_shape=jax.ShapeDtypeStruct((V, R), jnp.float32),
-        in_specs=[SMEM] + [VMEM] * (2 + len(given) + len(pieces)),
+        in_specs=[SMEM] + [VMEM] * (3 + len(pieces)),
         out_specs=VMEM,
         scratch_shapes=[pltpu.VMEM((count, S, R), jnp.bfloat16), pltpu.VMEM((count, S, R), jnp.bfloat16)],
-        compiler_params=pltpu.CompilerParams(vmem_limit_bytes=limit << 20),
+        compiler_params=pltpu.CompilerParams(vmem_limit_bytes=12 << 20),
         cost_estimate=pl.CostEstimate(
-            flops=(count + 2 * fresh) * 6 * R * S * V, bytes_accessed=count * 4 * S * (R + V), transcendentals=0
+            flops=count * 6 * R * S * V, bytes_accessed=count * 4 * S * (R + V), transcendentals=0
         ),
-    )(me, depth, basis, *given, *pieces)
+    )(me, depth, basis, before, *pieces)
 
 
 def plan_ab(slot):
@@ -233,7 +247,7 @@
 
 
 PLAN_C = [(u >> 3, (u & 7) * UNIT) for u in range(UNITS)]
-PLAN_D = [(2, u * UNIT) for u in range(UNITS)]
+PLAN_D = [(0, u * UNIT) for u in range(UNITS)]
 
 
 def local(kernel, rows, *arrays):
@@ -373,17 +387,19 @@
     c_low = c_low + send(c_low, pairs(along_z(2), along_z(4)))
     m4 = send(c_low, pairs(None, shifted_z(2)))
     (c_half,) = local(whole_kernel, (128,), me, c_low, c_high, m2, m4)
-    cd_pieces = (c_half, send(c_half, near), d)
-
-    their_cd = tuple(send(piece, SWAP) for piece in cd_pieces)
+    c_pieces = (c_half, send(c_half, near))
+
+    their_c = tuple(send(piece, SWAP) for piece in c_pieces)
+    their_d = send(d, SWAP)
     their_ab = tuple(send(piece, SWAP) for piece in ab_pieces)
 
+    result = leaf(high, low, depth, basis)
+    result = images([(2, 0, PLAN_C), (2, 1, shift_pieces(PLAN_C, 2))], me, depth, basis, result, c_pieces + their_c)
     result = images(
-        [(2, 0, PLAN_C), (3, 0, PLAN_D), (2, 1, shift_pieces(PLAN_C, 3)), (3, 1, shift_pieces(PLAN_D, 3))],
-        True, 16, me, depth, basis, (high, low), cd_pieces + their_cd,
+        [(3, 0, PLAN_D), (3, 1, shift_pieces(PLAN_D, 1)), (0, 0, shift_pieces(plan_ab(0), 2)), (1, 0, shift_pieces(plan_ab(1), 2))],
+        me, depth, basis, result, (d, their_d) + ab_pieces,
     )
-    result = images([(0, 0, plan_ab(0)), (1, 0, plan_ab(1))], False, 12, me, depth, basis, (result,), ab_pieces)
-    return images([(0, 1, plan_ab(0)), (1, 1, plan_ab(1))], False, 12, me, depth, basis, (result,), their_ab)
+    return images([(0, 1, plan_ab(0)), (1, 1, plan_ab(1))], me, depth, basis, result, their_ab)
 
 
 def solution(mesh):

time: 107 us -> 124 us (1.16)
  the two profiles are of different devices: /device:TPU:1 before, /device:TPU:3 now
where the time goes in v3:
time: 124 us
  starting transfers between devices  81.6 us (66%)
  waiting for transfers between devices  22.3 us (18%)
  Pallas kernels  19.1 us (15%)
    ppermute x30, starting transfers between devices, send(): return lax.ppermute(array, 'leaf', perm)  81.6 us
    ppermute x30, waiting for transfers between devices, send(): return lax.ppermute(array, 'leaf', perm)  22.3 us
    pallas_call x3, Pallas kernels, images(): pl.pallas_call(functools.partial(image_kernel, work), out_shape=jax.Shape...  7.51 us
    pallas_call x1, Pallas kernels, first_partials(): pl.pallas_call(first_kernel, out_shape=(jax.ShapeDtypeStruct((2 * S, R),...  4.65 us
    pallas_call x3, Pallas kernels, partials(): pl.pallas_call(functools.partial(partial_kernel, work), out_shape=jax.Sha...  4.49 us
  transfers between devices with their start and end apart: 30, of which 6 were waited for; matrix products, arithmetic and copies ran while one was open for 0% of the time, Pallas kernels for 9%

profile of v3, /device:TPU:3, one launch (start us, length us, event | category | flops | bytes accessed | tf_op | source)
XLA Modules:
  0.0 124.2 jit_solution(1655923592592537920)
XLA Ops:
  0.7 4.7 %send_ab.1 = (f32[512,768]{1,0:T(8,128)S(1)}, bf16[512,768]{1,0:T(8,128)(2,1)S(1)}, bf16[512,768]{1,0:T(8,128)(2,1)S(1)}, f32[512,128]{1,0:T(8,128)S(1)}) custom-call(s32[1]{0:T(128)} %bitcast.me, s32[1,512]{1,0:T(1,128)S(1)} %bitcast.2, f32[512,768]{1,0:T(8,128)} %rhs_hbm.1, f32[9,512,256]{2,1,0:T(8,128)} %basis.13), custom_call_target="tpu_custom_call" | custom-call | flops 1207959552 | bytes 2621440 | tf_op jit(solution)/shard_map/send_ab/pallas_call | solution.py:146
  6.1 1.5 %shard_map.38 = f32[512,768]{1,0:T(8,128)S(1)} custom-call(s32[1]{0:T(128)} %bitcast.me, bf16[512,768]{1,0:T(8,128)(2,1)S(1)} %get-tuple-element.29.high, bf16[512,768]{1,0:T(8,128)(2,1)S(1)} %get-tuple-element.30.low, f32[512,128]{1,0:T(8,128)S(1)} %get-tuple-element.28.depth, f32[9,512,256]{2,1,0:T(8,128)S(1)} %copy-done), custom_call_target="tpu_custom_call" | custom-call | flops 1207959552 | bytes 2621440 | tf_op jit(solution)/shard_map/pallas_call | solution.py:176
  7.7 1.5 %shard_map.44.kept = f32[512,768]{1,0:T(8,128)S(1)} custom-call(s32[1]{0:T(128)} %bitcast.me, bf16[512,768]{1,0:T(8,128)(2,1)S(1)} %get-tuple-element.29.high, bf16[512,768]{1,0:T(8,128)(2,1)S(1)} %get-tuple-element.30.low, f32[512,128]{1,0:T(8,128)S(1)} %get-tuple-element.28.depth, f32[9,512,256]{2,1,0:T(8,128)S(1)} %copy-done), custom_call_target="tpu_custom_call" | custom-call | flops 1207959552 | bytes 2621440 | tf_op jit(solution)/shard_map/pallas_call | solution.py:176
  9.4 2.0 %collective-permute-start.11 = (f32[192,768]{1,0:T(8,128)S(1)}, f32[192,768]{1,0:T(8,128)S(1)}, u32[]{:S(2)}, u32[]{:S(2)}) collective-permute-start(f32[192,768]{1,0:T(8,128)S(1)} %get-tuple-element.38), channel_id=1, source_target_pairs={{0,16},{1,65},{2,18},{3,67},{4,20},{5,69},{6,22},{7,71},{8,24},{9,... | collective-permute-start | bytes 1769480 | tf_op jit(solution)/shard_map/ppermute | solution.py:56
  12.7 1.5 %shard_map.37.kept = f32[512,768]{1,0:T(8,128)S(1)} custom-call(s32[1]{0:T(128)} %bitcast.me, bf16[512,768]{1,0:T(8,128)(2,1)S(1)} %get-tuple-element.29.high, bf16[512,768]{1,0:T(8,128)(2,1)S(1)} %get-tuple-element.30.low, f32[512,128]{1,0:T(8,128)S(1)} %get-tuple-element.28.depth, f32[9,512,256]{2,1,0:T(8,128)S(1)} %copy-done), custom_call_target="tpu_custom_call" | custom-call | flops 1207959552 | bytes 2621440 | tf_op jit(solution)/shard_map/pallas_call | solution.py:176
  14.4 5.1 %collective-permute-start.1 = (f32[128,768]{1,0:T(8,128)S(1)}, f32[128,768]{1,0:T(8,128)S(1)}, u32[]{:S(2)}, u32[]{:S(2)}) collective-permute-start(f32[128,768]{1,0:T(8,128)S(1)} %get-tuple-element.32), channel_id=1, source_target_pairs={{0,2},{1,15},{2,0},{3,5},{4,6},{5,3},{6,4},{7,9},{8,10},{9,7},{10,... | collective-permute-start | bytes 1179656 | tf_op jit(solution)/shard_map/ppermute | solution.py:56
  19.5 1.8 %collective-permute-done.12.r2 = f32[64,768]{1,0:T(8,128)S(1)} collective-permute-done((f32[64,768]{1,0:T(8,128)S(1)}, f32[64,768]{1,0:T(8,128)S(1)}, u32[]{:S(2)}, u32[]{:S(2)}) %collective-permute-start.12) | collective-permute-done | bytes 196640 | tf_op jit(solution)/shard_map/ppermute | solution.py:56
  21.4 1.7 %collective-permute-start.14 = (f32[48,768]{1,0:T(8,128)S(1)}, f32[48,768]{1,0:T(8,128)S(1)}, u32[]{:S(2)}, u32[]{:S(2)}) collective-permute-start(f32[48,768]{1,0:T(8,128)S(1)} %get-tuple-element.43), channel_id=1, source_target_pairs={{0,14},{1,17},{2,4},{3,19},{4,2},{5,21},{6,8},{7,23},{8,6},{9,25},... | collective-permute-start | bytes 442376 | tf_op jit(solution)/shard_map/ppermute | solution.py:56
  23.0 2.3 %collective-permute-start.15 = (f32[48,768]{1,0:T(8,128)S(1)}, f32[48,768]{1,0:T(8,128)S(1)}, u32[]{:S(2)}, u32[]{:S(2)}) collective-permute-start(f32[48,768]{1,0:T(8,128)S(1)} %get-tuple-element.44), channel_id=1, source_target_pairs={{0,14},{1,33},{2,4},{3,35},{4,2},{5,37},{6,8},{7,39},{8,6},{9,41},... | collective-permute-start | bytes 442376 | tf_op jit(solution)/shard_map/ppermute | solution.py:56
  25.4 2.1 %collective-permute-start.16 = (f32[48,768]{1,0:T(8,128)S(1)}, f32[48,768]{1,0:T(8,128)S(1)}, u32[]{:S(2)}, u32[]{:S(2)}) collective-permute-start(f32[48,768]{1,0:T(8,128)S(1)} %get-tuple-element.42.u3), channel_id=1, source_target_pairs={{1,49},{3,51},{5,53},{7,55},{9,57},{11,59},{13,61},{15,63},{17,33}... | collective-permute-start | bytes 442376 | tf_op jit(solution)/shard_map/ppermute | solution.py:56
  28.2 1.3 %collective-permute-done.15.t2 = f32[48,768]{1,0:T(8,128)S(1)} collective-permute-done((f32[48,768]{1,0:T(8,128)S(1)}, f32[48,768]{1,0:T(8,128)S(1)}, u32[]{:S(2)}, u32[]{:S(2)}) %collective-permute-start.15) | collective-permute-done | bytes 147488 | tf_op jit(solution)/shard_map/ppermute | solution.py:56
  29.5 3.3 %collective-permute-done.16.t3 = f32[48,768]{1,0:T(8,128)S(1)} collective-permute-done((f32[48,768]{1,0:T(8,128)S(1)}, f32[48,768]{1,0:T(8,128)S(1)}, u32[]{:S(2)}, u32[]{:S(2)}) %collective-permute-start.16) | collective-permute-done | bytes 147488 | tf_op jit(solution)/shard_map/ppermute | solution.py:56
  32.8 1.4 %collective-permute-start.17 = (f32[48,768]{1,0:T(8,128)S(1)}, f32[48,768]{1,0:T(8,128)S(1)}, u32[]{:S(2)}, u32[]{:S(2)}) collective-permute-start(f32[48,768]{1,0:T(8,128)S(1)} %get-tuple-element.46), channel_id=1, source_target_pairs={{0,12},{1,3},{2,6},{3,1},{4,8},{5,7},{6,2},{7,5},{8,4},{9,11},{10,... | collective-permute-start | bytes 442376 | tf_op jit(solution)/shard_map/ppermute | solution.py:56
  34.3 5.4 %collective-permute-start.2 = (f32[64,768]{1,0:T(8,128)S(1)}, f32[64,768]{1,0:T(8,128)S(1)}, u32[]{:S(2)}, u32[]{:S(2)}) collective-permute-start(f32[64,768]{1,0:T(8,128)S(1)} %get-tuple-element.34.c_high), channel_id=1, source_target_pairs={{0,4},{1,13},{2,6},{3,7},{4,0},{5,9},{6,2},{7,3},{8,12},{9,5},{10,... | collective-permute-start | bytes 589832 | tf_op jit(solution)/shard_map/ppermute | solution.py:56
  39.7 7.4 %collective-permute-start.18 = (f32[48,768]{1,0:T(8,128)S(1)}, f32[48,768]{1,0:T(8,128)S(1)}, u32[]{:S(2)}, u32[]{:S(2)}) collective-permute-start(f32[48,768]{1,0:T(8,128)S(1)} %add.14), channel_id=1, source_target_pairs={{0,8},{1,5},{2,10},{3,7},{4,12},{5,1},{6,14},{7,3},{8,0},{9,13},{1... | collective-permute-start | bytes 442376 | tf_op jit(solution)/shard_map/ppermute | solution.py:56
  47.1 6.4 %collective-permute-done.2.m2 = f32[64,768]{1,0:T(8,128)S(1)} collective-permute-done((f32[64,768]{1,0:T(8,128)S(1)}, f32[64,768]{1,0:T(8,128)S(1)}, u32[]{:S(2)}, u32[]{:S(2)}) %collective-permute-start.2) | collective-permute-done | bytes 196640 | tf_op jit(solution)/shard_map/ppermute | solution.py:56
  53.5 1.5 %collective-permute-start.3 = (f32[64,768]{1,0:T(8,128)S(1)}, f32[64,768]{1,0:T(8,128)S(1)}, u32[]{:S(2)}, u32[]{:S(2)}) collective-permute-start(f32[64,768]{1,0:T(8,128)S(1)} %shard_map.41), channel_id=1, source_target_pairs={{0,4},{1,9},{2,6},{3,11},{4,0},{5,13},{6,2},{7,15},{8,12},{9,1},{1... | collective-permute-start | bytes 589832 | tf_op jit(solution)/shard_map/ppermute | solution.py:56
  55.1 4.0 %collective-permute-start.19 = (f32[48,768]{1,0:T(8,128)S(1)}, f32[48,768]{1,0:T(8,128)S(1)}, u32[]{:S(2)}, u32[]{:S(2)}) collective-permute-start(f32[48,768]{1,0:T(8,128)S(1)} %add.15.total), channel_id=1, source_target_pairs={{0,12},{1,9},{2,6},{3,11},{4,8},{5,13},{6,2},{7,15},{8,4},{9,1},{1... | collective-permute-start | bytes 442376 | tf_op jit(solution)/shard_map/ppermute | solution.py:56
  59.1 6.8 %collective-permute-done.19.other = f32[48,768]{1,0:T(8,128)S(1)} collective-permute-done((f32[48,768]{1,0:T(8,128)S(1)}, f32[48,768]{1,0:T(8,128)S(1)}, u32[]{:S(2)}, u32[]{:S(2)}) %collective-permute-start.19) | collective-permute-done | bytes 147488 | tf_op jit(solution)/shard_map/ppermute | solution.py:56
  66.0 1.6 %collective-permute-start.21 = (f32[48,768]{1,0:T(8,128)S(1)}, f32[48,768]{1,0:T(8,128)S(1)}, u32[]{:S(2)}, u32[]{:S(2)}) collective-permute-start(f32[48,768]{1,0:T(8,128)S(1)} %get-tuple-element.48), channel_id=1, source_target_pairs={{0,14},{1,33},{2,4},{3,35},{4,2},{5,37},{6,8},{7,39},{8,6},{9,41},... | collective-permute-start | bytes 442376 | tf_op jit(solution)/shard_map/ppermute | solution.py:56
  67.6 4.1 %collective-permute-start.22 = (f32[48,768]{1,0:T(8,128)S(1)}, f32[48,768]{1,0:T(8,128)S(1)}, u32[]{:S(2)}, u32[]{:S(2)}) collective-permute-start(f32[48,768]{1,0:T(8,128)S(1)} %get-tuple-element.47.total), channel_id=1, source_target_pairs={{1,49},{3,51},{5,53},{7,55},{9,57},{11,59},{13,61},{15,63},{17,33}... | collective-permute-start | bytes 442376 | tf_op jit(solution)/shard_map/ppermute | solution.py:56
  71.8 4.2 %collective-permute-start.4 = (f32[64,768]{1,0:T(8,128)S(1)}, f32[64,768]{1,0:T(8,128)S(1)}, u32[]{:S(2)}, u32[]{:S(2)}) collective-permute-start(f32[64,768]{1,0:T(8,128)S(1)} %add.12.c_low), channel_id=1, source_target_pairs={{1,13},{3,7},{5,9},{7,3},{9,5},{11,15},{13,1},{15,11},{17,29},{19,... | collective-permute-start | bytes 589832 | tf_op jit(solution)/shard_map/ppermute | solution.py:56
  76.1 9.6 %collective-permute-start.23 = (f32[192,768]{1,0:T(8,128)S(1)}, f32[192,768]{1,0:T(8,128)S(1)}, u32[]{:S(2)}, u32[]{:S(2)}) collective-permute-start(f32[192,768]{1,0:T(8,128)S(1)} %get-tuple-element.49.refs_2_), channel_id=1, source_target_pairs={{0,16},{1,65},{2,18},{3,67},{4,20},{5,69},{6,22},{7,71},{8,24},{9,... | collective-permute-start | bytes 1769480 | tf_op jit(solution)/shard_map/ppermute | solution.py:56
  85.9 12.0 %collective-permute-start.9 = (f32[256,768]{1,0:T(8,128)S(1)}, f32[256,768]{1,0:T(8,128)S(1)}, u32[]{:S(2)}, u32[]{:S(2)}) collective-permute-start(f32[256,768]{1,0:T(8,128)S(1)} %add.13.refs_0_), channel_id=1, source_target_pairs={{0,1},{1,0},{2,3},{3,2},{4,5},{5,4},{6,7},{7,6},{8,9},{9,8},{10,11... | collective-permute-start | bytes 2359304 | tf_op jit(solution)/shard_map/ppermute | solution.py:56
  98.0 7.4 %collective-permute-start.7 = (f32[128,768]{1,0:T(8,128)S(1)}, f32[128,768]{1,0:T(8,128)S(1)}, u32[]{:S(2)}, u32[]{:S(2)}) collective-permute-start(f32[128,768]{1,0:T(8,128)S(1)} %collective-permute-done.5.refs_1_), channel_id=1, source_target_pairs={{0,1},{1,0},{2,3},{3,2},{4,5},{5,4},{6,7},{7,6},{8,9},{9,8},{10,11... | collective-permute-start | bytes 1179656 | tf_op jit(solution)/shard_map/ppermute | solution.py:56
  105.5 1.9 %collective-permute-start.27 = (f32[192,768]{1,0:T(8,128)S(1)}, f32[192,768]{1,0:T(8,128)S(1)}, u32[]{:S(2)}, u32[]{:S(2)}) collective-permute-start(f32[192,768]{1,0:T(8,128)S(1)} %collective-permute-done.23.refs_3_), channel_id=1, source_target_pairs={{0,1},{1,0},{2,3},{3,2},{4,5},{5,4},{6,7},{7,6},{8,9},{9,8},{10,11... | collective-permute-start | bytes 1769480 | tf_op jit(solution)/shard_map/ppermute | solution.py:56
  107.4 1.8 %leaf.1.before = f32[512,768]{1,0:T(8,128)S(1)} custom-call(bf16[512,768]{1,0:T(8,128)(2,1)S(1)} %get-tuple-element.29.high, bf16[512,768]{1,0:T(8,128)(2,1)S(1)} %get-tuple-element.30.low, f32[512,128]{1,0:T(8,128)S(1)} %get-tuple-element.28.depth, f32[9,512,256]{2,1,0:T(8,128)S(1)} %copy-done), custom_call_target="tpu_custom_call" | custom-call | flops 1207959552 | bytes 1572864 | tf_op jit(solution)/shard_map/leaf/pallas_call | solution.py:194
  109.3 2.7 %collective-permute-done.25.refs_5_ = f32[64,768]{1,0:T(8,128)S(1)} collective-permute-done((f32[64,768]{1,0:T(8,128)S(1)}, f32[64,768]{1,0:T(8,128)S(1)}, u32[]{:S(2)}, u32[]{:S(2)}) %collective-permute-start.25) | collective-permute-done | bytes 196640 | tf_op jit(solution)/shard_map/ppermute | solution.py:56
  112.0 4.6 %collective-permute-start.28 = (f32[64,768]{1,0:T(8,128)S(1)}, f32[64,768]{1,0:T(8,128)S(1)}, u32[]{:S(2)}, u32[]{:S(2)}) collective-permute-start(f32[64,768]{1,0:T(8,128)S(1)} %collective-permute-done.24.refs_4_), channel_id=1, source_target_pairs={{0,1},{1,0},{2,3},{3,2},{4,5},{5,4},{6,7},{7,6},{8,9},{9,8},{10,11... | collective-permute-start | bytes 589832 | tf_op jit(solution)/shard_map/ppermute | solution.py:56
  116.6 1.7 %shard_map.43.before = f32[512,768]{1,0:T(8,128)S(1)} custom-call(s32[1]{0:T(128)} %bitcast.me, f32[512,128]{1,0:T(8,128)S(1)} %get-tuple-element.28.depth, f32[9,512,256]{2,1,0:T(8,128)S(1)} %copy-done, f32[512,768]{1,0:T(8,128)S(1)} %leaf.1.before, f32[128,768]{1,0:T(8,128)S(1)} %shard_map.42.refs_0_, f32[128,768]{1,0:T(8,128)S(1)} %collective-permute-done.5.refs_1_, ...), custom_call_target="tpu_custom_call" | custom-call | flops 1207959552 | bytes 2621440 | tf_op jit(solution)/shard_map/pallas_call | solution.py:221
  118.3 3.0 %shard_map.50.before = f32[512,768]{1,0:T(8,128)S(1)} custom-call(s32[1]{0:T(128)} %bitcast.me, f32[512,128]{1,0:T(8,128)S(1)} %get-tuple-element.28.depth, f32[9,512,256]{2,1,0:T(8,128)S(1)} %copy-done, f32[512,768]{1,0:T(8,128)S(1)} %shard_map.43.before, f32[256,768]{1,0:T(8,128)S(1)} %add.13.refs_0_, f32[256,768]{1,0:T(8,128)S(1)} %collective-permute-done.9.refs_1_, ...), custom_call_target="tpu_custom_call" | custom-call | flops 2415919104 | bytes 5242880 | tf_op jit(solution)/shard_map/pallas_call | solution.py:221
  121.3 2.8 %shard_map.51 = f32[512,768]{1,0:T(8,128)} custom-call(s32[1]{0:T(128)} %bitcast.me, f32[512,128]{1,0:T(8,128)S(1)} %get-tuple-element.28.depth, f32[9,512,256]{2,1,0:T(8,128)S(1)} %copy-done, f32[512,768]{1,0:T(8,128)S(1)} %shard_map.50.before, f32[192,768]{1,0:T(8,128)S(1)} %collective-permute-done.26.refs_0_, ...), custom_call_target="tpu_custom_call" | custom-call | flops 1207959552 | bytes 2621440 | tf_op jit(solution)/shard_map/pallas_call | solution.py:221
  (53 shorter events, 4.7 us)
Async XLA Ops:
  0.0 0.7 copy-start.1
  0.7 5.4 %copy-start = (f32[9,512,256]{2,1,0:T(8,128)S(1)}, f32[9,512,256]{2,1,0:T(8,128)}, u32[]{:S(2)}) copy-start(f32[9,512,256]{2,1,0:T(8,128)} %basis.13) | copy-start | bytes 14155780
  5.3 3.9 %collective-permute-start.10 = (f32[512,768]{1,0:T(8,128)S(1)}, f32[512,768]{1,0:T(8,128)S(1)}, u32[]{:S(2)}, u32[]{:S(2)}) collective-permute-start(f32[512,768]{1,0:T(8,128)S(1)} %get-tuple-element.36), channel_id=1, source_target_pairs={{0,1},{1,0},{2,3},{3,2},{4,5},{5,4},{6,7},{7,6},{8,9},{9,8},{10,11... | collective-permute-start | bytes 4718600 | tf_op jit(solution)/shard_map/ppermute | solution.py:56
  7.6 6.6 %collective-permute-start = (f32[512,768]{1,0:T(8,128)S(1)}, f32[512,768]{1,0:T(8,128)S(1)}, u32[]{:S(2)}, u32[]{:S(2)}) collective-permute-start(f32[512,768]{1,0:T(8,128)S(1)} %shard_map.38), channel_id=1, source_target_pairs={{0,1},{1,0},{2,3},{3,2},{4,5},{5,4},{6,7},{7,6},{8,9},{9,8},{10,11... | collective-permute-start | bytes 4718600 | tf_op jit(solution)/shard_map/ppermute | solution.py:56
  9.4 11.9 %collective-permute-start.11 = (f32[192,768]{1,0:T(8,128)S(1)}, f32[192,768]{1,0:T(8,128)S(1)}, u32[]{:S(2)}, u32[]{:S(2)}) collective-permute-start(f32[192,768]{1,0:T(8,128)S(1)} %get-tuple-element.38), channel_id=1, source_target_pairs={{0,16},{1,65},{2,18},{3,67},{4,20},{5,69},{6,22},{7,71},{8,24},{9,... | collective-permute-start | bytes 1769480 | tf_op jit(solution)/shard_map/ppermute | solution.py:56
  11.5 9.8 %collective-permute-start.12 = (f32[64,768]{1,0:T(8,128)S(1)}, f32[64,768]{1,0:T(8,128)S(1)}, u32[]{:S(2)}, u32[]{:S(2)}) collective-permute-start(f32[64,768]{1,0:T(8,128)S(1)} %get-tuple-element.39), channel_id=1, source_target_pairs={{0,32},{1,129},{2,34},{3,131},{4,36},{5,133},{6,38},{7,135},{8,40}... | collective-permute-start | bytes 589832 | tf_op jit(solution)/shard_map/ppermute | solution.py:56
  11.9 9.4 %collective-permute-start.13 = (f32[64,768]{1,0:T(8,128)S(1)}, f32[64,768]{1,0:T(8,128)S(1)}, u32[]{:S(2)}, u32[]{:S(2)}) collective-permute-start(f32[64,768]{1,0:T(8,128)S(1)} %get-tuple-element.40), channel_id=1, source_target_pairs={{0,48},{1,193},{2,50},{3,195},{4,52},{5,197},{6,54},{7,199},{8,56}... | collective-permute-start | bytes 589832 | tf_op jit(solution)/shard_map/ppermute | solution.py:56
  14.4 19.8 %collective-permute-start.1 = (f32[128,768]{1,0:T(8,128)S(1)}, f32[128,768]{1,0:T(8,128)S(1)}, u32[]{:S(2)}, u32[]{:S(2)}) collective-permute-start(f32[128,768]{1,0:T(8,128)S(1)} %get-tuple-element.32), channel_id=1, source_target_pairs={{0,2},{1,15},{2,0},{3,5},{4,6},{5,3},{6,4},{7,9},{8,10},{9,7},{10,... | collective-permute-start | bytes 1179656 | tf_op jit(solution)/shard_map/ppermute | solution.py:56
  21.4 6.8 %collective-permute-start.14 = (f32[48,768]{1,0:T(8,128)S(1)}, f32[48,768]{1,0:T(8,128)S(1)}, u32[]{:S(2)}, u32[]{:S(2)}) collective-permute-start(f32[48,768]{1,0:T(8,128)S(1)} %get-tuple-element.43), channel_id=1, source_target_pairs={{0,14},{1,17},{2,4},{3,19},{4,2},{5,21},{6,8},{7,23},{8,6},{9,25},... | collective-permute-start | bytes 442376 | tf_op jit(solution)/shard_map/ppermute | solution.py:56
  23.0 6.4 %collective-permute-start.15 = (f32[48,768]{1,0:T(8,128)S(1)}, f32[48,768]{1,0:T(8,128)S(1)}, u32[]{:S(2)}, u32[]{:S(2)}) collective-permute-start(f32[48,768]{1,0:T(8,128)S(1)} %get-tuple-element.44), channel_id=1, source_target_pairs={{0,14},{1,33},{2,4},{3,35},{4,2},{5,37},{6,8},{7,39},{8,6},{9,41},... | collective-permute-start | bytes 442376 | tf_op jit(solution)/shard_map/ppermute | solution.py:56
  25.4 7.4 %collective-permute-start.16 = (f32[48,768]{1,0:T(8,128)S(1)}, f32[48,768]{1,0:T(8,128)S(1)}, u32[]{:S(2)}, u32[]{:S(2)}) collective-permute-start(f32[48,768]{1,0:T(8,128)S(1)} %get-tuple-element.42.u3), channel_id=1, source_target_pairs={{1,49},{3,51},{5,53},{7,55},{9,57},{11,59},{13,61},{15,63},{17,33}... | collective-permute-start | bytes 442376 | tf_op jit(solution)/shard_map/ppermute | solution.py:56
  27.4 58.4 %collective-permute-start.8 = (f32[256,768]{1,0:T(8,128)S(1)}, f32[256,768]{1,0:T(8,128)S(1)}, u32[]{:S(2)}, u32[]{:S(2)}) collective-permute-start(f32[256,768]{1,0:T(8,128)S(1)} %get-tuple-element.35), channel_id=1, source_target_pairs={{0,2},{2,0},{4,6},{6,4},{8,10},{10,8},{12,14},{14,12},{16,18},{18,... | collective-permute-start | bytes 2359304 | tf_op jit(solution)/shard_map/ppermute | solution.py:56
  32.8 6.9 %collective-permute-start.17 = (f32[48,768]{1,0:T(8,128)S(1)}, f32[48,768]{1,0:T(8,128)S(1)}, u32[]{:S(2)}, u32[]{:S(2)}) collective-permute-start(f32[48,768]{1,0:T(8,128)S(1)} %get-tuple-element.46), channel_id=1, source_target_pairs={{0,12},{1,3},{2,6},{3,1},{4,8},{5,7},{6,2},{7,5},{8,4},{9,11},{10,... | collective-permute-start | bytes 442376 | tf_op jit(solution)/shard_map/ppermute | solution.py:56
  34.3 19.2 %collective-permute-start.2 = (f32[64,768]{1,0:T(8,128)S(1)}, f32[64,768]{1,0:T(8,128)S(1)}, u32[]{:S(2)}, u32[]{:S(2)}) collective-permute-start(f32[64,768]{1,0:T(8,128)S(1)} %get-tuple-element.34.c_high), channel_id=1, source_target_pairs={{0,4},{1,13},{2,6},{3,7},{4,0},{5,9},{6,2},{7,3},{8,12},{9,5},{10,... | collective-permute-start | bytes 589832 | tf_op jit(solution)/shard_map/ppermute | solution.py:56
  39.7 15.4 %collective-permute-start.18 = (f32[48,768]{1,0:T(8,128)S(1)}, f32[48,768]{1,0:T(8,128)S(1)}, u32[]{:S(2)}, u32[]{:S(2)}) collective-permute-start(f32[48,768]{1,0:T(8,128)S(1)} %add.14), channel_id=1, source_target_pairs={{0,8},{1,5},{2,10},{3,7},{4,12},{5,1},{6,14},{7,3},{8,0},{9,13},{1... | collective-permute-start | bytes 442376 | tf_op jit(solution)/shard_map/ppermute | solution.py:56
  53.5 18.2 %collective-permute-start.3 = (f32[64,768]{1,0:T(8,128)S(1)}, f32[64,768]{1,0:T(8,128)S(1)}, u32[]{:S(2)}, u32[]{:S(2)}) collective-permute-start(f32[64,768]{1,0:T(8,128)S(1)} %shard_map.41), channel_id=1, source_target_pairs={{0,4},{1,9},{2,6},{3,11},{4,0},{5,13},{6,2},{7,15},{8,12},{9,1},{1... | collective-permute-start | bytes 589832 | tf_op jit(solution)/shard_map/ppermute | solution.py:56
  55.1 10.8 %collective-permute-start.19 = (f32[48,768]{1,0:T(8,128)S(1)}, f32[48,768]{1,0:T(8,128)S(1)}, u32[]{:S(2)}, u32[]{:S(2)}) collective-permute-start(f32[48,768]{1,0:T(8,128)S(1)} %add.15.total), channel_id=1, source_target_pairs={{0,12},{1,9},{2,6},{3,11},{4,8},{5,13},{6,2},{7,15},{8,4},{9,1},{1... | collective-permute-start | bytes 442376 | tf_op jit(solution)/shard_map/ppermute | solution.py:56
  65.9 10.1 %collective-permute-start.20 = (f32[48,768]{1,0:T(8,128)S(1)}, f32[48,768]{1,0:T(8,128)S(1)}, u32[]{:S(2)}, u32[]{:S(2)}) collective-permute-start(f32[48,768]{1,0:T(8,128)S(1)} %get-tuple-element.47.total), channel_id=1, source_target_pairs={{0,14},{1,17},{2,4},{3,19},{4,2},{5,21},{6,8},{7,23},{8,6},{9,25},... | collective-permute-start | bytes 442376 | tf_op jit(solution)/shard_map/ppermute | solution.py:56
  66.0 10.0 %collective-permute-start.21 = (f32[48,768]{1,0:T(8,128)S(1)}, f32[48,768]{1,0:T(8,128)S(1)}, u32[]{:S(2)}, u32[]{:S(2)}) collective-permute-start(f32[48,768]{1,0:T(8,128)S(1)} %get-tuple-element.48), channel_id=1, source_target_pairs={{0,14},{1,33},{2,4},{3,35},{4,2},{5,37},{6,8},{7,39},{8,6},{9,41},... | collective-permute-start | bytes 442376 | tf_op jit(solution)/shard_map/ppermute | solution.py:56
  67.6 8.4 %collective-permute-start.22 = (f32[48,768]{1,0:T(8,128)S(1)}, f32[48,768]{1,0:T(8,128)S(1)}, u32[]{:S(2)}, u32[]{:S(2)}) collective-permute-start(f32[48,768]{1,0:T(8,128)S(1)} %get-tuple-element.47.total), channel_id=1, source_target_pairs={{1,49},{3,51},{5,53},{7,55},{9,57},{11,59},{13,61},{15,63},{17,33}... | collective-permute-start | bytes 442376 | tf_op jit(solution)/shard_map/ppermute | solution.py:56
  71.8 13.9 %collective-permute-start.4 = (f32[64,768]{1,0:T(8,128)S(1)}, f32[64,768]{1,0:T(8,128)S(1)}, u32[]{:S(2)}, u32[]{:S(2)}) collective-permute-start(f32[64,768]{1,0:T(8,128)S(1)} %add.12.c_low), channel_id=1, source_target_pairs={{1,13},{3,7},{5,9},{7,3},{9,5},{11,15},{13,1},{15,11},{17,29},{19,... | collective-permute-start | bytes 589832 | tf_op jit(solution)/shard_map/ppermute | solution.py:56
  76.1 29.4 %collective-permute-start.23 = (f32[192,768]{1,0:T(8,128)S(1)}, f32[192,768]{1,0:T(8,128)S(1)}, u32[]{:S(2)}, u32[]{:S(2)}) collective-permute-start(f32[192,768]{1,0:T(8,128)S(1)} %get-tuple-element.49.refs_2_), channel_id=1, source_target_pairs={{0,16},{1,65},{2,18},{3,67},{4,20},{5,69},{6,22},{7,71},{8,24},{9,... | collective-permute-start | bytes 1769480 | tf_op jit(solution)/shard_map/ppermute | solution.py:56
  85.7 12.3 %collective-permute-start.5 = (f32[128,768]{1,0:T(8,128)S(1)}, f32[128,768]{1,0:T(8,128)S(1)}, u32[]{:S(2)}, u32[]{:S(2)}) collective-permute-start(f32[128,768]{1,0:T(8,128)S(1)} %shard_map.42.refs_0_), channel_id=1, source_target_pairs={{0,2},{1,15},{2,0},{3,5},{4,6},{5,3},{6,4},{7,9},{8,10},{9,7},{10,... | collective-permute-start | bytes 1179656 | tf_op jit(solution)/shard_map/ppermute | solution.py:56
  85.9 32.3 %collective-permute-start.9 = (f32[256,768]{1,0:T(8,128)S(1)}, f32[256,768]{1,0:T(8,128)S(1)}, u32[]{:S(2)}, u32[]{:S(2)}) collective-permute-start(f32[256,768]{1,0:T(8,128)S(1)} %add.13.refs_0_), channel_id=1, source_target_pairs={{0,1},{1,0},{2,3},{3,2},{4,5},{5,4},{6,7},{7,6},{8,9},{9,8},{10,11... | collective-permute-start | bytes 2359304 | tf_op jit(solution)/shard_map/ppermute | solution.py:56
  97.9 7.6 %collective-permute-start.6 = (f32[128,768]{1,0:T(8,128)S(1)}, f32[128,768]{1,0:T(8,128)S(1)}, u32[]{:S(2)}, u32[]{:S(2)}) collective-permute-start(f32[128,768]{1,0:T(8,128)S(1)} %shard_map.42.refs_0_), channel_id=1, source_target_pairs={{0,1},{1,0},{2,3},{3,2},{4,5},{5,4},{6,7},{7,6},{8,9},{9,8},{10,11... | collective-permute-start | bytes 1179656 | tf_op jit(solution)/shard_map/ppermute | solution.py:56
  98.0 9.4 %collective-permute-start.24 = (f32[64,768]{1,0:T(8,128)S(1)}, f32[64,768]{1,0:T(8,128)S(1)}, u32[]{:S(2)}, u32[]{:S(2)}) collective-permute-start(f32[64,768]{1,0:T(8,128)S(1)} %get-tuple-element.50), channel_id=1, source_target_pairs={{0,32},{1,129},{2,34},{3,131},{4,36},{5,133},{6,38},{7,135},{8,40}... | collective-permute-start | bytes 589832 | tf_op jit(solution)/shard_map/ppermute | solution.py:56
  98.0 18.5 %collective-permute-start.7 = (f32[128,768]{1,0:T(8,128)S(1)}, f32[128,768]{1,0:T(8,128)S(1)}, u32[]{:S(2)}, u32[]{:S(2)}) collective-permute-start(f32[128,768]{1,0:T(8,128)S(1)} %collective-permute-done.5.refs_1_), channel_id=1, source_target_pairs={{0,1},{1,0},{2,3},{3,2},{4,5},{5,4},{6,7},{7,6},{8,9},{9,8},{10,11... | collective-permute-start | bytes 1179656 | tf_op jit(solution)/shard_map/ppermute | solution.py:56
  105.5 15.8 %collective-permute-start.26 = (f32[192,768]{1,0:T(8,128)S(1)}, f32[192,768]{1,0:T(8,128)S(1)}, u32[]{:S(2)}, u32[]{:S(2)}) collective-permute-start(f32[192,768]{1,0:T(8,128)S(1)} %get-tuple-element.49.refs_2_), channel_id=1, source_target_pairs={{0,1},{1,0},{2,3},{3,2},{4,5},{5,4},{6,7},{7,6},{8,9},{9,8},{10,11... | collective-permute-start | bytes 1769480 | tf_op jit(solution)/shard_map/ppermute | solution.py:56
  105.5 15.8 %collective-permute-start.27 = (f32[192,768]{1,0:T(8,128)S(1)}, f32[192,768]{1,0:T(8,128)S(1)}, u32[]{:S(2)}, u32[]{:S(2)}) collective-permute-start(f32[192,768]{1,0:T(8,128)S(1)} %collective-permute-done.23.refs_3_), channel_id=1, source_target_pairs={{0,1},{1,0},{2,3},{3,2},{4,5},{5,4},{6,7},{7,6},{8,9},{9,8},{10,11... | collective-permute-start | bytes 1769480 | tf_op jit(solution)/shard_map/ppermute | solution.py:56
  107.4 4.5 %collective-permute-start.25 = (f32[64,768]{1,0:T(8,128)S(1)}, f32[64,768]{1,0:T(8,128)S(1)}, u32[]{:S(2)}, u32[]{:S(2)}) collective-permute-start(f32[64,768]{1,0:T(8,128)S(1)} %get-tuple-element.50), channel_id=1, source_target_pairs={{0,48},{1,193},{2,50},{3,195},{4,52},{5,197},{6,54},{7,199},{8,56}... | collective-permute-start | bytes 589832 | tf_op jit(solution)/shard_map/ppermute | solution.py:56
  112.0 9.3 %collective-permute-start.28 = (f32[64,768]{1,0:T(8,128)S(1)}, f32[64,768]{1,0:T(8,128)S(1)}, u32[]{:S(2)}, u32[]{:S(2)}) collective-permute-start(f32[64,768]{1,0:T(8,128)S(1)} %collective-permute-done.24.refs_4_), channel_id=1, source_target_pairs={{0,1},{1,0},{2,3},{3,2},{4,5},{5,4},{6,7},{7,6},{8,9},{9,8},{10,11... | collective-permute-start | bytes 589832 | tf_op jit(solution)/shard_map/ppermute | solution.py:56
  116.6 4.7 %collective-permute-start.29 = (f32[64,768]{1,0:T(8,128)S(1)}, f32[64,768]{1,0:T(8,128)S(1)}, u32[]{:S(2)}, u32[]{:S(2)}) collective-permute-start(f32[64,768]{1,0:T(8,128)S(1)} %collective-permute-done.25.refs_5_), channel_id=1, source_target_pairs={{0,1},{1,0},{2,3},{3,2},{4,5},{5,4},{6,7},{7,6},{8,9},{9,8},{10,11... | collective-permute-start | bytes 589832 | tf_op jit(solution)/shard_map/ppermute | solution.py:56

commit v4 on v3

--- a/solution.py
+++ b/solution.py
@@ -126,8 +126,8 @@
 def first_kernel(me, depth_hbm, rhs_hbm, basis_hbm, out, high, low, depth_out, depth, rhs, basis, sems):
     levels, masks = slots(me[0], 1 - (me[0] & 1))
     copies = [pltpu.make_async_copy(rhs_hbm, rhs, sems.at[0])]
-    for slot in (0, 1):
-        copies.append(pltpu.make_async_copy(basis_hbm.at[levels[slot]], basis.at[slot], sems.at[slot + 1]))
+    for number, slot in enumerate((2, 3)):
+        copies.append(pltpu.make_async_copy(basis_hbm.at[levels[slot]], basis.at[number], sems.at[number + 1]))
     depth_copy = pltpu.make_async_copy(depth_hbm, depth, sems.at[3])
     depth_copy.start()
     for copy in copies:
@@ -136,9 +136,9 @@
     depth_out[...] = jnp.broadcast_to(depth[...].astype(jnp.float32), (128, V)).T
     copies[0].wait()
     high[...], low[...] = split(rhs[...])
-    for slot in (0, 1):
-        copies[slot + 1].wait()
-        product = dot3(masked(basis.at[slot][...], depth_out, levels[slot]), (high[...], low[...]), 0)
+    for number, slot in enumerate((2, 3)):
+        copies[number + 1].wait()
+        product = dot3(masked(basis.at[number][...], depth_out, levels[slot]), (high[...], low[...]), 0)
         put(product, out, slot, masks[slot])
 
 
@@ -161,7 +161,7 @@
         ],
         compiler_params=pltpu.CompilerParams(vmem_limit_bytes=50 << 20),
         cost_estimate=pl.CostEstimate(flops=12 * R * S * V, bytes_accessed=2 * 4 * S * (R + V), transcendentals=0),
-        name="send_ab",
+        name="send_cd",
     )(me, depth, rhs, basis)
 
 
@@ -298,13 +298,13 @@
     by_core(me, zero, one)
 
 
-def finish_kernel(me, total, other, out, passed):
+def finish_kernel(me, total, far, side, back, out, passed):
     def zero():
-        out[...] = total[...]
-        passed[...] = other[...]
+        out[...] = total[...] + far[...]
+        passed[...] = side[...] + back[...]
 
     def one():
-        out[...] = total[...] + other[...]
+        out[...] = (total[...] + far[...]) + (side[...] + back[...])
         passed[...] = out[...]
 
     by_core(me, zero, one)
@@ -333,12 +333,12 @@
 
 
 def whole_kernel(me, c_low, c_high, m2, m4, out):
-    out[:64, :] = c_low[...]
-
     def zero():
+        out[:64, :] = c_low[...] + m4[...]
         out[64:, :] = c_high[...] + m2[...]
 
     def one():
+        out[:64, :] = c_low[...]
         out[64:, :] = m4[...]
 
     by_core(me, zero, one)
@@ -348,21 +348,21 @@
     index_here = lax.axis_index("leaf")
     me = index_here.reshape(1)
 
-    send_ab, high, low, depth = first_partials(me, vertex_tier_depth.reshape(1, V), rhs, basis)
+    send_cd, high, low, depth = first_partials(me, vertex_tier_depth.reshape(1, V), rhs, basis)
+    got_cd = send(send_cd, SWAP)
+    send_ab = partials([(0, 1), (1, 1)], me, high, low, depth, basis)
     got_ab = send(send_ab, SWAP)
+    keep_cd = partials([(2, 0), (3, 0)], me, high, low, depth, basis)
+
+    near, mid = pairs(along_z(1), shifted_z(1)), pairs(along_z(2), shifted_z(2))
+    c_low, c_high, d = local(cut_kernel, (128, 128, 256), keep_cd, got_cd)
+
     keep_ab = partials([(0, 0), (1, 0)], me, high, low, depth, basis)
-
     step = [None] + [pairs(along_y(j), along_x(j)) for j in (1, 2, 3)]
     base, s1, s2, s3 = local(cut_kernel, (192, 192, 64, 64), keep_ab, got_ab)
     r1 = send(s1, step[1])
     r2 = send(s2, step[2])
     r3 = send(s3, step[3])
-
-    send_cd = partials([(2, 1), (3, 1)], me, high, low, depth, basis)
-    got_cd = send(send_cd, SWAP)
-    keep_cd = partials([(2, 0), (3, 0)], me, high, low, depth, basis)
-    near, mid = pairs(along_z(1), shifted_z(1)), pairs(along_z(2), shifted_z(2))
-    c_low, c_high, d = local(cut_kernel, (128, 128, 256), keep_cd, got_cd)
     c_low, c_high = local(cut_kernel, (64, 64), c_low, send(c_high, near))
     d = d + send(d, pairs(along_z(1), None))
 
@@ -372,20 +372,21 @@
     t3 = send(u3, pairs(None, along_y(3)))
     total, passed = local(settle_kernel, (48, 48), me, u0, u3, t1, t2, t3)
     total = total + send(passed, pairs(shifted_z(2), along_z(1)))
-    total = total + send(total, pairs(along_z(4), along_z(2)))
-    other = send(total, pairs(shifted_z(2), along_z(4)))
-    total, passed = local(finish_kernel, (48, 48), me, total, other)
+    far = send(total, pairs(along_z(4), along_z(4)))
+    side = send(total, pairs(shifted_z(2), along_z(2)))
+    back = send(total, pairs(shifted_z(6), along_z(6)))
+    total, passed = local(finish_kernel, (48, 48), me, total, far, side, back)
     g1 = send(total, pairs(shifted_z(1), along_y(1)))
     g2 = send(passed, pairs(shifted_z(1), along_y(2)))
     g3 = send(total, pairs(None, along_y(3)))
-    done, top = local(stack_kernel, (192, 64), me, total, g1, g2, g3, other)
+    done, top = local(stack_kernel, (192, 64), me, total, g1, g2, g3, passed)
     q1, q2, q3 = send(done, step[1]), send(top, step[2]), send(top, step[3])
     ab_pieces = (done, q1, q2, q3)
 
     m2 = send(c_high, mid)
     (c_low,) = local(half_kernel, (64,), me, c_low, m2)
-    c_low = c_low + send(c_low, pairs(along_z(2), along_z(4)))
-    m4 = send(c_low, pairs(None, shifted_z(2)))
+    c_low = c_low + send(c_low, pairs(None, along_z(4)))
+    m4 = send(c_low, mid)
     (c_half,) = local(whole_kernel, (128,), me, c_low, c_high, m2, m4)
     c_pieces = (c_half, send(c_half, near))
 
@@ -394,12 +395,11 @@
     their_ab = tuple(send(piece, SWAP) for piece in ab_pieces)
 
     result = leaf(high, low, depth, basis)
-    result = images([(2, 0, PLAN_C), (2, 1, shift_pieces(PLAN_C, 2))], me, depth, basis, result, c_pieces + their_c)
-    result = images(
-        [(3, 0, PLAN_D), (3, 1, shift_pieces(PLAN_D, 1)), (0, 0, shift_pieces(plan_ab(0), 2)), (1, 0, shift_pieces(plan_ab(1), 2))],
-        me, depth, basis, result, (d, their_d) + ab_pieces,
-    )
-    return images([(0, 1, plan_ab(0)), (1, 1, plan_ab(1))], me, depth, basis, result, their_ab)
+    own_ab, their_plan = [(0, 0, plan_ab(0)), (1, 0, plan_ab(1))], [(0, 1, plan_ab(0)), (1, 1, plan_ab(1))]
+    result = images([(3, 0, PLAN_D), (3, 1, shift_pieces(PLAN_D, 1))], me, depth, basis, result, (d, their_d))
+    own_ab, their_plan = [(0, 0, plan_ab(0)), (1, 0, plan_ab(1))], [(0, 1, plan_ab(0)), (1, 1, plan_ab(1))]
+    result = images(own_ab + [(2, 0, shift_pieces(PLAN_C, 4))], me, depth, basis, result, ab_pieces + c_pieces)
+    return images(their_plan + [(2, 1, shift_pieces(PLAN_C, 4))], me, depth, basis, result, their_ab + their_c)
 
 
 def solution(mesh):

time: 124 us -> 113 us (0.911)
  the two profiles are of different devices: /device:TPU:3 before, /device:TPU:1 now
where the time goes in v4:
time: 113 us; the launch traced here: 112 us
  starting transfers between devices  47.6 us (42%)
  waiting for transfers between devices  44.5 us (39%)
  Pallas kernels  19.2 us (17%)
    ppermute x31, starting transfers between devices, send(): return lax.ppermute(array, 'leaf', perm)  47.6 us
    ppermute x31, waiting for transfers between devices, send(): return lax.ppermute(array, 'leaf', perm)  44.5 us
    pallas_call x3, Pallas kernels, images(): pl.pallas_call(functools.partial(image_kernel, work), out_shape=jax.Shape...  7.54 us
    pallas_call x1, Pallas kernels, first_partials(): pl.pallas_call(first_kernel, out_shape=(jax.ShapeDtypeStruct((2 * S, R),...  4.65 us
    pallas_call x3, Pallas kernels, partials(): pl.pallas_call(functools.partial(partial_kernel, work), out_shape=jax.Sha...  4.49 us
  transfers between devices with their start and end apart: 31, of which 13 were waited for; matrix products, arithmetic and copies ran while one was open for 0% of the time, Pallas kernels for 8%

profile of v4, /device:TPU:1, one launch (start us, length us, event | category | flops | bytes accessed | tf_op | source)
XLA Modules:
  0.0 112.5 jit_solution(14098938816329935188)
XLA Ops:
  0.7 4.7 %send_cd.1 = (f32[512,768]{1,0:T(8,128)S(1)}, bf16[512,768]{1,0:T(8,128)(2,1)S(1)}, bf16[512,768]{1,0:T(8,128)(2,1)S(1)}, f32[512,128]{1,0:T(8,128)S(1)}) custom-call(s32[1]{0:T(128)} %bitcast.me, s32[1,512]{1,0:T(1,128)S(1)} %bitcast.2, f32[512,768]{1,0:T(8,128)} %rhs_hbm.1, f32[9,512,256]{2,1,0:T(8,128)} %basis.13), custom_call_target="tpu_custom_call" | custom-call | flops 1207959552 | bytes 2621440 | tf_op jit(solution)/shard_map/send_cd/pallas_call | solution.py:146
  5.4 1.5 %shard_map.41 = f32[512,768]{1,0:T(8,128)S(1)} custom-call(s32[1]{0:T(128)} %bitcast.me, bf16[512,768]{1,0:T(8,128)(2,1)S(1)} %get-tuple-element.29.high, bf16[512,768]{1,0:T(8,128)(2,1)S(1)} %get-tuple-element.30.low, f32[512,128]{1,0:T(8,128)S(1)} %get-tuple-element.28.depth, f32[9,512,256]{2,1,0:T(8,128)S(1)} %copy-done), custom_call_target="tpu_custom_call" | custom-call | flops 1207959552 | bytes 2621440 | tf_op jit(solution)/shard_map/pallas_call | solution.py:176
  6.9 3.3 %collective-permute-start.3 = (f32[512,768]{1,0:T(8,128)S(1)}, f32[512,768]{1,0:T(8,128)S(1)}, u32[]{:S(2)}, u32[]{:S(2)}) collective-permute-start(f32[512,768]{1,0:T(8,128)S(1)} %shard_map.41), channel_id=1, source_target_pairs={{0,1},{1,0},{2,3},{3,2},{4,5},{5,4},{6,7},{7,6},{8,9},{9,8},{10,11... | collective-permute-start | bytes 4718600 | tf_op jit(solution)/shard_map/ppermute | solution.py:56
  10.2 1.5 %shard_map.40.kept = f32[512,768]{1,0:T(8,128)S(1)} custom-call(s32[1]{0:T(128)} %bitcast.me, bf16[512,768]{1,0:T(8,128)(2,1)S(1)} %get-tuple-element.29.high, bf16[512,768]{1,0:T(8,128)(2,1)S(1)} %get-tuple-element.30.low, f32[512,128]{1,0:T(8,128)S(1)} %get-tuple-element.28.depth, f32[9,512,256]{2,1,0:T(8,128)S(1)} %copy-done), custom_call_target="tpu_custom_call" | custom-call | flops 1207959552 | bytes 2621440 | tf_op jit(solution)/shard_map/pallas_call | solution.py:176
  11.8 1.4 %collective-permute-done.3.got = f32[512,768]{1,0:T(8,128)S(1)} collective-permute-done((f32[512,768]{1,0:T(8,128)S(1)}, f32[512,768]{1,0:T(8,128)S(1)}, u32[]{:S(2)}, u32[]{:S(2)}) %collective-permute-start.3) | collective-permute-done | bytes 1572896 | tf_op jit(solution)/shard_map/ppermute | solution.py:56
  13.4 1.5 %shard_map.37.kept = f32[512,768]{1,0:T(8,128)S(1)} custom-call(s32[1]{0:T(128)} %bitcast.me, bf16[512,768]{1,0:T(8,128)(2,1)S(1)} %get-tuple-element.29.high, bf16[512,768]{1,0:T(8,128)(2,1)S(1)} %get-tuple-element.30.low, f32[512,128]{1,0:T(8,128)S(1)} %get-tuple-element.28.depth, f32[9,512,256]{2,1,0:T(8,128)S(1)} %copy-done), custom_call_target="tpu_custom_call" | custom-call | flops 1207959552 | bytes 2621440 | tf_op jit(solution)/shard_map/pallas_call | solution.py:176
  15.6 4.7 %collective-permute-start.20 = (f32[128,768]{1,0:T(8,128)S(1)}, f32[128,768]{1,0:T(8,128)S(1)}, u32[]{:S(2)}, u32[]{:S(2)}) collective-permute-start(f32[128,768]{1,0:T(8,128)S(1)} %get-tuple-element.48), channel_id=1, source_target_pairs={{0,2},{1,15},{2,0},{3,5},{4,6},{5,3},{6,4},{7,9},{8,10},{9,7},{10,... | collective-permute-start | bytes 1179656 | tf_op jit(solution)/shard_map/ppermute | solution.py:56
  20.3 2.4 %collective-permute-start.5 = (f32[64,768]{1,0:T(8,128)S(1)}, f32[64,768]{1,0:T(8,128)S(1)}, u32[]{:S(2)}, u32[]{:S(2)}) collective-permute-start(f32[64,768]{1,0:T(8,128)S(1)} %get-tuple-element.35), channel_id=1, source_target_pairs={{0,32},{1,129},{2,34},{3,131},{4,36},{5,133},{6,38},{7,135},{8,40}... | collective-permute-start | bytes 589832 | tf_op jit(solution)/shard_map/ppermute | solution.py:56
  23.9 2.4 %collective-permute-done.5.r2 = f32[64,768]{1,0:T(8,128)S(1)} collective-permute-done((f32[64,768]{1,0:T(8,128)S(1)}, f32[64,768]{1,0:T(8,128)S(1)}, u32[]{:S(2)}, u32[]{:S(2)}) %collective-permute-start.5) | collective-permute-done | bytes 196640 | tf_op jit(solution)/shard_map/ppermute | solution.py:56
  26.3 2.2 %collective-permute-done.6.r3 = f32[64,768]{1,0:T(8,128)S(1)} collective-permute-done((f32[64,768]{1,0:T(8,128)S(1)}, f32[64,768]{1,0:T(8,128)S(1)}, u32[]{:S(2)}, u32[]{:S(2)}) %collective-permute-start.6) | collective-permute-done | bytes 196640 | tf_op jit(solution)/shard_map/ppermute | solution.py:56
  28.6 1.4 %collective-permute-start.7 = (f32[48,768]{1,0:T(8,128)S(1)}, f32[48,768]{1,0:T(8,128)S(1)}, u32[]{:S(2)}, u32[]{:S(2)}) collective-permute-start(f32[48,768]{1,0:T(8,128)S(1)} %get-tuple-element.39), channel_id=1, source_target_pairs={{0,14},{1,17},{2,4},{3,19},{4,2},{5,21},{6,8},{7,23},{8,6},{9,25},... | collective-permute-start | bytes 442376 | tf_op jit(solution)/shard_map/ppermute | solution.py:56
  30.0 2.6 %collective-permute-start.8 = (f32[48,768]{1,0:T(8,128)S(1)}, f32[48,768]{1,0:T(8,128)S(1)}, u32[]{:S(2)}, u32[]{:S(2)}) collective-permute-start(f32[48,768]{1,0:T(8,128)S(1)} %get-tuple-element.40), channel_id=1, source_target_pairs={{0,14},{1,33},{2,4},{3,35},{4,2},{5,37},{6,8},{7,39},{8,6},{9,41},... | collective-permute-start | bytes 442376 | tf_op jit(solution)/shard_map/ppermute | solution.py:56
  32.6 1.9 %collective-permute-start.9 = (f32[48,768]{1,0:T(8,128)S(1)}, f32[48,768]{1,0:T(8,128)S(1)}, u32[]{:S(2)}, u32[]{:S(2)}) collective-permute-start(f32[48,768]{1,0:T(8,128)S(1)} %get-tuple-element.38.u3), channel_id=1, source_target_pairs={{1,49},{3,51},{5,53},{7,55},{9,57},{11,59},{13,61},{15,63},{17,33}... | collective-permute-start | bytes 442376 | tf_op jit(solution)/shard_map/ppermute | solution.py:56
  34.5 2.2 %collective-permute-done.8.t2 = f32[48,768]{1,0:T(8,128)S(1)} collective-permute-done((f32[48,768]{1,0:T(8,128)S(1)}, f32[48,768]{1,0:T(8,128)S(1)}, u32[]{:S(2)}, u32[]{:S(2)}) %collective-permute-start.8) | collective-permute-done | bytes 147488 | tf_op jit(solution)/shard_map/ppermute | solution.py:56
  36.7 3.3 %collective-permute-done.9.t3 = f32[48,768]{1,0:T(8,128)S(1)} collective-permute-done((f32[48,768]{1,0:T(8,128)S(1)}, f32[48,768]{1,0:T(8,128)S(1)}, u32[]{:S(2)}, u32[]{:S(2)}) %collective-permute-start.9) | collective-permute-done | bytes 147488 | tf_op jit(solution)/shard_map/ppermute | solution.py:56
  40.2 3.4 %collective-permute-start.21 = (f32[64,768]{1,0:T(8,128)S(1)}, f32[64,768]{1,0:T(8,128)S(1)}, u32[]{:S(2)}, u32[]{:S(2)}) collective-permute-start(f32[64,768]{1,0:T(8,128)S(1)} %get-tuple-element.50.c_high), channel_id=1, source_target_pairs={{0,4},{1,13},{2,6},{3,7},{4,0},{5,9},{6,2},{7,3},{8,12},{9,5},{10,... | collective-permute-start | bytes 589832 | tf_op jit(solution)/shard_map/ppermute | solution.py:56
  44.1 3.4 %collective-permute-start.11 = (f32[48,768]{1,0:T(8,128)S(1)}, f32[48,768]{1,0:T(8,128)S(1)}, u32[]{:S(2)}, u32[]{:S(2)}) collective-permute-start(f32[48,768]{1,0:T(8,128)S(1)} %add.10.total), channel_id=1, source_target_pairs={{0,8},{1,9},{2,10},{3,11},{4,12},{5,13},{6,14},{7,15},{8,0},{9,1},... | collective-permute-start | bytes 442376 | tf_op jit(solution)/shard_map/ppermute | solution.py:56
  47.6 7.0 %collective-permute-start.12 = (f32[48,768]{1,0:T(8,128)S(1)}, f32[48,768]{1,0:T(8,128)S(1)}, u32[]{:S(2)}, u32[]{:S(2)}) collective-permute-start(f32[48,768]{1,0:T(8,128)S(1)} %add.10.total), channel_id=1, source_target_pairs={{0,12},{1,5},{2,6},{3,7},{4,8},{5,1},{6,2},{7,3},{8,4},{9,13},{10,... | collective-permute-start | bytes 442376 | tf_op jit(solution)/shard_map/ppermute | solution.py:56
  54.5 4.0 %collective-permute-done.21.m2 = f32[64,768]{1,0:T(8,128)S(1)} collective-permute-done((f32[64,768]{1,0:T(8,128)S(1)}, f32[64,768]{1,0:T(8,128)S(1)}, u32[]{:S(2)}, u32[]{:S(2)}) %collective-permute-start.21) | collective-permute-done | bytes 196640 | tf_op jit(solution)/shard_map/ppermute | solution.py:56
  58.6 4.7 %collective-permute-start.22 = (f32[64,768]{1,0:T(8,128)S(1)}, f32[64,768]{1,0:T(8,128)S(1)}, u32[]{:S(2)}, u32[]{:S(2)}) collective-permute-start(f32[64,768]{1,0:T(8,128)S(1)} %shard_map.48), channel_id=1, source_target_pairs={{1,9},{3,11},{5,13},{7,15},{9,1},{11,3},{13,5},{15,7},{17,25},{19,... | collective-permute-start | bytes 589832 | tf_op jit(solution)/shard_map/ppermute | solution.py:56
  63.3 8.2 %collective-permute-done.12.side = f32[48,768]{1,0:T(8,128)S(1)} collective-permute-done((f32[48,768]{1,0:T(8,128)S(1)}, f32[48,768]{1,0:T(8,128)S(1)}, u32[]{:S(2)}, u32[]{:S(2)}) %collective-permute-start.12) | collective-permute-done | bytes 147488 | tf_op jit(solution)/shard_map/ppermute | solution.py:56
  71.7 1.4 %collective-permute-start.15 = (f32[48,768]{1,0:T(8,128)S(1)}, f32[48,768]{1,0:T(8,128)S(1)}, u32[]{:S(2)}, u32[]{:S(2)}) collective-permute-start(f32[48,768]{1,0:T(8,128)S(1)} %get-tuple-element.44.other), channel_id=1, source_target_pairs={{0,14},{1,33},{2,4},{3,35},{4,2},{5,37},{6,8},{7,39},{8,6},{9,41},... | collective-permute-start | bytes 442376 | tf_op jit(solution)/shard_map/ppermute | solution.py:56
  73.1 4.4 %collective-permute-start.16 = (f32[48,768]{1,0:T(8,128)S(1)}, f32[48,768]{1,0:T(8,128)S(1)}, u32[]{:S(2)}, u32[]{:S(2)}) collective-permute-start(f32[48,768]{1,0:T(8,128)S(1)} %get-tuple-element.43.total), channel_id=1, source_target_pairs={{1,49},{3,51},{5,53},{7,55},{9,57},{11,59},{13,61},{15,63},{17,33}... | collective-permute-start | bytes 442376 | tf_op jit(solution)/shard_map/ppermute | solution.py:56
  77.5 2.3 %collective-permute-start.23 = (f32[64,768]{1,0:T(8,128)S(1)}, f32[64,768]{1,0:T(8,128)S(1)}, u32[]{:S(2)}, u32[]{:S(2)}) collective-permute-start(f32[64,768]{1,0:T(8,128)S(1)} %add.11.c_low), channel_id=1, source_target_pairs={{0,4},{1,13},{2,6},{3,7},{4,0},{5,9},{6,2},{7,3},{8,12},{9,5},{10,... | collective-permute-start | bytes 589832 | tf_op jit(solution)/shard_map/ppermute | solution.py:56
  80.9 7.5 %collective-permute-done.23.m4 = f32[64,768]{1,0:T(8,128)S(1)} collective-permute-done((f32[64,768]{1,0:T(8,128)S(1)}, f32[64,768]{1,0:T(8,128)S(1)}, u32[]{:S(2)}, u32[]{:S(2)}) %collective-permute-start.23) | collective-permute-done | bytes 196640 | tf_op jit(solution)/shard_map/ppermute | solution.py:56
  88.5 1.1 collective-permute-start.18
  89.6 6.7 %collective-permute-done.24.refs_5_ = f32[128,768]{1,0:T(8,128)S(1)} collective-permute-done((f32[128,768]{1,0:T(8,128)S(1)}, f32[128,768]{1,0:T(8,128)S(1)}, u32[]{:S(2)}, u32[]{:S(2)}) %collective-permute-start.24) | collective-permute-done | bytes 393248 | tf_op jit(solution)/shard_map/ppermute | solution.py:56
  96.9 5.2 %collective-permute-done.19.refs_3_ = f32[64,768]{1,0:T(8,128)S(1)} collective-permute-done((f32[64,768]{1,0:T(8,128)S(1)}, f32[64,768]{1,0:T(8,128)S(1)}, u32[]{:S(2)}, u32[]{:S(2)}) %collective-permute-start.19) | collective-permute-done | bytes 196640 | tf_op jit(solution)/shard_map/ppermute | solution.py:56
  102.1 1.8 %leaf.1.before = f32[512,768]{1,0:T(8,128)S(1)} custom-call(bf16[512,768]{1,0:T(8,128)(2,1)S(1)} %get-tuple-element.29.high, bf16[512,768]{1,0:T(8,128)(2,1)S(1)} %get-tuple-element.30.low, f32[512,128]{1,0:T(8,128)S(1)} %get-tuple-element.28.depth, f32[9,512,256]{2,1,0:T(8,128)S(1)} %copy-done), custom_call_target="tpu_custom_call" | custom-call | flops 1207959552 | bytes 1572864 | tf_op jit(solution)/shard_map/leaf/pallas_call | solution.py:194
  104.8 1.5 %shard_map.39.before = f32[512,768]{1,0:T(8,128)S(1)} custom-call(s32[1]{0:T(128)} %bitcast.me, f32[512,128]{1,0:T(8,128)S(1)} %get-tuple-element.28.depth, f32[9,512,256]{2,1,0:T(8,128)S(1)} %copy-done, f32[512,768]{1,0:T(8,128)S(1)} %leaf.1.before, f32[256,768]{1,0:T(8,128)S(1)} %add.9.refs_0_, f32[256,768]{1,0:T(8,128)S(1)} %collective-permute-done.2.refs_1_), custom_call_target="tpu_custom_call" | custom-call | flops 1207959552 | bytes 2621440 | tf_op jit(solution)/shard_map/pallas_call | solution.py:221
  106.4 2.4 %shard_map.50.before = f32[512,768]{1,0:T(8,128)S(1)} custom-call(s32[1]{0:T(128)} %bitcast.me, f32[512,128]{1,0:T(8,128)S(1)} %get-tuple-element.28.depth, f32[9,512,256]{2,1,0:T(8,128)S(1)} %copy-done, f32[512,768]{1,0:T(8,128)S(1)} %shard_map.39.before, f32[192,768]{1,0:T(8,128)S(1)} %get-tuple-element.45.refs_0_, ...), custom_call_target="tpu_custom_call" | custom-call | flops 1811939328 | bytes 3932160 | tf_op jit(solution)/shard_map/pallas_call | solution.py:221
  108.9 3.6 %shard_map.51 = f32[512,768]{1,0:T(8,128)} custom-call(s32[1]{0:T(128)} %bitcast.me, f32[512,128]{1,0:T(8,128)S(1)} %get-tuple-element.28.depth, f32[9,512,256]{2,1,0:T(8,128)S(1)} %copy-done, f32[512,768]{1,0:T(8,128)S(1)} %shard_map.50.before, f32[192,768]{1,0:T(8,128)S(1)} %collective-permute-done.25.refs_0_, ...), custom_call_target="tpu_custom_call" | custom-call | flops 1811939328 | bytes 3932160 | tf_op jit(solution)/shard_map/pallas_call | solution.py:221
  (54 shorter events, 6.4 us)
Async XLA Ops:
  0.7 4.7 %copy-start = (f32[9,512,256]{2,1,0:T(8,128)S(1)}, f32[9,512,256]{2,1,0:T(8,128)}, u32[]{:S(2)}) copy-start(f32[9,512,256]{2,1,0:T(8,128)} %basis.13) | copy-start | bytes 14155780
  6.9 6.3 %collective-permute-start.3 = (f32[512,768]{1,0:T(8,128)S(1)}, f32[512,768]{1,0:T(8,128)S(1)}, u32[]{:S(2)}, u32[]{:S(2)}) collective-permute-start(f32[512,768]{1,0:T(8,128)S(1)} %shard_map.41), channel_id=1, source_target_pairs={{0,1},{1,0},{2,3},{3,2},{4,5},{5,4},{6,7},{7,6},{8,9},{9,8},{10,11... | collective-permute-start | bytes 4718600 | tf_op jit(solution)/shard_map/ppermute | solution.py:56
  10.1 5.3 %collective-permute-start = (f32[512,768]{1,0:T(8,128)S(1)}, f32[512,768]{1,0:T(8,128)S(1)}, u32[]{:S(2)}, u32[]{:S(2)}) collective-permute-start(f32[512,768]{1,0:T(8,128)S(1)} %get-tuple-element.31), channel_id=1, source_target_pairs={{0,1},{1,0},{2,3},{3,2},{4,5},{5,4},{6,7},{7,6},{8,9},{9,8},{10,11... | collective-permute-start | bytes 4718600 | tf_op jit(solution)/shard_map/ppermute | solution.py:56
  13.3 15.1 %collective-permute-start.4 = (f32[192,768]{1,0:T(8,128)S(1)}, f32[192,768]{1,0:T(8,128)S(1)}, u32[]{:S(2)}, u32[]{:S(2)}) collective-permute-start(f32[192,768]{1,0:T(8,128)S(1)} %get-tuple-element.34), channel_id=1, source_target_pairs={{0,16},{1,65},{2,18},{3,67},{4,20},{5,69},{6,22},{7,71},{8,24},{9,... | collective-permute-start | bytes 1769480 | tf_op jit(solution)/shard_map/ppermute | solution.py:56
  15.6 24.5 %collective-permute-start.20 = (f32[128,768]{1,0:T(8,128)S(1)}, f32[128,768]{1,0:T(8,128)S(1)}, u32[]{:S(2)}, u32[]{:S(2)}) collective-permute-start(f32[128,768]{1,0:T(8,128)S(1)} %get-tuple-element.48), channel_id=1, source_target_pairs={{0,2},{1,15},{2,0},{3,5},{4,6},{5,3},{6,4},{7,9},{8,10},{9,7},{10,... | collective-permute-start | bytes 1179656 | tf_op jit(solution)/shard_map/ppermute | solution.py:56
  20.3 6.0 %collective-permute-start.5 = (f32[64,768]{1,0:T(8,128)S(1)}, f32[64,768]{1,0:T(8,128)S(1)}, u32[]{:S(2)}, u32[]{:S(2)}) collective-permute-start(f32[64,768]{1,0:T(8,128)S(1)} %get-tuple-element.35), channel_id=1, source_target_pairs={{0,32},{1,129},{2,34},{3,131},{4,36},{5,133},{6,38},{7,135},{8,40}... | collective-permute-start | bytes 589832 | tf_op jit(solution)/shard_map/ppermute | solution.py:56
  22.7 5.7 %collective-permute-start.6 = (f32[64,768]{1,0:T(8,128)S(1)}, f32[64,768]{1,0:T(8,128)S(1)}, u32[]{:S(2)}, u32[]{:S(2)}) collective-permute-start(f32[64,768]{1,0:T(8,128)S(1)} %get-tuple-element.36), channel_id=1, source_target_pairs={{0,48},{1,193},{2,50},{3,195},{4,52},{5,197},{6,54},{7,199},{8,56}... | collective-permute-start | bytes 589832 | tf_op jit(solution)/shard_map/ppermute | solution.py:56
  23.2 57.2 %collective-permute-start.1 = (f32[256,768]{1,0:T(8,128)S(1)}, f32[256,768]{1,0:T(8,128)S(1)}, u32[]{:S(2)}, u32[]{:S(2)}) collective-permute-start(f32[256,768]{1,0:T(8,128)S(1)} %get-tuple-element.32), channel_id=1, source_target_pairs={{0,2},{2,0},{4,6},{6,4},{8,10},{10,8},{12,14},{14,12},{16,18},{18,... | collective-permute-start | bytes 2359304 | tf_op jit(solution)/shard_map/ppermute | solution.py:56
  28.6 5.9 %collective-permute-start.7 = (f32[48,768]{1,0:T(8,128)S(1)}, f32[48,768]{1,0:T(8,128)S(1)}, u32[]{:S(2)}, u32[]{:S(2)}) collective-permute-start(f32[48,768]{1,0:T(8,128)S(1)} %get-tuple-element.39), channel_id=1, source_target_pairs={{0,14},{1,17},{2,4},{3,19},{4,2},{5,21},{6,8},{7,23},{8,6},{9,25},... | collective-permute-start | bytes 442376 | tf_op jit(solution)/shard_map/ppermute | solution.py:56
  30.0 6.7 %collective-permute-start.8 = (f32[48,768]{1,0:T(8,128)S(1)}, f32[48,768]{1,0:T(8,128)S(1)}, u32[]{:S(2)}, u32[]{:S(2)}) collective-permute-start(f32[48,768]{1,0:T(8,128)S(1)} %get-tuple-element.40), channel_id=1, source_target_pairs={{0,14},{1,33},{2,4},{3,35},{4,2},{5,37},{6,8},{7,39},{8,6},{9,41},... | collective-permute-start | bytes 442376 | tf_op jit(solution)/shard_map/ppermute | solution.py:56
  32.6 7.4 %collective-permute-start.9 = (f32[48,768]{1,0:T(8,128)S(1)}, f32[48,768]{1,0:T(8,128)S(1)}, u32[]{:S(2)}, u32[]{:S(2)}) collective-permute-start(f32[48,768]{1,0:T(8,128)S(1)} %get-tuple-element.38.u3), channel_id=1, source_target_pairs={{1,49},{3,51},{5,53},{7,55},{9,57},{11,59},{13,61},{15,63},{17,33}... | collective-permute-start | bytes 442376 | tf_op jit(solution)/shard_map/ppermute | solution.py:56
  40.0 4.1 %collective-permute-start.10 = (f32[48,768]{1,0:T(8,128)S(1)}, f32[48,768]{1,0:T(8,128)S(1)}, u32[]{:S(2)}, u32[]{:S(2)}) collective-permute-start(f32[48,768]{1,0:T(8,128)S(1)} %get-tuple-element.42), channel_id=1, source_target_pairs={{0,12},{1,3},{2,6},{3,1},{4,8},{5,7},{6,2},{7,5},{8,4},{9,11},{10,... | collective-permute-start | bytes 442376 | tf_op jit(solution)/shard_map/ppermute | solution.py:56
  40.2 18.4 %collective-permute-start.21 = (f32[64,768]{1,0:T(8,128)S(1)}, f32[64,768]{1,0:T(8,128)S(1)}, u32[]{:S(2)}, u32[]{:S(2)}) collective-permute-start(f32[64,768]{1,0:T(8,128)S(1)} %get-tuple-element.50.c_high), channel_id=1, source_target_pairs={{0,4},{1,13},{2,6},{3,7},{4,0},{5,9},{6,2},{7,3},{8,12},{9,5},{10,... | collective-permute-start | bytes 589832 | tf_op jit(solution)/shard_map/ppermute | solution.py:56
  44.1 19.2 %collective-permute-start.11 = (f32[48,768]{1,0:T(8,128)S(1)}, f32[48,768]{1,0:T(8,128)S(1)}, u32[]{:S(2)}, u32[]{:S(2)}) collective-permute-start(f32[48,768]{1,0:T(8,128)S(1)} %add.10.total), channel_id=1, source_target_pairs={{0,8},{1,9},{2,10},{3,11},{4,12},{5,13},{6,14},{7,15},{8,0},{9,1},... | collective-permute-start | bytes 442376 | tf_op jit(solution)/shard_map/ppermute | solution.py:56
  47.6 24.0 %collective-permute-start.12 = (f32[48,768]{1,0:T(8,128)S(1)}, f32[48,768]{1,0:T(8,128)S(1)}, u32[]{:S(2)}, u32[]{:S(2)}) collective-permute-start(f32[48,768]{1,0:T(8,128)S(1)} %add.10.total), channel_id=1, source_target_pairs={{0,12},{1,5},{2,6},{3,7},{4,8},{5,1},{6,2},{7,3},{8,4},{9,13},{10,... | collective-permute-start | bytes 442376 | tf_op jit(solution)/shard_map/ppermute | solution.py:56
  54.5 17.0 %collective-permute-start.13 = (f32[48,768]{1,0:T(8,128)S(1)}, f32[48,768]{1,0:T(8,128)S(1)}, u32[]{:S(2)}, u32[]{:S(2)}) collective-permute-start(f32[48,768]{1,0:T(8,128)S(1)} %add.10.total), channel_id=1, source_target_pairs={{0,4},{1,13},{2,14},{3,15},{4,0},{5,9},{6,10},{7,11},{8,12},{9,5},... | collective-permute-start | bytes 442376 | tf_op jit(solution)/shard_map/ppermute | solution.py:56
  58.6 18.9 %collective-permute-start.22 = (f32[64,768]{1,0:T(8,128)S(1)}, f32[64,768]{1,0:T(8,128)S(1)}, u32[]{:S(2)}, u32[]{:S(2)}) collective-permute-start(f32[64,768]{1,0:T(8,128)S(1)} %shard_map.48), channel_id=1, source_target_pairs={{1,9},{3,11},{5,13},{7,15},{9,1},{11,3},{13,5},{15,7},{17,25},{19,... | collective-permute-start | bytes 589832 | tf_op jit(solution)/shard_map/ppermute | solution.py:56
  71.6 8.2 %collective-permute-start.14 = (f32[48,768]{1,0:T(8,128)S(1)}, f32[48,768]{1,0:T(8,128)S(1)}, u32[]{:S(2)}, u32[]{:S(2)}) collective-permute-start(f32[48,768]{1,0:T(8,128)S(1)} %get-tuple-element.43.total), channel_id=1, source_target_pairs={{0,14},{1,17},{2,4},{3,19},{4,2},{5,21},{6,8},{7,23},{8,6},{9,25},... | collective-permute-start | bytes 442376 | tf_op jit(solution)/shard_map/ppermute | solution.py:56
  71.7 8.1 %collective-permute-start.15 = (f32[48,768]{1,0:T(8,128)S(1)}, f32[48,768]{1,0:T(8,128)S(1)}, u32[]{:S(2)}, u32[]{:S(2)}) collective-permute-start(f32[48,768]{1,0:T(8,128)S(1)} %get-tuple-element.44.other), channel_id=1, source_target_pairs={{0,14},{1,33},{2,4},{3,35},{4,2},{5,37},{6,8},{7,39},{8,6},{9,41},... | collective-permute-start | bytes 442376 | tf_op jit(solution)/shard_map/ppermute | solution.py:56
  73.1 7.1 %collective-permute-start.16 = (f32[48,768]{1,0:T(8,128)S(1)}, f32[48,768]{1,0:T(8,128)S(1)}, u32[]{:S(2)}, u32[]{:S(2)}) collective-permute-start(f32[48,768]{1,0:T(8,128)S(1)} %get-tuple-element.43.total), channel_id=1, source_target_pairs={{1,49},{3,51},{5,53},{7,55},{9,57},{11,59},{13,61},{15,63},{17,33}... | collective-permute-start | bytes 442376 | tf_op jit(solution)/shard_map/ppermute | solution.py:56
  77.5 10.9 %collective-permute-start.23 = (f32[64,768]{1,0:T(8,128)S(1)}, f32[64,768]{1,0:T(8,128)S(1)}, u32[]{:S(2)}, u32[]{:S(2)}) collective-permute-start(f32[64,768]{1,0:T(8,128)S(1)} %add.11.c_low), channel_id=1, source_target_pairs={{0,4},{1,13},{2,6},{3,7},{4,0},{5,9},{6,2},{7,3},{8,12},{9,5},{10,... | collective-permute-start | bytes 589832 | tf_op jit(solution)/shard_map/ppermute | solution.py:56
  80.3 16.1 %collective-permute-start.17 = (f32[192,768]{1,0:T(8,128)S(1)}, f32[192,768]{1,0:T(8,128)S(1)}, u32[]{:S(2)}, u32[]{:S(2)}) collective-permute-start(f32[192,768]{1,0:T(8,128)S(1)} %get-tuple-element.45.refs_0_), channel_id=1, source_target_pairs={{0,16},{1,65},{2,18},{3,67},{4,20},{5,69},{6,22},{7,71},{8,24},{9,... | collective-permute-start | bytes 1769480 | tf_op jit(solution)/shard_map/ppermute | solution.py:56
  80.5 24.1 %collective-permute-start.2 = (f32[256,768]{1,0:T(8,128)S(1)}, f32[256,768]{1,0:T(8,128)S(1)}, u32[]{:S(2)}, u32[]{:S(2)}) collective-permute-start(f32[256,768]{1,0:T(8,128)S(1)} %add.9.refs_0_), channel_id=1, source_target_pairs={{0,1},{1,0},{2,3},{3,2},{4,5},{5,4},{6,7},{7,6},{8,9},{9,8},{10,11... | collective-permute-start | bytes 2359304 | tf_op jit(solution)/shard_map/ppermute | solution.py:56
  88.4 7.9 %collective-permute-start.24 = (f32[128,768]{1,0:T(8,128)S(1)}, f32[128,768]{1,0:T(8,128)S(1)}, u32[]{:S(2)}, u32[]{:S(2)}) collective-permute-start(f32[128,768]{1,0:T(8,128)S(1)} %shard_map.49.refs_4_), channel_id=1, source_target_pairs={{0,2},{1,15},{2,0},{3,5},{4,6},{5,3},{6,4},{7,9},{8,10},{9,7},{10,... | collective-permute-start | bytes 1179656 | tf_op jit(solution)/shard_map/ppermute | solution.py:56
  88.5 7.8 %collective-permute-start.18 = (f32[64,768]{1,0:T(8,128)S(1)}, f32[64,768]{1,0:T(8,128)S(1)}, u32[]{:S(2)}, u32[]{:S(2)}) collective-permute-start(f32[64,768]{1,0:T(8,128)S(1)} %get-tuple-element.46), channel_id=1, source_target_pairs={{0,32},{1,129},{2,34},{3,131},{4,36},{5,133},{6,38},{7,135},{8,40}... | collective-permute-start | bytes 589832 | tf_op jit(solution)/shard_map/ppermute | solution.py:56
  89.6 14.3 %collective-permute-start.29 = (f32[128,768]{1,0:T(8,128)S(1)}, f32[128,768]{1,0:T(8,128)S(1)}, u32[]{:S(2)}, u32[]{:S(2)}) collective-permute-start(f32[128,768]{1,0:T(8,128)S(1)} %shard_map.49.refs_4_), channel_id=1, source_target_pairs={{0,1},{1,0},{2,3},{3,2},{4,5},{5,4},{6,7},{7,6},{8,9},{9,8},{10,11... | collective-permute-start | bytes 1179656 | tf_op jit(solution)/shard_map/ppermute | solution.py:56
  96.3 5.7 %collective-permute-start.19 = (f32[64,768]{1,0:T(8,128)S(1)}, f32[64,768]{1,0:T(8,128)S(1)}, u32[]{:S(2)}, u32[]{:S(2)}) collective-permute-start(f32[64,768]{1,0:T(8,128)S(1)} %get-tuple-element.46), channel_id=1, source_target_pairs={{0,48},{1,193},{2,50},{3,195},{4,52},{5,197},{6,54},{7,199},{8,56}... | collective-permute-start | bytes 589832 | tf_op jit(solution)/shard_map/ppermute | solution.py:56
  96.3 12.5 %collective-permute-start.25 = (f32[192,768]{1,0:T(8,128)S(1)}, f32[192,768]{1,0:T(8,128)S(1)}, u32[]{:S(2)}, u32[]{:S(2)}) collective-permute-start(f32[192,768]{1,0:T(8,128)S(1)} %get-tuple-element.45.refs_0_), channel_id=1, source_target_pairs={{0,1},{1,0},{2,3},{3,2},{4,5},{5,4},{6,7},{7,6},{8,9},{9,8},{10,11... | collective-permute-start | bytes 1769480 | tf_op jit(solution)/shard_map/ppermute | solution.py:56
  96.4 12.5 %collective-permute-start.26 = (f32[192,768]{1,0:T(8,128)S(1)}, f32[192,768]{1,0:T(8,128)S(1)}, u32[]{:S(2)}, u32[]{:S(2)}) collective-permute-start(f32[192,768]{1,0:T(8,128)S(1)} %collective-permute-done.17.refs_1_), channel_id=1, source_target_pairs={{0,1},{1,0},{2,3},{3,2},{4,5},{5,4},{6,7},{7,6},{8,9},{9,8},{10,11... | collective-permute-start | bytes 1769480 | tf_op jit(solution)/shard_map/ppermute | solution.py:56
  102.1 6.8 %collective-permute-start.30 = (f32[128,768]{1,0:T(8,128)S(1)}, f32[128,768]{1,0:T(8,128)S(1)}, u32[]{:S(2)}, u32[]{:S(2)}) collective-permute-start(f32[128,768]{1,0:T(8,128)S(1)} %collective-permute-done.24.refs_5_), channel_id=1, source_target_pairs={{0,1},{1,0},{2,3},{3,2},{4,5},{5,4},{6,7},{7,6},{8,9},{9,8},{10,11... | collective-permute-start | bytes 1179656 | tf_op jit(solution)/shard_map/ppermute | solution.py:56
  103.9 4.9 %collective-permute-start.27 = (f32[64,768]{1,0:T(8,128)S(1)}, f32[64,768]{1,0:T(8,128)S(1)}, u32[]{:S(2)}, u32[]{:S(2)}) collective-permute-start(f32[64,768]{1,0:T(8,128)S(1)} %collective-permute-done.18.refs_2_), channel_id=1, source_target_pairs={{0,1},{1,0},{2,3},{3,2},{4,5},{5,4},{6,7},{7,6},{8,9},{9,8},{10,11... | collective-permute-start | bytes 589832 | tf_op jit(solution)/shard_map/ppermute | solution.py:56
  104.5 4.3 %collective-permute-start.28 = (f32[64,768]{1,0:T(8,128)S(1)}, f32[64,768]{1,0:T(8,128)S(1)}, u32[]{:S(2)}, u32[]{:S(2)}) collective-permute-start(f32[64,768]{1,0:T(8,128)S(1)} %collective-permute-done.19.refs_3_), channel_id=1, source_target_pairs={{0,1},{1,0},{2,3},{3,2},{4,5},{5,4},{6,7},{7,6},{8,9},{9,8},{10,11... | collective-permute-start | bytes 589832 | tf_op jit(solution)/shard_map/ppermute | solution.py:56
  (1 other events, 0.7 us)
